TPU v7x, 32 devices: a whole 2x2x4 slice. The times are simulated.
32 devices in a mesh: comm: 4 (over z), arc: 8 (over y, x, core).
Axes of the slice: x: 2, y: 2, z: 4, core: 2. Of those that a mesh axis runs over, the one named last changes fastest.
Arguments:
- prev_dist: float32 [512, 2048], P('comm', 'arc'), may hold values from 0 to 4
- source_node: int32 [512], P('comm'), may hold values from 0 to 2047, as said below
- arc_tail: int32 [16, 2048], P(None, 'arc'), may hold values from 0 to 2047, as said below
- base_cost: float32 [16, 2048], P(None, 'arc'), may hold values from 0.05 to 1
- arc_price: float32 [16, 2048], P(None, 'arc'), may hold values from 0 to 1
- capacity: float32 [16, 2048], P(None, 'arc')
- path_arcs: int32 [512, 128], P(('comm', 'arc')), may hold values from 0 to 32767, as said below
- demand: float32 [512], P(('comm', 'arc')), may hold values from 0.5 to 2
Outputs:
- final_dist: float32 [512, 2048], P('comm', 'arc')
- new_price: float32 [16, 2048], P(None, 'arc')
Inputs may be any that keep to these rules, and one draw needn't show every extreme that they name: `arc_tail`: the tail of arc s * 2048 + v lies in a node block (nodes 128 b to 128 b + 127) at most 2 blocks before or after v's block, counted around the cycle of blocks. Row k is a walk: the head of path_arcs[k, h + 1] (its id modulo 2048) is the tail of path_arcs[k, h]. `source_node`: the tail of path_arcs[k, 127].
All inputs are finite; a program needn't handle non-finite values.
Results may differ from a plain program's by a relative error of at most 0.00002.
Values sent between devices are 32-bit elements; how exact they have to be, the bound alone decides.
No kernel may reach another device: no remote copies, remote signals or barrier semaphores. Data moves between devices by JAX's collectives and lax.ppermute only.
A program may use at most 64 MiB of HBM per device.

v0:
```python
import jax
import jax.numpy as jnp
from jax import lax
from jax.sharding import PartitionSpec as P

SWEEPS = 8


step_size = 0.25
eps_value = 1e-06


def with_halo(cells, sides, width):
    for axis, dim in sides:
        count = lax.axis_size(axis)
        head = lax.slice_in_dim(cells, 0, width, axis=dim)
        tail = lax.slice_in_dim(cells, cells.shape[dim] - width, cells.shape[dim], axis=dim)
        cells = jnp.concatenate(
            [
                lax.ppermute(tail, axis, [(i, (i + 1) % count) for i in range(count)]),
                cells,
                lax.ppermute(head, axis, [((i + 1) % count, i) for i in range(count)]),
            ],
            axis=dim,
        )
    return cells


def relax(window, window_start, tail_nodes, weights, current, node_count):
    degree = tail_nodes.shape[0]
    node_span = tail_nodes.shape[1]
    local_index = jnp.mod(tail_nodes - window_start, node_count).reshape(-1)
    picked = jnp.take(window, local_index, axis=0).reshape(degree, node_span, window.shape[1])
    candidate = picked + weights[:, :, None]
    return jnp.minimum(current, jnp.min(candidate, axis=0))


def shards(prev_dist, source_node, arc_tail, base_cost, arc_price, capacity, path_arcs, demand):
    shard_nodes = prev_dist.shape[1]
    arc_devices = lax.axis_size("arc")
    node_count = shard_nodes * arc_devices
    degree = arc_tail.shape[0]
    sweep_total = SWEEPS
    first_node = lax.axis_index("arc") * shard_nodes
    node_ids = first_node + jnp.arange(shard_nodes, dtype=jnp.int32)
    arc_weight = base_cost + arc_price
    node_major = jnp.where(node_ids[:, None] == source_node[None, :], jnp.float32(0.0), prev_dist.T)
    for sweep_number in range(sweep_total):
        window = with_halo(node_major, (("arc", 0),), shard_nodes)
        node_major = relax(
            window, first_node - shard_nodes, arc_tail, arc_weight, node_major, node_count
        )
    distance = node_major.T
    amounts = jnp.broadcast_to(demand[:, None], path_arcs.shape).reshape(-1)
    flattened = (
        jnp.zeros((degree * node_count,), jnp.float32).at[path_arcs.reshape(-1)].add(amounts)
    )
    partial_flow = lax.psum_scatter(
        flattened.reshape(degree, node_count), "arc", scatter_dimension=1, tiled=True
    )
    arc_flow = lax.psum(partial_flow, "comm")
    gradient = arc_flow - capacity
    square_sum = lax.psum(jnp.sum(gradient * gradient), "arc")
    scale_root = jnp.sqrt(square_sum / (degree * node_count) + eps_value)
    new_price = jnp.maximum(arc_price + step_size * gradient / scale_root, jnp.float32(0.0))
    return (distance, new_price)


def solution(mesh):
    in_specs = (
        P("comm", "arc"),
        P("comm"),
        P(None, "arc"),
        P(None, "arc"),
        P(None, "arc"),
        P(None, "arc"),
        P(("comm", "arc"), None),
        P(("comm", "arc")),
    )
    out_specs = (P("comm", "arc"), P(None, "arc"))
    return jax.shard_map(shards, mesh=mesh, in_specs=in_specs, out_specs=out_specs, check_vma=False)
```

profile of v0, /device:TPU:0, one launch (start us, length us, event | category | flops | bytes accessed | tf_op | source)
XLA Modules:
  0.0 245.0 jit_solution(11023003977533881316)
XLA Ops:
  7.2 1.0 copy.10
  8.2 0.8 bitcast_select_fusion
  9.0 3.4 %collective-permute-start.1 = (f32[256,128]{1,0:T(8,128)S(1)}, f32[256,128]{1,0:T(8,128)S(1)}, u32[]{:S(2)}, u32[]{:S(2)}) collective-permute-start(f32[256,128]{1,0:T(8,128)S(1)} %bitcast_select_fusion), channel_id=1, source_target_pairs={{1,0},{2,1},{3,2},{4,3},{5,4},{6,5},{7,6},{0,7},{9,8},{10,9},{11,1... | collective-permute-start | bytes 393224 | tf_op jit(solution)/shard_map/ppermute | solution.py:22
  12.4 0.7 compare_select_fusion
  13.2 11.3 %scatter_custom_fusion = f32[32768]{0:T(1024)S(1)} fusion(s32[2048]{0:T(1024)S(1)} %bitcast.60, f32[2048]{0:T(1024)S(1)} %broadcast_bitcast_fusion, f32[]{:T(128)} %constant.60.clone.1), kind=kCustom, calls=%fused_computation.42 | custom fusion | flops 2048 | bytes 131076 | tf_op jit(solution)/shard_map/scatter-add | solution.py:56
  25.2 0.7 fusion.3
  26.1 14.1 %gather_fusion = f32[4096,128]{1,0:T(8,128)} fusion(f32[768,128]{1,0:T(8,128)S(1)} %pad_maximum_fusion, s32[4096]{0:T(1024)S(1)} %fusion.4), kind=kCustom, calls=%fused_computation.clone | custom fusion | bytes 4210688 | tf_op jit(solution)/shard_map/jit(_take)/gather | solution.py:33
  40.2 20.2 %reduce-scatter.2.cloned.1.call-done = f32[16,256]{1,0:T(8,128)} async-done(((f32[16,2048]{1,0:T(8,128)}), f32[16,256]{1,0:T(8,128)}) %reduce-scatter.2.cloned.1.call-update) | async-done | bytes 16400 | tf_op jit(solution)/shard_map/reduce_scatter | solution.py:58
  60.4 19.4 %psum.14 = f32[16,256]{1,0:T(8,128)S(1)} all-reduce(f32[16,256]{1,0:T(8,128)} %reduce-scatter.2.cloned.1.call-done), channel_id=1, replica_groups=mesh['comm'=4,'arc'=8] {'comm'}, use_global_device_ids=true, to_apply=%region_10.12 | all-reduce | flops 4096 | bytes 32768 | tf_op jit(solution)/shard_map/psum | solution.py:61
  80.4 3.6 %broadcast_select_fusion.7 = f32[4096,128]{1,0:T(8,128)S(1)} fusion(f32[4096,128]{1,0:T(8,128)} %gather_fusion, pred[4096]{0:T(1024)(128)(4,1)S(1)} %compare_and_fusion), kind=kLoop, calls=%fused_computation.24 | loop fusion | flops 524288 | bytes 4198400 | tf_op jit(solution)/shard_map/jit(_take)/select_n | solution.py:33
  84.0 12.5 %psum.15 = f32[]{:T(128)} all-reduce(f32[]{:T(128)} %multiply_reduce_fusion), channel_id=1, replica_groups=mesh['comm'=4,'arc'=8] {'arc'}, use_global_device_ids=true, to_apply=%region_12.14 | all-reduce | flops 1 | bytes 8 | tf_op jit(solution)/shard_map/psum | solution.py:63
  99.2 2.5 %collective-permute-done.3 = f32[256,128]{1,0:T(8,128)S(1)} collective-permute-done((f32[256,128]{1,0:T(8,128)S(1)}, f32[256,128]{1,0:T(8,128)S(1)}, u32[]{:S(2)}, u32[]{:S(2)}) %collective-permute-start.3) | collective-permute-done | bytes 131104 | tf_op jit(solution)/shard_map/ppermute | solution.py:22
  101.7 3.7 %collective-permute-done.2 = f32[256,128]{1,0:T(8,128)S(1)} collective-permute-done((f32[256,128]{1,0:T(8,128)S(1)}, f32[256,128]{1,0:T(8,128)S(1)}, u32[]{:S(2)}, u32[]{:S(2)}) %collective-permute-start.2) | collective-permute-done | bytes 131104 | tf_op jit(solution)/shard_map/ppermute | solution.py:20
  105.4 10.8 %gather_fusion.1 = f32[4096,128]{1,0:T(8,128)S(1)} fusion(f32[768,128]{1,0:T(8,128)S(1)} %pad_maximum_fusion.1, s32[4096]{0:T(1024)S(1)} %fusion.4), kind=kCustom, calls=%fused_computation.1.clone | custom fusion | bytes 4210688 | tf_op jit(solution)/shard_map/jit(_take)/gather | solution.py:33
  116.2 2.1 broadcast_select_fusion.6
  118.4 0.7 add_reduce_fusion.6
  119.7 3.2 %collective-permute-done.5 = f32[256,128]{1,0:T(8,128)S(1)} collective-permute-done((f32[256,128]{1,0:T(8,128)S(1)}, f32[256,128]{1,0:T(8,128)S(1)}, u32[]{:S(2)}, u32[]{:S(2)}) %collective-permute-start.5) | collective-permute-done | bytes 131104 | tf_op jit(solution)/shard_map/ppermute | solution.py:22
  122.9 2.3 collective-permute-done.4
  125.3 10.8 %gather_fusion.2 = f32[4096,128]{1,0:T(8,128)S(1)} fusion(f32[768,128]{1,0:T(8,128)S(1)} %pad_maximum_fusion.2, s32[4096]{0:T(1024)S(1)} %fusion.4), kind=kCustom, calls=%fused_computation.2.clone | custom fusion | bytes 4210688 | tf_op jit(solution)/shard_map/jit(_take)/gather | solution.py:33
  136.0 2.1 broadcast_select_fusion.5
  138.2 0.7 add_reduce_fusion.5
  139.5 3.2 %collective-permute-done.7 = f32[256,128]{1,0:T(8,128)S(1)} collective-permute-done((f32[256,128]{1,0:T(8,128)S(1)}, f32[256,128]{1,0:T(8,128)S(1)}, u32[]{:S(2)}, u32[]{:S(2)}) %collective-permute-start.7) | collective-permute-done | bytes 131104 | tf_op jit(solution)/shard_map/ppermute | solution.py:22
  142.7 2.0 collective-permute-done.6
  144.8 10.8 %gather_fusion.3 = f32[4096,128]{1,0:T(8,128)S(1)} fusion(f32[768,128]{1,0:T(8,128)S(1)} %pad_maximum_fusion.3, s32[4096]{0:T(1024)S(1)} %fusion.4), kind=kCustom, calls=%fused_computation.3.clone | custom fusion | bytes 4210688 | tf_op jit(solution)/shard_map/jit(_take)/gather | solution.py:33
  155.5 2.1 broadcast_select_fusion.4
  157.7 0.7 add_reduce_fusion.4
  158.4 0.8 collective-permute-start.9
  159.2 2.9 %collective-permute-done.9 = f32[256,128]{1,0:T(8,128)S(1)} collective-permute-done((f32[256,128]{1,0:T(8,128)S(1)}, f32[256,128]{1,0:T(8,128)S(1)}, u32[]{:S(2)}, u32[]{:S(2)}) %collective-permute-start.9) | collective-permute-done | bytes 131104 | tf_op jit(solution)/shard_map/ppermute | solution.py:22
  162.2 2.3 collective-permute-done.8
  164.6 10.8 %gather_fusion.4 = f32[4096,128]{1,0:T(8,128)S(1)} fusion(f32[768,128]{1,0:T(8,128)S(1)} %pad_maximum_fusion.4, s32[4096]{0:T(1024)S(1)} %fusion.4), kind=kCustom, calls=%fused_computation.4.clone | custom fusion | bytes 4210688 | tf_op jit(solution)/shard_map/jit(_take)/gather | solution.py:33
  175.3 2.1 broadcast_select_fusion.3
  177.5 0.7 add_reduce_fusion.3
  178.8 3.2 %collective-permute-done.11 = f32[256,128]{1,0:T(8,128)S(1)} collective-permute-done((f32[256,128]{1,0:T(8,128)S(1)}, f32[256,128]{1,0:T(8,128)S(1)}, u32[]{:S(2)}, u32[]{:S(2)}) %collective-permute-start.11) | collective-permute-done | bytes 131104 | tf_op jit(solution)/shard_map/ppermute | solution.py:22
  182.0 2.0 collective-permute-done.10
  184.1 10.8 %gather_fusion.5 = f32[4096,128]{1,0:T(8,128)S(1)} fusion(f32[768,128]{1,0:T(8,128)S(1)} %pad_maximum_fusion.5, s32[4096]{0:T(1024)S(1)} %fusion.4), kind=kCustom, calls=%fused_computation.5.clone | custom fusion | bytes 4210688 | tf_op jit(solution)/shard_map/jit(_take)/gather | solution.py:33
  194.9 2.1 broadcast_select_fusion.2
  197.0 0.7 add_reduce_fusion.2
  197.7 0.8 collective-permute-start.13
  198.6 2.9 %collective-permute-done.13 = f32[256,128]{1,0:T(8,128)S(1)} collective-permute-done((f32[256,128]{1,0:T(8,128)S(1)}, f32[256,128]{1,0:T(8,128)S(1)}, u32[]{:S(2)}, u32[]{:S(2)}) %collective-permute-start.13) | collective-permute-done | bytes 131104 | tf_op jit(solution)/shard_map/ppermute | solution.py:22
  201.5 2.3 collective-permute-done.12
  203.9 10.8 %gather_fusion.6 = f32[4096,128]{1,0:T(8,128)S(1)} fusion(f32[768,128]{1,0:T(8,128)S(1)} %pad_maximum_fusion.6, s32[4096]{0:T(1024)S(1)} %fusion.4), kind=kCustom, calls=%fused_computation.6.clone | custom fusion | bytes 4210688 | tf_op jit(solution)/shard_map/jit(_take)/gather | solution.py:33
  214.7 2.1 broadcast_select_fusion.1
  218.1 3.2 %collective-permute-done.15 = f32[256,128]{1,0:T(8,128)S(1)} collective-permute-done((f32[256,128]{1,0:T(8,128)S(1)}, f32[256,128]{1,0:T(8,128)S(1)}, u32[]{:S(2)}, u32[]{:S(2)}) %collective-permute-start.15) | collective-permute-done | bytes 131104 | tf_op jit(solution)/shard_map/ppermute | solution.py:22
  221.3 2.0 collective-permute-done.14
  223.4 10.8 %gather_fusion.7 = f32[4096,128]{1,0:T(8,128)S(1)} fusion(f32[768,128]{1,0:T(8,128)S(1)} %pad_maximum_fusion.7, s32[4096]{0:T(1024)S(1)} %fusion.4), kind=kCustom, calls=%fused_computation.7.clone | custom fusion | bytes 4210688 | tf_op jit(solution)/shard_map/jit(_take)/gather | solution.py:33
  234.2 2.1 broadcast_select_fusion
  236.3 0.7 add_reduce_fusion
  237.4 0.8 copy.12
  (61 shorter events, 7.1 us)
Async XLA Ops:
  7.2 6.0 %copy-start = (f32[16]{0:T(128)S(1)}, f32[16]{0:T(128)}, u32[]{:S(2)}) copy-start(f32[16]{0:T(128)} %param.17) | copy-start | bytes 196
  7.2 53.2 %reduce-scatter.2.cloned.1.call-start = ((), (), s32[]{:S(2)}) async-start(), calls=%async_computation.1 | async-start | bytes 147456 | tf_op jit(solution)/shard_map/reduce_scatter | solution.py:58
  9.0 17.0 %collective-permute-start.1 = (f32[256,128]{1,0:T(8,128)S(1)}, f32[256,128]{1,0:T(8,128)S(1)}, u32[]{:S(2)}, u32[]{:S(2)}) collective-permute-start(f32[256,128]{1,0:T(8,128)S(1)} %bitcast_select_fusion), channel_id=1, source_target_pairs={{1,0},{2,1},{3,2},{4,3},{5,4},{6,5},{7,6},{0,7},{9,8},{10,9},{11,1... | collective-permute-start | bytes 393224 | tf_op jit(solution)/shard_map/ppermute | solution.py:22
  12.4 13.6 %collective-permute-start = (f32[256,128]{1,0:T(8,128)S(1)}, f32[256,128]{1,0:T(8,128)S(1)}, u32[]{:S(2)}, u32[]{:S(2)}) collective-permute-start(f32[256,128]{1,0:T(8,128)S(1)} %bitcast_select_fusion), channel_id=1, source_target_pairs={{0,1},{1,2},{2,3},{3,4},{4,5},{5,6},{6,7},{7,0},{8,9},{9,10},{10,1... | collective-permute-start | bytes 393224 | tf_op jit(solution)/shard_map/ppermute | solution.py:20
  26.1 53.7 %copy-start.5 = (f32[16,256]{1,0:T(8,128)S(1)}, f32[16,256]{1,0:T(8,128)}, u32[]{:S(2)}) copy-start(f32[16,256]{1,0:T(8,128)} %param.15) | copy-start | bytes 49156
  80.4 16.8 %copy-start.6 = (f32[16,256]{1,0:T(8,128)S(1)}, f32[16,256]{1,0:T(8,128)}, u32[]{:S(2)}) copy-start(f32[16,256]{1,0:T(8,128)} %param.14) | copy-start | bytes 49156
  80.4 16.8 %copy-start.7 = (f32[16,256]{1,0:T(8,128)S(1)}, f32[16,256]{1,0:T(8,128)}, u32[]{:S(2)}) copy-start(f32[16,256]{1,0:T(8,128)} %param.13) | copy-start | bytes 49156
  84.0 14.5 %copy-start.8 = (s32[128]{0:T(128)S(1)}, s32[128]{0:T(128)}, u32[]{:S(2)}) copy-start(s32[128]{0:T(128)} %param.11) | copy-start | bytes 1540
  98.5 17.7 %copy-start.3 = (f32[256,128]{1,0:T(8,128)}, f32[256,128]{1,0:T(8,128)S(1)}, u32[]{:S(2)}) copy-start(f32[256,128]{1,0:T(8,128)S(1)} %add_reduce_fusion.7) | copy-start | bytes 393220
  98.6 3.0 %collective-permute-start.3 = (f32[256,128]{1,0:T(8,128)S(1)}, f32[256,128]{1,0:T(8,128)S(1)}, u32[]{:S(2)}, u32[]{:S(2)}) collective-permute-start(f32[256,128]{1,0:T(8,128)S(1)} %fusion.5), channel_id=1, source_target_pairs={{1,0},{2,1},{3,2},{4,3},{5,4},{6,5},{7,6},{0,7},{9,8},{10,9},{11,1... | collective-permute-start | bytes 393224 | tf_op jit(solution)/shard_map/ppermute | solution.py:22
  98.7 6.7 %collective-permute-start.2 = (f32[256,128]{1,0:T(8,128)S(1)}, f32[256,128]{1,0:T(8,128)S(1)}, u32[]{:S(2)}, u32[]{:S(2)}) collective-permute-start(f32[256,128]{1,0:T(8,128)S(1)} %fusion.5), channel_id=1, source_target_pairs={{0,1},{1,2},{2,3},{3,4},{4,5},{5,6},{6,7},{7,0},{8,9},{9,10},{10,1... | collective-permute-start | bytes 393224 | tf_op jit(solution)/shard_map/ppermute | solution.py:20
  119.1 3.8 %collective-permute-start.5 = (f32[256,128]{1,0:T(8,128)S(1)}, f32[256,128]{1,0:T(8,128)S(1)}, u32[]{:S(2)}, u32[]{:S(2)}) collective-permute-start(f32[256,128]{1,0:T(8,128)S(1)} %min.49), channel_id=1, source_target_pairs={{1,0},{2,1},{3,2},{4,3},{5,4},{6,5},{7,6},{0,7},{9,8},{10,9},{11,1... | collective-permute-start | bytes 393224 | tf_op jit(solution)/shard_map/ppermute | solution.py:22
  119.2 6.0 %collective-permute-start.4 = (f32[256,128]{1,0:T(8,128)S(1)}, f32[256,128]{1,0:T(8,128)S(1)}, u32[]{:S(2)}, u32[]{:S(2)}) collective-permute-start(f32[256,128]{1,0:T(8,128)S(1)} %min.49), channel_id=1, source_target_pairs={{0,1},{1,2},{2,3},{3,4},{4,5},{5,6},{6,7},{7,0},{8,9},{9,10},{10,1... | collective-permute-start | bytes 393224 | tf_op jit(solution)/shard_map/ppermute | solution.py:20
  138.9 3.8 %collective-permute-start.7 = (f32[256,128]{1,0:T(8,128)S(1)}, f32[256,128]{1,0:T(8,128)S(1)}, u32[]{:S(2)}, u32[]{:S(2)}) collective-permute-start(f32[256,128]{1,0:T(8,128)S(1)} %min.51), channel_id=1, source_target_pairs={{1,0},{2,1},{3,2},{4,3},{5,4},{6,5},{7,6},{0,7},{9,8},{10,9},{11,1... | collective-permute-start | bytes 393224 | tf_op jit(solution)/shard_map/ppermute | solution.py:22
  139.4 5.3 %collective-permute-start.6 = (f32[256,128]{1,0:T(8,128)S(1)}, f32[256,128]{1,0:T(8,128)S(1)}, u32[]{:S(2)}, u32[]{:S(2)}) collective-permute-start(f32[256,128]{1,0:T(8,128)S(1)} %min.51), channel_id=1, source_target_pairs={{0,1},{1,2},{2,3},{3,4},{4,5},{5,6},{6,7},{7,0},{8,9},{9,10},{10,1... | collective-permute-start | bytes 393224 | tf_op jit(solution)/shard_map/ppermute | solution.py:20
  158.4 3.8 %collective-permute-start.9 = (f32[256,128]{1,0:T(8,128)S(1)}, f32[256,128]{1,0:T(8,128)S(1)}, u32[]{:S(2)}, u32[]{:S(2)}) collective-permute-start(f32[256,128]{1,0:T(8,128)S(1)} %min.53), channel_id=1, source_target_pairs={{1,0},{2,1},{3,2},{4,3},{5,4},{6,5},{7,6},{0,7},{9,8},{10,9},{11,1... | collective-permute-start | bytes 393224 | tf_op jit(solution)/shard_map/ppermute | solution.py:22
  159.2 5.3 %collective-permute-start.8 = (f32[256,128]{1,0:T(8,128)S(1)}, f32[256,128]{1,0:T(8,128)S(1)}, u32[]{:S(2)}, u32[]{:S(2)}) collective-permute-start(f32[256,128]{1,0:T(8,128)S(1)} %min.53), channel_id=1, source_target_pairs={{0,1},{1,2},{2,3},{3,4},{4,5},{5,6},{6,7},{7,0},{8,9},{9,10},{10,1... | collective-permute-start | bytes 393224 | tf_op jit(solution)/shard_map/ppermute | solution.py:20
  178.2 3.8 %collective-permute-start.11 = (f32[256,128]{1,0:T(8,128)S(1)}, f32[256,128]{1,0:T(8,128)S(1)}, u32[]{:S(2)}, u32[]{:S(2)}) collective-permute-start(f32[256,128]{1,0:T(8,128)S(1)} %min.55), channel_id=1, source_target_pairs={{1,0},{2,1},{3,2},{4,3},{5,4},{6,5},{7,6},{0,7},{9,8},{10,9},{11,1... | collective-permute-start | bytes 393224 | tf_op jit(solution)/shard_map/ppermute | solution.py:22
  178.7 5.3 %collective-permute-start.10 = (f32[256,128]{1,0:T(8,128)S(1)}, f32[256,128]{1,0:T(8,128)S(1)}, u32[]{:S(2)}, u32[]{:S(2)}) collective-permute-start(f32[256,128]{1,0:T(8,128)S(1)} %min.55), channel_id=1, source_target_pairs={{0,1},{1,2},{2,3},{3,4},{4,5},{5,6},{6,7},{7,0},{8,9},{9,10},{10,1... | collective-permute-start | bytes 393224 | tf_op jit(solution)/shard_map/ppermute | solution.py:20
  197.7 6.2 %copy-start.1 = (f32[256,128]{1,0:T(8,128)}, f32[256,128]{1,0:T(8,128)S(1)}, u32[]{:S(2)}) copy-start(f32[256,128]{1,0:T(8,128)S(1)} %add_reduce_fusion.2) | copy-start | bytes 393220
  197.7 3.8 %collective-permute-start.13 = (f32[256,128]{1,0:T(8,128)S(1)}, f32[256,128]{1,0:T(8,128)S(1)}, u32[]{:S(2)}, u32[]{:S(2)}) collective-permute-start(f32[256,128]{1,0:T(8,128)S(1)} %min.57), channel_id=1, source_target_pairs={{1,0},{2,1},{3,2},{4,3},{5,4},{6,5},{7,6},{0,7},{9,8},{10,9},{11,1... | collective-permute-start | bytes 393224 | tf_op jit(solution)/shard_map/ppermute | solution.py:22
  198.6 5.3 %collective-permute-start.12 = (f32[256,128]{1,0:T(8,128)S(1)}, f32[256,128]{1,0:T(8,128)S(1)}, u32[]{:S(2)}, u32[]{:S(2)}) collective-permute-start(f32[256,128]{1,0:T(8,128)S(1)} %min.57), channel_id=1, source_target_pairs={{0,1},{1,2},{2,3},{3,4},{4,5},{5,6},{6,7},{7,0},{8,9},{9,10},{10,1... | collective-permute-start | bytes 393224 | tf_op jit(solution)/shard_map/ppermute | solution.py:20
  217.6 3.8 %collective-permute-start.15 = (f32[256,128]{1,0:T(8,128)S(1)}, f32[256,128]{1,0:T(8,128)S(1)}, u32[]{:S(2)}, u32[]{:S(2)}) collective-permute-start(f32[256,128]{1,0:T(8,128)S(1)} %min.59), channel_id=1, source_target_pairs={{1,0},{2,1},{3,2},{4,3},{5,4},{6,5},{7,6},{0,7},{9,8},{10,9},{11,1... | collective-permute-start | bytes 393224 | tf_op jit(solution)/shard_map/ppermute | solution.py:22
  218.1 5.3 %collective-permute-start.14 = (f32[256,128]{1,0:T(8,128)S(1)}, f32[256,128]{1,0:T(8,128)S(1)}, u32[]{:S(2)}, u32[]{:S(2)}) collective-permute-start(f32[256,128]{1,0:T(8,128)S(1)} %min.59), channel_id=1, source_target_pairs={{0,1},{1,2},{2,3},{3,4},{4,5},{5,6},{6,7},{7,0},{8,9},{9,10},{10,1... | collective-permute-start | bytes 393224 | tf_op jit(solution)/shard_map/ppermute | solution.py:20
  236.3 0.9 copy-start.2
  236.3 1.0 copy-start.4
Sparse Core Ops, SparseCore 0:
  25.3 35.0 reduce-scatter.1
where the time goes:
time: 245 us
  local copies, waits for them, and re-layouts  92.3 us (38%)
  waiting for transfers between devices  58.3 us (24%)
  other arithmetic  39.5 us (16%)
  blocking collectives  31.8 us (13%)
  between operations  15.2 us (6%)
  starting transfers between devices  7.89 us (3%)
    gather x8, local copies, waits for them, and re-layouts, relax(): jnp.take(window, local_index, axis=0)  89.5 us
    ppermute x8, waiting for transfers between devices, with_halo(): lax.ppermute(head, axis, [((i + 1) % count, i) for i in range(count)])  21.2 us
    reduce_scatter x1, waiting for transfers between devices, shards(): lax.psum_scatter(flattened.reshape(degree, node_count), 'arc', scatter_di...  20.2 us
    psum x1, blocking collectives, shards(): arc_flow = lax.psum(partial_flow, 'comm')  19.4 us
    select_n x8, other arithmetic, relax(): jnp.take(window, local_index, axis=0)  18.6 us
    ppermute x8, waiting for transfers between devices, with_halo(): lax.ppermute(tail, axis, [(i, (i + 1) % count) for i in range(count)])  16.9 us
    psum x1, blocking collectives, shards(): square_sum = lax.psum(jnp.sum(gradient * gradient), 'arc')  12.5 us
    scatter-add x1, other arithmetic, shards(): jnp.zeros((degree * node_count,), jnp.float32).at[path_arcs.reshape(-1)]  11.3 us
  transfers between devices with their start and end apart: 17, of which 15 were waited for; matrix products, arithmetic and copies ran while one was open for 11% of the time, Pallas kernels for 0%

commit v1 on v0

v1 whole, which is shorter than its diff:
```python
import functools

import jax
import jax.numpy as jnp
from jax import lax
from jax.experimental import pallas as pl
from jax.experimental.pallas import tpu as pltpu
from jax.sharding import PartitionSpec as P

SWEEPS = 8
REACH = 2
LANES = 128
SUB = 8

step_size = 0.25
eps_value = 1e-06


def vmem_spec():
    return pl.BlockSpec(memory_space=pltpu.VMEM)


def smem_spec():
    return pl.BlockSpec(memory_space=pltpu.SMEM)


def three_parts(x):
    first = x.astype(jnp.bfloat16)
    rest = x - first.astype(jnp.float32)
    second = rest.astype(jnp.bfloat16)
    third = (rest - second.astype(jnp.float32)).astype(jnp.bfloat16)
    return first, second, third


def pack_kernel(
    node_count, demand_ref, dist_ref, tail_ref, cost_ref, price_ref, path_ref, out_ref
):
    peers = out_ref.shape[0]
    degree, shard_nodes = tail_ref.shape
    shard_blocks = shard_nodes // LANES
    mine = dist_ref.shape[0] // peers
    block_total = node_count // LANES
    routes, hops = path_ref.shape

    path = path_ref[...]
    slot = path // node_count
    node = path - slot * node_count
    block = node // LANES
    lane = node - block * LANES
    row = block * degree + slot
    row_total = block_total * degree
    row_ids = lax.broadcasted_iota(jnp.int32, (row_total, hops), 0)
    lane_ids = lax.broadcasted_iota(jnp.int32, (LANES, hops), 0)
    left = [[], [], []]
    right = []
    for k in range(routes):
        hit = row_ids == row[k : k + 1, :]
        amount = jnp.full((1, hops), demand_ref[k], jnp.float32)
        for part, piece in enumerate(three_parts(amount)):
            left[part].append(
                jnp.where(hit, piece.astype(jnp.float32), jnp.float32(0.0)).astype(jnp.bfloat16)
            )
        right.append(
            jnp.where(lane_ids == lane[k : k + 1, :], jnp.float32(1.0), jnp.float32(0.0)).astype(
                jnp.bfloat16
            )
        )
    right = jnp.concatenate(right, axis=1)
    flow = None
    for part in (2, 1, 0):
        term = lax.dot_general(
            jnp.concatenate(left[part], axis=1),
            right,
            (((1,), (1,)), ((), ())),
            preferred_element_type=jnp.float32,
        )
        flow = term if flow is None else flow + term

    tail = tail_ref[...].astype(jnp.float32)
    weight = cost_ref[...] + price_ref[...]
    arc_rows = degree * shard_blocks
    base = mine * shard_blocks
    for j in range(peers):
        for b in range(shard_blocks):
            cols = slice(b * LANES, (b + 1) * LANES)
            out_ref[j, b * mine : (b + 1) * mine, :] = dist_ref[j * mine : (j + 1) * mine, cols]
            out_ref[j, base + b * degree : base + (b + 1) * degree, :] = tail[:, cols]
            start = base + arc_rows + b * degree
            out_ref[j, start : start + degree, :] = weight[:, cols]
        start = base + 2 * arc_rows
        out_ref[j, start : start + arc_rows, :] = flow[j * arc_rows : (j + 1) * arc_rows, :]


def halo_store(ref, k, half, groups, span, value):
    blocks = groups * SUB
    base = k * span + SUB
    ref[base + half * SUB : base + (half + 1) * SUB, :] = value
    if half == groups - 1:
        ref[base - REACH : base, :] = value[SUB - REACH :, :]
    if half == 0:
        ref[base + blocks : base + blocks + REACH, :] = value[:REACH, :]


def unpack_kernel(mine, degree, source_ref, first_ref, buf_ref, x_ref, idx_ref, off_ref, w_ref, flow_ref, stage, stage_idx):
    peers = buf_ref.shape[0]
    span = x_ref.shape[0] // mine
    block_total = span - 2 * SUB
    groups = block_total // SUB
    shard_blocks = block_total // peers
    arc_rows = degree * shard_blocks
    base = mine * shard_blocks
    total = None
    for i in range(peers):
        part = buf_ref[i, base + 2 * arc_rows : base + 3 * arc_rows, :]
        total = part if total is None else total + part
    flow_ref[...] = total
    for i in range(peers):
        for b in range(shard_blocks):
            blk = i * shard_blocks + b
            stage[pl.ds(blk, mine, stride=block_total), :] = buf_ref[i, b * mine : (b + 1) * mine, :]
            s0 = base + b * degree
            stage_idx[pl.ds(blk, degree, stride=block_total), :] = buf_ref[i, s0 : s0 + degree, :]
            s1 = base + arc_rows + b * degree
            w_ref[pl.ds(blk, degree, stride=block_total), :] = buf_ref[i, s1 : s1 + degree, :]
    rows = lax.broadcasted_iota(jnp.int32, (SUB, LANES), 0)
    lanes = lax.broadcasted_iota(jnp.int32, (SUB, LANES), 1)
    first = first_ref[0]
    for half in range(groups):
        node = (rows + half * SUB) * LANES + lanes
        for k in range(mine):
            at = k * block_total + half * SUB
            value = jnp.where(node == source_ref[first + k], jnp.float32(0.0), stage[at : at + SUB, :])
            halo_store(x_ref, k, half, groups, span, value)
        for s in range(degree):
            at = s * block_total + half * SUB
            tail = stage_idx[at : at + SUB, :].astype(jnp.int32)
            tail_block = tail // LANES
            idx_ref[at : at + SUB, :] = tail - tail_block * LANES
            off = tail_block - (rows + half * SUB) + REACH
            off = jnp.where(off < 0, off + block_total, off)
            off_ref[at : at + SUB, :] = jnp.where(off >= block_total, off - block_total, off)


def sweep_once(mine, degree, src, dst, idx_ref, off_ref, w_ref):
    span = src.shape[0] // mine
    block_total = span - 2 * SUB
    groups = block_total // SUB
    for half in range(groups):
        best = [src[k * span + SUB + half * SUB : k * span + SUB + (half + 1) * SUB, :] for k in range(mine)]
        for s in range(degree):
            at = s * block_total + half * SUB
            idx = idx_ref[at : at + SUB, :]
            off = off_ref[at : at + SUB, :]
            w = w_ref[at : at + SUB, :]
            masks = [off == o for o in range(2 * REACH)]
            for k in range(mine):
                base = k * span + SUB + half * SUB - REACH
                picked = None
                for o in reversed(range(2 * REACH + 1)):
                    value = jnp.take_along_axis(
                        src[base + o : base + o + SUB, :], idx, axis=1, mode="promise_in_bounds"
                    )
                    picked = value if picked is None else jnp.where(masks[o], value, picked)
                best[k] = jnp.minimum(best[k], picked + w)
        for k in range(mine):
            halo_store(dst, k, half, groups, span, best[k])


def sweep_kernel(mine, degree, count, x_ref, idx_ref, off_ref, w_ref, out_ref, other):
    span = x_ref.shape[0] // mine
    args = (idx_ref, off_ref, w_ref)
    pairs, odd = divmod(count, 2)
    if odd:
        sweep_once(mine, degree, x_ref, out_ref, *args)
    else:
        out_ref[...] = x_ref[...]
    if pairs:
        @pl.loop(0, pairs)
        def _(_):
            sweep_once(mine, degree, out_ref, other, *args)
            sweep_once(mine, degree, other, out_ref, *args)


def out_kernel(mine, x_ref, flow_ref, cap_ref, out_ref, grad_ref):
    peers = out_ref.shape[0]
    span = x_ref.shape[0] // mine
    block_total = span - 2 * SUB
    shard_blocks = block_total // peers
    degree = cap_ref.shape[0]
    square = None
    for b in range(shard_blocks):
        cols = slice(b * LANES, (b + 1) * LANES)
        grad = flow_ref[b * degree : (b + 1) * degree, :] - cap_ref[:, cols]
        grad_ref[:, cols] = grad
        term = grad * grad
        square = term if square is None else square + term
    folded = jnp.sum(square.reshape(degree // SUB, SUB, LANES), axis=0)
    base = mine * shard_blocks
    for i in range(peers):
        for b in range(shard_blocks):
            blk = SUB + i * shard_blocks + b
            out_ref[i, b * mine : (b + 1) * mine, :] = x_ref[pl.ds(blk, mine, stride=span), :]
        out_ref[i, base : base + SUB, :] = folded


def final_kernel(mine, arc_total, buf_ref, grad_ref, price_ref, dist_ref, new_ref):
    peers = buf_ref.shape[0]
    shard_blocks = dist_ref.shape[1] // LANES
    base = mine * shard_blocks
    total = None
    for i in range(peers):
        for b in range(shard_blocks):
            dist_ref[i * mine : (i + 1) * mine, b * LANES : (b + 1) * LANES] = buf_ref[
                i, b * mine : (b + 1) * mine, :
            ]
        part = buf_ref[i, base : base + SUB, :]
        total = part if total is None else total + part
    square_sum = jnp.sum(jnp.sum(total, axis=1, keepdims=True), axis=0, keepdims=True)
    scale_root = jnp.sqrt(square_sum / arc_total + eps_value)
    new_ref[...] = jnp.maximum(
        price_ref[...] + step_size * grad_ref[...] / scale_root, jnp.float32(0.0)
    )


def comm_sum_parts(sweeps, size):
    steps = max(size.bit_length() - 1, 1)
    return [sweeps // steps + (1 if n < sweeps % steps else 0) for n in range(steps)]


def shards(prev_dist, source_node, arc_tail, base_cost, arc_price, capacity, path_arcs, demand):
    commodities, shard_nodes = prev_dist.shape
    peers = lax.axis_size("arc")
    groups = lax.axis_size("comm")
    node_count = shard_nodes * peers
    degree = arc_tail.shape[0]
    mine = commodities // peers
    shard_blocks = shard_nodes // LANES
    block_total = node_count // LANES
    span = block_total + 2 * SUB
    arc_rows = degree * shard_blocks
    f32, i32 = jnp.float32, jnp.int32
    shape = jax.ShapeDtypeStruct
    v, s = vmem_spec, smem_spec

    packed = pl.pallas_call(
        functools.partial(pack_kernel, node_count),
        out_shape=shape((peers, mine * shard_blocks + 3 * arc_rows, LANES), f32),
        in_specs=[s(), v(), v(), v(), v(), v()],
        out_specs=v(),
        name="pack",
    )(demand, prev_dist, arc_tail, base_cost, arc_price, path_arcs)
    received = lax.all_to_all(packed, "arc", 0, 0, tiled=True)
    first = (lax.axis_index("arc") * mine).astype(i32).reshape(1)
    table = degree * block_total
    x, idx, off, w, flow = pl.pallas_call(
        functools.partial(unpack_kernel, mine, degree),
        out_shape=(
            shape((mine * span, LANES), f32),
            shape((table, LANES), i32),
            shape((table, LANES), i32),
            shape((table, LANES), f32),
            shape((arc_rows, LANES), f32),
        ),
        in_specs=[s(), s(), v()],
        out_specs=(v(), v(), v(), v(), v()),
        scratch_shapes=[
            pltpu.VMEM((mine * block_total, LANES), f32),
            pltpu.VMEM((table, LANES), f32),
        ],
        name="unpack",
    )(source_node, first, received)

    for step, count in enumerate(comm_sum_parts(SWEEPS, groups)):
        distance = 1 << step
        if distance < groups:
            arrived = lax.ppermute(flow, "comm", [(i, i ^ distance) for i in range(groups)])
        x = pl.pallas_call(
            functools.partial(sweep_kernel, mine, degree, count),
            out_shape=shape((mine * span, LANES), f32),
            in_specs=[v(), v(), v(), v()],
            out_specs=v(),
            scratch_shapes=[pltpu.VMEM((mine * span, LANES), f32)],
            name="sweeps",
        )(x, idx, off, w)
        if distance < groups:
            flow = flow + arrived

    back, gradient = pl.pallas_call(
        functools.partial(out_kernel, mine),
        out_shape=(
            shape((peers, mine * shard_blocks + SUB, LANES), f32),
            shape((degree, shard_nodes), f32),
        ),
        in_specs=[v(), v(), v()],
        out_specs=(v(), v()),
        name="give_back",
    )(x, flow, capacity)
    final = lax.all_to_all(back, "arc", 0, 0, tiled=True)
    return pl.pallas_call(
        functools.partial(final_kernel, mine, degree * node_count),
        out_shape=(shape((commodities, shard_nodes), f32), shape((degree, shard_nodes), f32)),
        in_specs=[v(), v(), v()],
        out_specs=(v(), v()),
        name="finish",
    )(final, gradient, arc_price)


def solution(mesh):
    in_specs = (
        P("comm", "arc"),
        P("comm"),
        P(None, "arc"),
        P(None, "arc"),
        P(None, "arc"),
        P(None, "arc"),
        P(("comm", "arc"), None),
        P(("comm", "arc")),
    )
    out_specs = (P("comm", "arc"), P(None, "arc"))
    return jax.shard_map(shards, mesh=mesh, in_specs=in_specs, out_specs=out_specs, check_vma=False)
```

time: 245 us -> 70.2 us (0.29)
  local copies, waits for them, and re-layouts: 92.3 us -> 0.79 us
  waiting for transfers between devices: 58.3 us -> 12.1 us
  other arithmetic: 39.5 us -> 1.33 us
  Pallas kernels: 0 us -> 35.7 us
  blocking collectives: 31.8 us -> 9.85 us
  between operations: 15.2 us -> 0.64 us
    gather x8 -> x0, local copies, waits for them, and re-layouts: 89.5 us -> none  [relax(): jnp.take(window, local_index, axis=0)]
    ppermute x16 -> x2, waiting for transfers between devices: 38.1 us -> 2.37 us  [shards(): lax.ppermute(flow, 'comm', [(i, i ^ distance) for i in range(groups)])]
    pallas_call x0 -> x6, Pallas kernels: none -> 35.7 us  [the longest x2 27.4 us: shards(): pl.pallas_call(functools.partial(sweep_kernel, mine, degree, count), out_...]
    psum x2 -> x0, blocking collectives: 31.8 us -> none  [the longest x1 19.4 us: shards(): arc_flow = lax.psum(partial_flow, 'comm')]
    reduce_scatter x1 -> x0, waiting for transfers between devices: 20.2 us -> none  [shards(): lax.psum_scatter(flattened.reshape(degree, node_count), 'arc', scatter_di...]
    select_n x10 -> x0, other arithmetic: 20.1 us -> none  [the longest x8 18.6 us: relax(): jnp.take(window, local_index, axis=0)]
    scatter-add x1 -> x0, other arithmetic: 11.3 us -> none  [shards(): jnp.zeros((degree * node_count,), jnp.float32).at[path_arcs.reshape(-1)]]
    all_to_all x0 -> x1, blocking collectives: none -> 9.85 us  [shards(): final = lax.all_to_all(back, 'arc', 0, 0, tiled=True)]
  transfers between devices with their start and end apart: 17 -> 3, of which waited for: 15 -> 2; matrix products, arithmetic and copies ran while one was open for 11% -> 0% of each run, Pallas kernels for 0% -> 39%
where the time goes in v1:
time: 70.2 us; the launch traced here: 69.7 us
  Pallas kernels  35.7 us (51%)
  waiting for transfers between devices  12.1 us (17%)
  blocking collectives  9.85 us (14%)
  starting transfers between devices  9.36 us (13%)
  other arithmetic  1.33 us (2%)
  local copies, waits for them, and re-layouts  0.79 us (1%)
    pallas_call x2, Pallas kernels, shards(): pl.pallas_call(functools.partial(sweep_kernel, mine, degree, count), out_...  27.4 us
    all_to_all x1, blocking collectives, shards(): final = lax.all_to_all(back, 'arc', 0, 0, tiled=True)  9.85 us
    all_to_all x1, waiting for transfers between devices, shards(): received = lax.all_to_all(packed, 'arc', 0, 0, tiled=True)  9.71 us
    all_to_all x1, starting transfers between devices, shards(): received = lax.all_to_all(packed, 'arc', 0, 0, tiled=True)  5.2 us
    ppermute x2, starting transfers between devices, shards(): lax.ppermute(flow, 'comm', [(i, i ^ distance) for i in range(groups)])  4.17 us
    pallas_call x1, Pallas kernels, shards(): pl.pallas_call(functools.partial(pack_kernel, node_count), out_shape=shap...  2.79 us
    ppermute x2, waiting for transfers between devices, shards(): lax.ppermute(flow, 'comm', [(i, i ^ distance) for i in range(groups)])  2.37 us
    pallas_call x1, Pallas kernels, shards(): pl.pallas_call(functools.partial(unpack_kernel, mine, degree), out_shape=...  2.05 us
  transfers between devices with their start and end apart: 3, of which 2 were waited for; matrix products, arithmetic and copies ran while one was open for 0% of the time, Pallas kernels for 39%

profile of v1, /device:TPU:0, one launch (start us, length us, event | category | flops | bytes accessed | tf_op | source)
XLA Modules:
  0.0 69.7 jit_solution(10673685853250387909)
XLA Ops:
  0.6 2.8 %pack.1 = f32[8,128,128]{2,1,0:T(8,128)} custom-call(f32[16]{0:T(128)} %demand_ref.1, f32[128,256]{1,0:T(8,128)} %dist_ref.1, s32[16,256]{1,0:T(8,128)} %tail_ref.1, f32[16,256]{1,0:T(8,128)} %cost_ref.1, f32[16,256]{1,0:T(8,128)} %price_ref.3, s32[16,128]{1,0:T(8,128)} %path_ref.1), custom_call_target="tpu_custom_call" | custom-call | tf_op jit(solution)/shard_map/pack/pallas_call | solution.py:245
  3.4 5.2 %all-to-all-start = ((f32[8,128,128]{2,1,0:T(8,128)}), f32[8,128,128]{2,1,0:T(8,128)S(1)}, u32[]{:S(2)}, u32[]{:S(2)}) async-start(f32[8,128,128]{2,1,0:T(8,128)} %pack.1), calls=%async_computation | async-start | bytes 1048576 | tf_op jit(solution)/shard_map/all_to_all | solution.py:252
  8.6 9.7 %all-to-all-done.buf_ref = f32[8,128,128]{2,1,0:T(8,128)S(1)} async-done(((f32[8,128,128]{2,1,0:T(8,128)}), f32[8,128,128]{2,1,0:T(8,128)S(1)}, u32[]{:S(2)}, u32[]{:S(2)}) %all-to-all-start) | async-done | bytes 524320 | tf_op jit(solution)/shard_map/all_to_all | solution.py:252
  18.3 0.0 copy-start
  18.3 0.8 %copy-done = f32[8,128,128]{2,1,0:T(8,128)} copy-done((f32[8,128,128]{2,1,0:T(8,128)}, f32[8,128,128]{2,1,0:T(8,128)S(1)}, u32[]{:S(2)}) %copy-start) | copy-done | bytes 524312
  19.1 2.1 %unpack.1 = (f32[512,128]{1,0:T(8,128)}, s32[256,128]{1,0:T(8,128)}, s32[256,128]{1,0:T(8,128)}, f32[256,128]{1,0:T(8,128)}, f32[32,128]{1,0:T(8,128)}) custom-call(s32[128]{0:T(128)} %source_ref.1, s32[1]{0:T(128)} %bitcast.first_ref, f32[8,128,128]{2,1,0:T(8,128)} %copy-done), custom_call_target="tpu_custom_call" | custom-call | tf_op jit(solution)/shard_map/unpack/pallas_call | solution.py:255
  21.2 1.6 %collective-permute-start = (f32[32,128]{1,0:T(8,128)}, f32[32,128]{1,0:T(8,128)S(1)}, u32[]{:S(2)}, u32[]{:S(2)}) collective-permute-start(f32[32,128]{1,0:T(8,128)} %get-tuple-element.13), channel_id=1, source_target_pairs={{0,8},{8,0},{16,24},{24,16},{1,9},{9,1},{17,25},{25,17},{2,10},{10... | collective-permute-start | bytes 49160 | tf_op jit(solution)/shard_map/ppermute | solution.py:276
  22.8 2.4 %collective-permute-done = f32[32,128]{1,0:T(8,128)S(1)} collective-permute-done((f32[32,128]{1,0:T(8,128)}, f32[32,128]{1,0:T(8,128)S(1)}, u32[]{:S(2)}, u32[]{:S(2)}) %collective-permute-start) | collective-permute-done | bytes 16416 | tf_op jit(solution)/shard_map/ppermute | solution.py:276
  25.1 0.7 %add.6 = f32[32,128]{1,0:T(8,128)S(1)} add(f32[32,128]{1,0:T(8,128)} %get-tuple-element.13, f32[32,128]{1,0:T(8,128)S(1)} %collective-permute-done) | non-fusion elementwise | flops 4096 | bytes 49152 | tf_op jit(solution)/shard_map/add | solution.py:286
  25.9 2.6 %collective-permute-start.1 = (f32[32,128]{1,0:T(8,128)S(1)}, f32[32,128]{1,0:T(8,128)S(1)}, u32[]{:S(2)}, u32[]{:S(2)}) collective-permute-start(f32[32,128]{1,0:T(8,128)S(1)} %add.6), channel_id=1, source_target_pairs={{0,16},{8,24},{16,0},{24,8},{1,17},{9,25},{17,1},{25,9},{2,18},{10... | collective-permute-start | bytes 49160 | tf_op jit(solution)/shard_map/ppermute | solution.py:276
  28.4 13.7 %sweeps.2.x_ref = f32[512,128]{1,0:T(8,128)} custom-call(f32[512,128]{1,0:T(8,128)} %get-tuple-element.9.x_ref, s32[256,128]{1,0:T(8,128)} %get-tuple-element.10.idx_ref, s32[256,128]{1,0:T(8,128)} %get-tuple-element.11.off_ref, f32[256,128]{1,0:T(8,128)} %get-tuple-element.12.w_ref), custom_call_target="tpu_custom_call" | custom-call | tf_op jit(solution)/shard_map/sweeps/pallas_call | solution.py:277
  42.2 13.7 %sweeps.3.x_ref = f32[512,128]{1,0:T(8,128)} custom-call(f32[512,128]{1,0:T(8,128)} %sweeps.2.x_ref, s32[256,128]{1,0:T(8,128)} %get-tuple-element.10.idx_ref, s32[256,128]{1,0:T(8,128)} %get-tuple-element.11.off_ref, f32[256,128]{1,0:T(8,128)} %get-tuple-element.12.w_ref), custom_call_target="tpu_custom_call" | custom-call | tf_op jit(solution)/shard_map/sweeps/pallas_call | solution.py:277
  55.9 0.0 collective-permute-done.1
  55.9 0.6 add.7.flow_ref
  56.5 1.7 %give_back.1 = (f32[8,40,128]{2,1,0:T(8,128)}, f32[16,256]{1,0:T(8,128)}) custom-call(f32[512,128]{1,0:T(8,128)} %sweeps.3.x_ref, f32[32,128]{1,0:T(8,128)} %add.7.flow_ref, f32[16,256]{1,0:T(8,128)} %cap_ref.1), custom_call_target="tpu_custom_call" | custom-call | tf_op jit(solution)/shard_map/give_back/pallas_call | solution.py:288
  58.2 9.9 %all_to_all.10.buf_ref = f32[8,40,128]{2,1,0:T(8,128)} all-to-all(f32[8,40,128]{2,1,0:T(8,128)} %get-tuple-element.14), channel_id=1, replica_groups=mesh['comm'=4,'arc'=8] {'arc'}, dimensions={0} | all-to-all | bytes 327680 | tf_op jit(solution)/shard_map/all_to_all | solution.py:298
  68.1 1.6 %finish.1 = (f32[128,256]{1,0:T(8,128)}, f32[16,256]{1,0:T(8,128)}) custom-call(f32[8,40,128]{2,1,0:T(8,128)} %all_to_all.10.buf_ref, f32[16,256]{1,0:T(8,128)} %get-tuple-element.15.grad_ref, f32[16,256]{1,0:T(8,128)} %price_ref.3), custom_call_target="tpu_custom_call" | custom-call | tf_op jit(solution)/shard_map/finish/pallas_call | solution.py:299
Async XLA Ops:
  3.4 14.9 %all-to-all-start = ((f32[8,128,128]{2,1,0:T(8,128)}), f32[8,128,128]{2,1,0:T(8,128)S(1)}, u32[]{:S(2)}, u32[]{:S(2)}) async-start(f32[8,128,128]{2,1,0:T(8,128)} %pack.1), calls=%async_computation | async-start | bytes 1048576 | tf_op jit(solution)/shard_map/all_to_all | solution.py:252
  18.3 0.8 %copy-start = (f32[8,128,128]{2,1,0:T(8,128)}, f32[8,128,128]{2,1,0:T(8,128)S(1)}, u32[]{:S(2)}) copy-start(f32[8,128,128]{2,1,0:T(8,128)S(1)} %all-to-all-done.buf_ref) | copy-start | bytes 1572868
  21.2 3.9 %collective-permute-start = (f32[32,128]{1,0:T(8,128)}, f32[32,128]{1,0:T(8,128)S(1)}, u32[]{:S(2)}, u32[]{:S(2)}) collective-permute-start(f32[32,128]{1,0:T(8,128)} %get-tuple-element.13), channel_id=1, source_target_pairs={{0,8},{8,0},{16,24},{24,16},{1,9},{9,1},{17,25},{25,17},{2,10},{10... | collective-permute-start | bytes 49160 | tf_op jit(solution)/shard_map/ppermute | solution.py:276
  25.9 30.0 %collective-permute-start.1 = (f32[32,128]{1,0:T(8,128)S(1)}, f32[32,128]{1,0:T(8,128)S(1)}, u32[]{:S(2)}, u32[]{:S(2)}) collective-permute-start(f32[32,128]{1,0:T(8,128)S(1)} %add.6), channel_id=1, source_target_pairs={{0,16},{8,24},{16,0},{24,8},{1,17},{9,25},{17,1},{25,9},{2,18},{10... | collective-permute-start | bytes 49160 | tf_op jit(solution)/shard_map/ppermute | solution.py:276

commit v2 on v1

--- a/solution.py
+++ b/solution.py
@@ -8,9 +8,13 @@
 from jax.sharding import PartitionSpec as P
 
 SWEEPS = 8
+EARLY_SWEEPS = 2
 REACH = 2
 LANES = 128
 SUB = 8
+VMEM_GRANT = 24 * 1024 * 1024
+
+TURNS = ((None, None), (0, 1), (2, 3), (4, 5), (6, 0), (1, 3))
 
 step_size = 0.25
 eps_value = 1e-06
@@ -101,7 +105,139 @@
         ref[base + blocks : base + blocks + REACH, :] = value[:REACH, :]
 
 
-def unpack_kernel(mine, degree, source_ref, first_ref, buf_ref, x_ref, idx_ref, off_ref, w_ref, flow_ref, stage, stage_idx):
+def flow_kernel(rows, buf_ref, flow_ref):
+    total = None
+    for i in range(buf_ref.shape[0]):
+        part = buf_ref[i, buf_ref.shape[1] - rows :, :]
+        total = part if total is None else total + part
+    flow_ref[...] = total
+
+
+def plan_rounds(degree, block_total, half, stage, idx_ref, w_ref, left_idx_ref, left_off_ref, left_w_ref):
+    groups = block_total // SUB
+    width = 2 * REACH + 1
+    rows = lax.broadcasted_iota(jnp.int32, (SUB, LANES), 0) + half * SUB
+    used = jnp.zeros((SUB, LANES), jnp.int32)
+    over = jnp.full((SUB, LANES), degree, jnp.int32)
+    lanes_of, weights, bits = [], [], []
+    for s in range(degree):
+        at = s * block_total + half * SUB
+        tail = stage[at : at + SUB, :].astype(jnp.int32)
+        block = tail // LANES
+        lane = tail - block * LANES
+        off = block - rows + REACH
+        off = jnp.where(off < 0, off + block_total, off)
+        off = jnp.where(off >= block_total, off - block_total, off)
+        weight = w_ref[at : at + SUB, :]
+        turned = [jnp.left_shift(1, off)]
+        for _ in range(3):
+            last = turned[-1]
+            turned.append(((last << 1) | (last >> (width - 1))) & (2**width - 1))
+        open_rounds = jnp.zeros_like(used)
+        for j, (low, high) in enumerate(TURNS):
+            if low is None:
+                spot = turned[0]
+            else:
+                by_low = ((lane >> low) & 1) == 1
+                by_high = ((lane >> high) & 1) == 1
+                spot = jnp.where(
+                    by_high,
+                    jnp.where(by_low, turned[3], turned[2]),
+                    jnp.where(by_low, turned[1], turned[0]),
+                )
+            open_rounds = open_rounds | (spot << (width * j))
+        open_rounds = open_rounds & ~used
+        bit = open_rounds & -open_rounds
+        used = used | bit
+        lost = bit == 0
+        over = jnp.minimum(over, jnp.where(lost, s, degree))
+        left_idx_ref[at : at + SUB, :] = lane
+        left_off_ref[at : at + SUB, :] = off
+        left_w_ref[at : at + SUB, :] = jnp.where(lost, weight, jnp.float32(jnp.inf))
+        lanes_of.append(lane)
+        weights.append(weight)
+        bits.append(bit)
+    for r in range(width * len(TURNS)):
+        idx = jnp.zeros((SUB, LANES), jnp.int32)
+        weight = jnp.full((SUB, LANES), jnp.inf, jnp.float32)
+        for s in range(degree):
+            hit = bits[s] == (1 << r)
+            idx = jnp.where(hit, lanes_of[s], idx)
+            weight = jnp.where(hit, weights[s], weight)
+        at = (r * groups + half) * SUB
+        idx_ref[at : at + SUB, :] = idx
+        w_ref[degree * block_total + at : degree * block_total + at + SUB, :] = weight
+    return over
+
+
+def sweep_once(mine, degree, first_over, src, dst, tables):
+    idx_ref, w_ref, left_idx_ref, left_off_ref, left_w_ref = tables
+    span = src.shape[0] // mine
+    block_total = span - 2 * SUB
+    groups = block_total // SUB
+    width = 2 * REACH + 1
+    w_base = degree * block_total
+    lane = lax.broadcasted_iota(jnp.int32, (SUB, LANES), 1)
+    bit_masks = [((lane >> t) & 1) == 1 for t in range(LANES.bit_length() - 1)]
+    for half in range(groups):
+        best = [src[k * span + SUB + half * SUB : k * span + SUB + (half + 1) * SUB, :] for k in range(mine)]
+        for j, (low, high) in enumerate(TURNS):
+            for q in range(width):
+                at = ((j * width + q) * groups + half) * SUB
+                idx = idx_ref[at : at + SUB, :]
+                w = w_ref[w_base + at : w_base + at + SUB, :]
+                for k in range(mine):
+                    base = k * span + SUB + half * SUB - REACH
+
+                    def block(turned):
+                        o = base + (q - turned) % width
+                        return src[o : o + SUB, :]
+
+                    if low is None:
+                        shown = block(0)
+                    else:
+                        shown = jnp.where(
+                            bit_masks[high],
+                            jnp.where(bit_masks[low], block(3), block(2)),
+                            jnp.where(bit_masks[low], block(1), block(0)),
+                        )
+                    value = jnp.take_along_axis(shown, idx, axis=1, mode="promise_in_bounds")
+                    best[k] = jnp.minimum(best[k], value + w)
+        for k in range(mine):
+            halo_store(dst, k, half, groups, span, best[k])
+
+    @pl.loop(first_over, degree)
+    def _(s):
+        for half in range(groups):
+            at = pl.multiple_of(s * block_total + half * SUB, SUB)
+            idx = left_idx_ref[pl.ds(at, SUB), :]
+            off = left_off_ref[pl.ds(at, SUB), :]
+            w = left_w_ref[pl.ds(at, SUB), :]
+            for k in range(mine):
+                base = k * span + SUB + half * SUB
+                picked = None
+                for o in range(width):
+                    start = base + o - REACH
+                    value = jnp.take_along_axis(
+                        src[start : start + SUB, :], idx, axis=1, mode="promise_in_bounds"
+                    )
+                    picked = value if picked is None else jnp.where(off == o, value, picked)
+                now = dst[base : base + SUB, :]
+                halo_store(dst, k, half, groups, span, jnp.minimum(now, picked + w))
+
+
+def sweep_pairs(count, mine, degree, first_over, one, two, tables):
+    @pl.loop(0, count // 2)
+    def _(_):
+        sweep_once(mine, degree, first_over, one, two, tables)
+        sweep_once(mine, degree, first_over, two, one, tables)
+
+
+def begin_kernel(
+    mine, degree, count, source_ref, first_ref, buf_ref,
+    x_ref, idx_ref, w_ref, left_idx_ref, left_off_ref, left_w_ref, over_ref,
+    stage, stage_tail, other,
+):
     peers = buf_ref.shape[0]
     span = x_ref.shape[0] // mine
     block_total = span - 2 * SUB
@@ -109,88 +245,57 @@
     shard_blocks = block_total // peers
     arc_rows = degree * shard_blocks
     base = mine * shard_blocks
-    total = None
-    for i in range(peers):
-        part = buf_ref[i, base + 2 * arc_rows : base + 3 * arc_rows, :]
-        total = part if total is None else total + part
-    flow_ref[...] = total
     for i in range(peers):
         for b in range(shard_blocks):
             blk = i * shard_blocks + b
             stage[pl.ds(blk, mine, stride=block_total), :] = buf_ref[i, b * mine : (b + 1) * mine, :]
             s0 = base + b * degree
-            stage_idx[pl.ds(blk, degree, stride=block_total), :] = buf_ref[i, s0 : s0 + degree, :]
+            stage_tail[pl.ds(blk, degree, stride=block_total), :] = buf_ref[i, s0 : s0 + degree, :]
             s1 = base + arc_rows + b * degree
             w_ref[pl.ds(blk, degree, stride=block_total), :] = buf_ref[i, s1 : s1 + degree, :]
     rows = lax.broadcasted_iota(jnp.int32, (SUB, LANES), 0)
     lanes = lax.broadcasted_iota(jnp.int32, (SUB, LANES), 1)
     first = first_ref[0]
+    over = None
     for half in range(groups):
         node = (rows + half * SUB) * LANES + lanes
         for k in range(mine):
             at = k * block_total + half * SUB
             value = jnp.where(node == source_ref[first + k], jnp.float32(0.0), stage[at : at + SUB, :])
             halo_store(x_ref, k, half, groups, span, value)
-        for s in range(degree):
-            at = s * block_total + half * SUB
-            tail = stage_idx[at : at + SUB, :].astype(jnp.int32)
-            tail_block = tail // LANES
-            idx_ref[at : at + SUB, :] = tail - tail_block * LANES
-            off = tail_block - (rows + half * SUB) + REACH
-            off = jnp.where(off < 0, off + block_total, off)
-            off_ref[at : at + SUB, :] = jnp.where(off >= block_total, off - block_total, off)
-
-
-def sweep_once(mine, degree, src, dst, idx_ref, off_ref, w_ref):
-    span = src.shape[0] // mine
-    block_total = span - 2 * SUB
-    groups = block_total // SUB
-    for half in range(groups):
-        best = [src[k * span + SUB + half * SUB : k * span + SUB + (half + 1) * SUB, :] for k in range(mine)]
-        for s in range(degree):
-            at = s * block_total + half * SUB
-            idx = idx_ref[at : at + SUB, :]
-            off = off_ref[at : at + SUB, :]
-            w = w_ref[at : at + SUB, :]
-            masks = [off == o for o in range(2 * REACH)]
-            for k in range(mine):
-                base = k * span + SUB + half * SUB - REACH
-                picked = None
-                for o in reversed(range(2 * REACH + 1)):
-                    value = jnp.take_along_axis(
-                        src[base + o : base + o + SUB, :], idx, axis=1, mode="promise_in_bounds"
-                    )
-                    picked = value if picked is None else jnp.where(masks[o], value, picked)
-                best[k] = jnp.minimum(best[k], picked + w)
-        for k in range(mine):
-            halo_store(dst, k, half, groups, span, best[k])
-
-
-def sweep_kernel(mine, degree, count, x_ref, idx_ref, off_ref, w_ref, out_ref, other):
-    span = x_ref.shape[0] // mine
-    args = (idx_ref, off_ref, w_ref)
-    pairs, odd = divmod(count, 2)
-    if odd:
-        sweep_once(mine, degree, x_ref, out_ref, *args)
-    else:
-        out_ref[...] = x_ref[...]
-    if pairs:
-        @pl.loop(0, pairs)
-        def _(_):
-            sweep_once(mine, degree, out_ref, other, *args)
-            sweep_once(mine, degree, other, out_ref, *args)
-
-
-def out_kernel(mine, x_ref, flow_ref, cap_ref, out_ref, grad_ref):
+        part = plan_rounds(
+            degree, block_total, half, stage_tail, idx_ref, w_ref,
+            left_idx_ref, left_off_ref, left_w_ref,
+        )
+        over = part if over is None else jnp.minimum(over, part)
+    first_over = jnp.min(over.astype(jnp.float32)).astype(jnp.int32)
+    over_ref[0] = first_over
+    tables = (idx_ref, w_ref, left_idx_ref, left_off_ref, left_w_ref)
+    sweep_pairs(count, mine, degree, first_over, x_ref, other, tables)
+
+
+def end_kernel(
+    mine, degree, count, parts, over_ref, start_ref, idx_ref, w_ref, left_idx_ref, left_off_ref,
+    left_w_ref, cap_ref, *refs,
+):
+    flow_refs, (out_ref, grad_ref, x_ref, other) = refs[:parts], refs[parts:]
     peers = out_ref.shape[0]
     span = x_ref.shape[0] // mine
     block_total = span - 2 * SUB
     shard_blocks = block_total // peers
-    degree = cap_ref.shape[0]
+    tables = (idx_ref, w_ref, left_idx_ref, left_off_ref, left_w_ref)
+    first_over = over_ref[0]
+    sweep_once(mine, degree, first_over, start_ref, other, tables)
+    sweep_once(mine, degree, first_over, other, x_ref, tables)
+    sweep_pairs(count - 2, mine, degree, first_over, x_ref, other, tables)
     square = None
     for b in range(shard_blocks):
         cols = slice(b * LANES, (b + 1) * LANES)
-        grad = flow_ref[b * degree : (b + 1) * degree, :] - cap_ref[:, cols]
+        flow = None
+        for ref in flow_refs:
+            part = ref[b * degree : (b + 1) * degree, :]
+            flow = part if flow is None else flow + part
+        grad = flow - cap_ref[:, cols]
         grad_ref[:, cols] = grad
         term = grad * grad
         square = term if square is None else square + term
@@ -222,11 +327,6 @@
     )
 
 
-def comm_sum_parts(sweeps, size):
-    steps = max(size.bit_length() - 1, 1)
-    return [sweeps // steps + (1 if n < sweeps % steps else 0) for n in range(steps)]
-
-
 def shards(prev_dist, source_node, arc_tail, base_cost, arc_price, capacity, path_arcs, demand):
     commodities, shard_nodes = prev_dist.shape
     peers = lax.axis_size("arc")
@@ -240,69 +340,81 @@
     arc_rows = degree * shard_blocks
     f32, i32 = jnp.float32, jnp.int32
     shape = jax.ShapeDtypeStruct
+    near = pltpu.VMEM
     v, s = vmem_spec, smem_spec
+
+    def held(x):
+        return pltpu.with_memory_space_constraint(x, pltpu.VMEM)
 
     packed = pl.pallas_call(
         functools.partial(pack_kernel, node_count),
-        out_shape=shape((peers, mine * shard_blocks + 3 * arc_rows, LANES), f32),
+        out_shape=near((peers, mine * shard_blocks + 3 * arc_rows, LANES), f32),
         in_specs=[s(), v(), v(), v(), v(), v()],
         out_specs=v(),
+        compiler_params=pltpu.CompilerParams(vmem_limit_bytes=VMEM_GRANT),
         name="pack",
     )(demand, prev_dist, arc_tail, base_cost, arc_price, path_arcs)
-    received = lax.all_to_all(packed, "arc", 0, 0, tiled=True)
+    received = held(lax.all_to_all(packed, "arc", 0, 0, tiled=True))
+
+    flow = pl.pallas_call(
+        functools.partial(flow_kernel, arc_rows),
+        out_shape=near((arc_rows, LANES), f32),
+        in_specs=[v()],
+        out_specs=v(),
+        compiler_params=pltpu.CompilerParams(vmem_limit_bytes=VMEM_GRANT),
+        name="flow",
+    )(received)
+    flows = [flow]
+    for d in range(1, groups):
+        flows.append(lax.ppermute(flow, "comm", [(i, (i + d) % groups) for i in range(groups)]))
+
     first = (lax.axis_index("arc") * mine).astype(i32).reshape(1)
+    rounds = (2 * REACH + 1) * len(TURNS)
     table = degree * block_total
-    x, idx, off, w, flow = pl.pallas_call(
-        functools.partial(unpack_kernel, mine, degree),
+    state = (mine * span, LANES)
+    *tables, over = pl.pallas_call(
+        functools.partial(begin_kernel, mine, degree, EARLY_SWEEPS),
         out_shape=(
-            shape((mine * span, LANES), f32),
-            shape((table, LANES), i32),
-            shape((table, LANES), i32),
-            shape((table, LANES), f32),
-            shape((arc_rows, LANES), f32),
+            near(state, f32),
+            near((rounds * block_total, LANES), i32),
+            near((table + rounds * block_total, LANES), f32),
+            near((table, LANES), i32),
+            near((table, LANES), i32),
+            near((table, LANES), f32),
+            shape((1,), i32),
         ),
         in_specs=[s(), s(), v()],
-        out_specs=(v(), v(), v(), v(), v()),
+        out_specs=(v(), v(), v(), v(), v(), v(), s()),
         scratch_shapes=[
             pltpu.VMEM((mine * block_total, LANES), f32),
             pltpu.VMEM((table, LANES), f32),
+            pltpu.VMEM(state, f32),
         ],
-        name="unpack",
+        compiler_params=pltpu.CompilerParams(vmem_limit_bytes=VMEM_GRANT),
+        name="begin",
     )(source_node, first, received)
 
-    for step, count in enumerate(comm_sum_parts(SWEEPS, groups)):
-        distance = 1 << step
-        if distance < groups:
-            arrived = lax.ppermute(flow, "comm", [(i, i ^ distance) for i in range(groups)])
-        x = pl.pallas_call(
-            functools.partial(sweep_kernel, mine, degree, count),
-            out_shape=shape((mine * span, LANES), f32),
-            in_specs=[v(), v(), v(), v()],
-            out_specs=v(),
-            scratch_shapes=[pltpu.VMEM((mine * span, LANES), f32)],
-            name="sweeps",
-        )(x, idx, off, w)
-        if distance < groups:
-            flow = flow + arrived
-
     back, gradient = pl.pallas_call(
-        functools.partial(out_kernel, mine),
+        functools.partial(end_kernel, mine, degree, SWEEPS - EARLY_SWEEPS, groups),
         out_shape=(
-            shape((peers, mine * shard_blocks + SUB, LANES), f32),
-            shape((degree, shard_nodes), f32),
+            near((peers, mine * shard_blocks + SUB, LANES), f32),
+            near((degree, shard_nodes), f32),
         ),
-        in_specs=[v(), v(), v()],
+        in_specs=[s()] + [v()] * (len(tables) + 1 + groups),
         out_specs=(v(), v()),
-        name="give_back",
-    )(x, flow, capacity)
-    final = lax.all_to_all(back, "arc", 0, 0, tiled=True)
+        scratch_shapes=[pltpu.VMEM(state, f32), pltpu.VMEM(state, f32)],
+        compiler_params=pltpu.CompilerParams(vmem_limit_bytes=VMEM_GRANT),
+        name="end",
+    )(over, *map(held, tables), capacity, *map(held, flows))
+    final = held(lax.all_to_all(back, "arc", 0, 0, tiled=True))
     return pl.pallas_call(
         functools.partial(final_kernel, mine, degree * node_count),
         out_shape=(shape((commodities, shard_nodes), f32), shape((degree, shard_nodes), f32)),
         in_specs=[v(), v(), v()],
         out_specs=(v(), v()),
+        compiler_params=pltpu.CompilerParams(vmem_limit_bytes=VMEM_GRANT),
         name="finish",
-    )(final, gradient, arc_price)
+    )(final, held(gradient), arc_price)
 
 
 def solution(mesh):

time: 70.2 us -> 50.6 us (0.72)
  Pallas kernels: 35.7 us -> 15.7 us
  blocking collectives: 9.85 us -> 23 us
  waiting for transfers between devices: 12.1 us -> 0.01 us
  local copies, waits for them, and re-layouts: 0.79 us -> 5.06 us
  starting transfers between devices: 9.36 us -> 5.57 us
  other arithmetic: 1.33 us -> 0 us
    pallas_call x5 -> x4, Pallas kernels: 34 us -> 15 us  [the longest x1 8.95 us: shards(): pl.pallas_call(functools.partial(end_kernel, mine, degree, SWEEPS - EARLY...]
    all_to_all x1 -> x2, blocking collectives: 9.85 us -> 23 us  [the longest x1 14.7 us: shards(): received = held(lax.all_to_all(packed, 'arc', 0, 0, tiled=True))]
    all_to_all x1 -> x0, waiting for transfers between devices: 9.71 us -> none  [shards(): received = lax.all_to_all(packed, 'arc', 0, 0, tiled=True)]
    all_to_all x1 -> x0, starting transfers between devices: 5.2 us -> none  [shards(): received = lax.all_to_all(packed, 'arc', 0, 0, tiled=True)]
    unnamed x2 -> x18, local copies, waits for them, and re-layouts: 0.79 us -> 5.06 us
    ppermute x2 -> x3, waiting for transfers between devices: 2.37 us -> 0.01 us  [shards(): lax.ppermute(flow, 'comm', [(i, (i + d) % groups) for i in range(groups)])]
    ppermute x2 -> x3, starting transfers between devices: 4.17 us -> 5.57 us  [shards(): lax.ppermute(flow, 'comm', [(i, (i + d) % groups) for i in range(groups)])]
    add x2 -> x0, other arithmetic: 1.33 us -> none  [shards(): flow = flow + arrived]
  transfers between devices with their start and end apart: 3 -> 3, of which waited for: 2 -> 0; matrix products, arithmetic and copies ran while one was open for 0% -> 0% of each run, Pallas kernels for 39% -> 9%
where the time goes in v2:
time: 50.6 us; the launch traced here: 50 us
  blocking collectives  23 us (45%)
  Pallas kernels  15.7 us (31%)
  starting transfers between devices  5.57 us (11%)
  local copies, waits for them, and re-layouts  5.06 us (10%)
  between operations  0.71 us (1%)
    all_to_all x1, blocking collectives, shards(): received = held(lax.all_to_all(packed, 'arc', 0, 0, tiled=True))  14.7 us
    pallas_call x1, Pallas kernels, shards(): pl.pallas_call(functools.partial(end_kernel, mine, degree, SWEEPS - EARLY...  8.95 us
    all_to_all x1, blocking collectives, shards(): final = held(lax.all_to_all(back, 'arc', 0, 0, tiled=True))  8.25 us
    ppermute x3, starting transfers between devices, shards(): lax.ppermute(flow, 'comm', [(i, (i + d) % groups) for i in range(groups)])  5.57 us
    unnamed x18, local copies, waits for them, and re-layouts  5.06 us
    pallas_call x1, Pallas kernels, shards(): pl.pallas_call(functools.partial(begin_kernel, mine, degree, EARLY_SWEEPS...  4.47 us
    pallas_call x1, Pallas kernels, shards(): pl.pallas_call(functools.partial(pack_kernel, node_count), out_shape=near...  1.58 us
  transfers between devices with their start and end apart: 3, of which 0 were waited for; matrix products, arithmetic and copies ran while one was open for 0% of the time, Pallas kernels for 9%

profile of v2, /device:TPU:0, one launch (start us, length us, event | category | flops | bytes accessed | tf_op | source)
XLA Modules:
  0.0 50.0 jit_solution(7019277084336468179)
XLA Ops:
  0.6 0.0 copy-start
  0.6 0.9 %copy-done = f32[128,256]{1,0:T(8,128)S(1)} copy-done((f32[128,256]{1,0:T(8,128)S(1)}, f32[128,256]{1,0:T(8,128)}, u32[]{:S(2)}) %copy-start) | copy-done | bytes 131096
  1.5 0.0 copy-start.1
  1.5 0.7 %copy-done.1 = f32[16,256]{1,0:T(8,128)S(1)} copy-done((f32[16,256]{1,0:T(8,128)S(1)}, f32[16,256]{1,0:T(8,128)}, u32[]{:S(2)}) %copy-start.1) | copy-done | bytes 16408
  2.3 0.0 copy-start.4
  2.3 0.7 %copy-done.4 = s32[16,256]{1,0:T(8,128)S(1)} copy-done((s32[16,256]{1,0:T(8,128)S(1)}, s32[16,256]{1,0:T(8,128)}, u32[]{:S(2)}) %copy-start.4) | copy-done | bytes 16408
  3.0 0.0 copy-start.5
  3.0 0.7 %copy-done.5 = f32[16,256]{1,0:T(8,128)S(1)} copy-done((f32[16,256]{1,0:T(8,128)S(1)}, f32[16,256]{1,0:T(8,128)}, u32[]{:S(2)}) %copy-start.5) | copy-done | bytes 16408
  3.7 0.0 copy-start.6
  3.7 0.7 %copy-done.6 = s32[16,128]{1,0:T(8,128)S(1)} copy-done((s32[16,128]{1,0:T(8,128)S(1)}, s32[16,128]{1,0:T(8,128)}, u32[]{:S(2)}) %copy-start.6) | copy-done | bytes 8216
  4.4 0.0 copy-start.7
  4.4 0.7 %copy-done.7 = f32[16]{0:T(128)S(1)} copy-done((f32[16]{0:T(128)S(1)}, f32[16]{0:T(128)}, u32[]{:S(2)}) %copy-start.7) | copy-done | bytes 88
  5.0 1.6 %pack.1 = f32[8,128,128]{2,1,0:T(8,128)S(1)} custom-call(f32[16]{0:T(128)S(1)} %copy-done.7, f32[128,256]{1,0:T(8,128)S(1)} %copy-done, s32[16,256]{1,0:T(8,128)S(1)} %copy-done.4, f32[16,256]{1,0:T(8,128)S(1)} %copy-done.5, f32[16,256]{1,0:T(8,128)S(1)} %copy-done.1, s32[16,128]{1,0:T(8,128)S(1)} %copy-done.6), custom_call_target="tpu_custom_call" | custom-call | tf_op jit(solution)/shard_map/pack/pallas_call | solution.py:349
  6.6 14.7 %all_to_all.10.buf_ref = f32[8,128,128]{2,1,0:T(8,128)S(1)} all-to-all(f32[8,128,128]{2,1,0:T(8,128)S(1)} %pack.1), channel_id=1, replica_groups=mesh['comm'=4,'arc'=8] {'arc'}, dimensions={0} | all-to-all | bytes 1048576 | tf_op jit(solution)/shard_map/all_to_all | solution.py:357
  21.4 1.6 %collective-permute-start = (f32[32,128]{1,0:T(8,128)S(1)}, f32[32,128]{1,0:T(8,128)S(1)}, u32[]{:S(2)}, u32[]{:S(2)}) collective-permute-start(f32[32,128]{1,0:T(8,128)S(1)} %flow.1.refs_0_), channel_id=1, source_target_pairs={{0,8},{8,16},{16,24},{24,0},{1,9},{9,17},{17,25},{25,1},{2,10},{10... | collective-permute-start | bytes 49160 | tf_op jit(solution)/shard_map/ppermute | solution.py:369
  23.0 2.6 %collective-permute-start.1 = (f32[32,128]{1,0:T(8,128)S(1)}, f32[32,128]{1,0:T(8,128)S(1)}, u32[]{:S(2)}, u32[]{:S(2)}) collective-permute-start(f32[32,128]{1,0:T(8,128)S(1)} %flow.1.refs_0_), channel_id=1, source_target_pairs={{0,16},{8,24},{16,0},{24,8},{1,17},{9,25},{17,1},{25,9},{2,18},{10... | collective-permute-start | bytes 49160 | tf_op jit(solution)/shard_map/ppermute | solution.py:369
  25.6 1.3 %collective-permute-start.2 = (f32[32,128]{1,0:T(8,128)S(1)}, f32[32,128]{1,0:T(8,128)S(1)}, u32[]{:S(2)}, u32[]{:S(2)}) collective-permute-start(f32[32,128]{1,0:T(8,128)S(1)} %flow.1.refs_0_), channel_id=1, source_target_pairs={{0,24},{8,0},{16,8},{24,16},{1,25},{9,1},{17,9},{25,17},{2,26},{10... | collective-permute-start | bytes 49160 | tf_op jit(solution)/shard_map/ppermute | solution.py:369
  26.9 0.0 copy-start.8
  26.9 0.7 %copy-done.8 = s32[128]{0:T(128)S(1)} copy-done((s32[128]{0:T(128)S(1)}, s32[128]{0:T(128)}, u32[]{:S(2)}) %copy-start.8) | copy-done | bytes 536
  27.6 0.0 copy-start.3
  27.6 4.5 %begin.1 = (f32[512,128]{1,0:T(8,128)S(1)}, s32[480,128]{1,0:T(8,128)S(1)}, f32[736,128]{1,0:T(8,128)S(1)}, s32[256,128]{1,0:T(8,128)S(1)}, s32[256,128]{1,0:T(8...) custom-call(s32[128]{0:T(128)S(1)} %copy-done.8, s32[1]{0:T(128)} %bitcast.first_ref, f32[8,128,128]{2,1,0:T(8,128)S(1)} %all_to_all.10.buf_ref), custom_call_target="tpu_custom_call" | custom-call | tf_op jit(solution)/shard_map/begin/pallas_call | solution.py:375
  32.1 0.0 collective-permute-done.refs_1_
  32.1 0.0 collective-permute-done.1.refs_2_
  32.1 0.0 collective-permute-done.2.refs_3_
  32.1 0.0 copy-done.3
  32.1 9.0 %end.1 = (f32[8,40,128]{2,1,0:T(8,128)S(1)}, f32[16,256]{1,0:T(8,128)S(1)}) custom-call(s32[1]{0:T(128)} %get-tuple-element.11.over_ref, f32[512,128]{1,0:T(8,128)S(1)} %get-tuple-element.12.start_ref, s32[480,128]{1,0:T(8,128)S(1)} %get-tuple-element.13.idx_ref, f32[736,128]{1,0:T(8,128)S(1)} %get-tuple-element.14.w_ref, ...), custom_call_target="tpu_custom_call" | custom-call | tf_op jit(solution)/shard_map/end/pallas_call | solution.py:397
  41.1 0.0 copy-start.2
  41.1 8.2 %all_to_all.11.buf_ref = f32[8,40,128]{2,1,0:T(8,128)S(1)} all-to-all(f32[8,40,128]{2,1,0:T(8,128)S(1)} %get-tuple-element.18), channel_id=1, replica_groups=mesh['comm'=4,'arc'=8] {'arc'}, dimensions={0} | all-to-all | bytes 327680 | tf_op jit(solution)/shard_map/all_to_all | solution.py:409
  49.3 0.0 copy-done.2
  49.3 0.7 %finish.1 = (f32[128,256]{1,0:T(8,128)}, f32[16,256]{1,0:T(8,128)}) custom-call(f32[8,40,128]{2,1,0:T(8,128)S(1)} %all_to_all.11.buf_ref, f32[16,256]{1,0:T(8,128)S(1)} %get-tuple-element.19.grad_ref, f32[16,256]{1,0:T(8,128)S(1)} %copy-done.2), custom_call_target="tpu_custom_call" | custom-call | tf_op jit(solution)/shard_map/finish/pallas_call | solution.py:410
  (1 shorter events, 0.0 us)
Async XLA Ops:
  0.6 0.9 %copy-start = (f32[128,256]{1,0:T(8,128)S(1)}, f32[128,256]{1,0:T(8,128)}, u32[]{:S(2)}) copy-start(f32[128,256]{1,0:T(8,128)} %dist_ref.1) | copy-start | bytes 393220
  1.5 0.7 %copy-start.1 = (f32[16,256]{1,0:T(8,128)S(1)}, f32[16,256]{1,0:T(8,128)}, u32[]{:S(2)}) copy-start(f32[16,256]{1,0:T(8,128)} %price_ref.3) | copy-start | bytes 49156
  2.3 0.7 %copy-start.4 = (s32[16,256]{1,0:T(8,128)S(1)}, s32[16,256]{1,0:T(8,128)}, u32[]{:S(2)}) copy-start(s32[16,256]{1,0:T(8,128)} %tail_ref.1) | copy-start | bytes 49156
  3.0 0.7 %copy-start.5 = (f32[16,256]{1,0:T(8,128)S(1)}, f32[16,256]{1,0:T(8,128)}, u32[]{:S(2)}) copy-start(f32[16,256]{1,0:T(8,128)} %cost_ref.1) | copy-start | bytes 49156
  3.7 0.7 %copy-start.6 = (s32[16,128]{1,0:T(8,128)S(1)}, s32[16,128]{1,0:T(8,128)}, u32[]{:S(2)}) copy-start(s32[16,128]{1,0:T(8,128)} %path_ref.1) | copy-start | bytes 24580
  4.4 0.7 %copy-start.7 = (f32[16]{0:T(128)S(1)}, f32[16]{0:T(128)}, u32[]{:S(2)}) copy-start(f32[16]{0:T(128)} %demand_ref.1) | copy-start | bytes 196
  21.4 10.7 %collective-permute-start = (f32[32,128]{1,0:T(8,128)S(1)}, f32[32,128]{1,0:T(8,128)S(1)}, u32[]{:S(2)}, u32[]{:S(2)}) collective-permute-start(f32[32,128]{1,0:T(8,128)S(1)} %flow.1.refs_0_), channel_id=1, source_target_pairs={{0,8},{8,16},{16,24},{24,0},{1,9},{9,17},{17,25},{25,1},{2,10},{10... | collective-permute-start | bytes 49160 | tf_op jit(solution)/shard_map/ppermute | solution.py:369
  23.0 9.1 %collective-permute-start.1 = (f32[32,128]{1,0:T(8,128)S(1)}, f32[32,128]{1,0:T(8,128)S(1)}, u32[]{:S(2)}, u32[]{:S(2)}) collective-permute-start(f32[32,128]{1,0:T(8,128)S(1)} %flow.1.refs_0_), channel_id=1, source_target_pairs={{0,16},{8,24},{16,0},{24,8},{1,17},{9,25},{17,1},{25,9},{2,18},{10... | collective-permute-start | bytes 49160 | tf_op jit(solution)/shard_map/ppermute | solution.py:369
  25.6 6.5 %collective-permute-start.2 = (f32[32,128]{1,0:T(8,128)S(1)}, f32[32,128]{1,0:T(8,128)S(1)}, u32[]{:S(2)}, u32[]{:S(2)}) collective-permute-start(f32[32,128]{1,0:T(8,128)S(1)} %flow.1.refs_0_), channel_id=1, source_target_pairs={{0,24},{8,0},{16,8},{24,16},{1,25},{9,1},{17,9},{25,17},{2,26},{10... | collective-permute-start | bytes 49160 | tf_op jit(solution)/shard_map/ppermute | solution.py:369
  26.9 0.7 %copy-start.8 = (s32[128]{0:T(128)S(1)}, s32[128]{0:T(128)}, u32[]{:S(2)}) copy-start(s32[128]{0:T(128)} %source_ref.1) | copy-start | bytes 1540
  27.6 4.5 %copy-start.3 = (f32[16,256]{1,0:T(8,128)S(1)}, f32[16,256]{1,0:T(8,128)}, u32[]{:S(2)}) copy-start(f32[16,256]{1,0:T(8,128)} %cap_ref.1) | copy-start | bytes 49156
  41.1 8.3 %copy-start.2 = (f32[16,256]{1,0:T(8,128)S(1)}, f32[16,256]{1,0:T(8,128)}, u32[]{:S(2)}) copy-start(f32[16,256]{1,0:T(8,128)} %price_ref.3) | copy-start | bytes 49156

commit v3 on v2

--- a/solution.py
+++ b/solution.py
@@ -8,13 +8,12 @@
 from jax.sharding import PartitionSpec as P
 
 SWEEPS = 8
-EARLY_SWEEPS = 2
 REACH = 2
 LANES = 128
 SUB = 8
 VMEM_GRANT = 24 * 1024 * 1024
 
-TURNS = ((None, None), (0, 1), (2, 3), (4, 5), (6, 0), (1, 3))
+TURNS = ((None, None), (0, 1), (2, 3), (4, 5), (6, 0))
 
 step_size = 0.25
 eps_value = 1e-06
@@ -36,9 +35,28 @@
     return first, second, third
 
 
+def fetch(pairs, sems):
+    copies = [pltpu.make_async_copy(src, dst, sems.at[n]) for n, (src, dst) in enumerate(pairs)]
+    for copy in copies:
+        copy.start()
+    return copies
+
+
 def pack_kernel(
-    node_count, demand_ref, dist_ref, tail_ref, cost_ref, price_ref, path_ref, out_ref
+    node_count, path_hbm, demand_hbm, tail_hbm, cost_hbm, price_hbm, dist_hbm, out_ref,
+    path_ref, demand_ref, tail_ref, cost_ref, price_ref, dist_ref, sems,
 ):
+    copies = fetch(
+        (
+            (path_hbm, path_ref),
+            (demand_hbm, demand_ref),
+            (tail_hbm, tail_ref),
+            (cost_hbm, cost_ref),
+            (price_hbm, price_ref),
+            (dist_hbm, dist_ref),
+        ),
+        sems,
+    )
     peers = out_ref.shape[0]
     degree, shard_nodes = tail_ref.shape
     shard_blocks = shard_nodes // LANES
@@ -46,6 +64,8 @@
     block_total = node_count // LANES
     routes, hops = path_ref.shape
 
+    copies[0].wait()
+    copies[1].wait()
     path = path_ref[...]
     slot = path // node_count
     node = path - slot * node_count
@@ -80,6 +100,8 @@
         )
         flow = term if flow is None else flow + term
 
+    for copy in copies[2:]:
+        copy.wait()
     tail = tail_ref[...].astype(jnp.float32)
     weight = cost_ref[...] + price_ref[...]
     arc_rows = degree * shard_blocks
@@ -119,7 +141,7 @@
     rows = lax.broadcasted_iota(jnp.int32, (SUB, LANES), 0) + half * SUB
     used = jnp.zeros((SUB, LANES), jnp.int32)
     over = jnp.full((SUB, LANES), degree, jnp.int32)
-    lanes_of, weights, bits = [], [], []
+    lanes_of, weights, bits, opens, offs = [], [], [], [], []
     for s in range(degree):
         at = s * block_total + half * SUB
         tail = stage[at : at + SUB, :].astype(jnp.int32)
@@ -146,17 +168,35 @@
                     jnp.where(by_low, turned[1], turned[0]),
                 )
             open_rounds = open_rounds | (spot << (width * j))
-        open_rounds = open_rounds & ~used
-        bit = open_rounds & -open_rounds
+        free = open_rounds & ~used
+        bit = free & -free
+        if s >= len(TURNS):
+            movable = jnp.zeros_like(used)
+            targets = []
+            for earlier, taken in zip(opens, bits):
+                target = earlier & ~used
+                targets.append(target)
+                movable = movable | jnp.where(target != 0, taken, 0)
+            wanted = open_rounds & movable
+            wanted = jnp.where(bit == 0, wanted & -wanted, 0)
+            for e, (target, taken) in enumerate(zip(targets, bits)):
+                moved = (taken & wanted) != 0
+                target = jnp.where(moved, target & -target, 0)
+                used = used | target
+                bits[e] = jnp.where(moved, target, taken)
+            bit = bit | wanted
         used = used | bit
-        lost = bit == 0
-        over = jnp.minimum(over, jnp.where(lost, s, degree))
-        left_idx_ref[at : at + SUB, :] = lane
-        left_off_ref[at : at + SUB, :] = off
-        left_w_ref[at : at + SUB, :] = jnp.where(lost, weight, jnp.float32(jnp.inf))
+        over = jnp.minimum(over, jnp.where(bit == 0, s, degree))
+        opens.append(open_rounds)
+        offs.append(off)
         lanes_of.append(lane)
         weights.append(weight)
         bits.append(bit)
+    for s in range(degree):
+        at = s * block_total + half * SUB
+        left_idx_ref[at : at + SUB, :] = lanes_of[s]
+        left_off_ref[at : at + SUB, :] = offs[s]
+        left_w_ref[at : at + SUB, :] = jnp.where(bits[s] == 0, weights[s], jnp.float32(jnp.inf))
     for r in range(width * len(TURNS)):
         idx = jnp.zeros((SUB, LANES), jnp.int32)
         weight = jnp.full((SUB, LANES), jnp.inf, jnp.float32)
@@ -234,10 +274,11 @@
 
 
 def begin_kernel(
-    mine, degree, count, source_ref, first_ref, buf_ref,
+    mine, degree, source_hbm, buf_ref,
     x_ref, idx_ref, w_ref, left_idx_ref, left_off_ref, left_w_ref, over_ref,
-    stage, stage_tail, other,
+    stage, stage_tail, source_ref, sems,
 ):
+    (copy,) = fetch(((source_hbm, source_ref),), sems)
     peers = buf_ref.shape[0]
     span = x_ref.shape[0] // mine
     block_total = span - 2 * SUB
@@ -253,25 +294,37 @@
             stage_tail[pl.ds(blk, degree, stride=block_total), :] = buf_ref[i, s0 : s0 + degree, :]
             s1 = base + arc_rows + b * degree
             w_ref[pl.ds(blk, degree, stride=block_total), :] = buf_ref[i, s1 : s1 + degree, :]
+    over = None
+    for half in range(groups):
+        part = plan_rounds(
+            degree, block_total, half, stage_tail, idx_ref, w_ref,
+            left_idx_ref, left_off_ref, left_w_ref,
+        )
+        over = part if over is None else jnp.minimum(over, part)
+    over_ref[0] = jnp.min(over.astype(jnp.float32)).astype(jnp.int32)
+    copy.wait()
     rows = lax.broadcasted_iota(jnp.int32, (SUB, LANES), 0)
     lanes = lax.broadcasted_iota(jnp.int32, (SUB, LANES), 1)
-    first = first_ref[0]
-    over = None
+    first = lax.axis_index("arc") * mine
     for half in range(groups):
         node = (rows + half * SUB) * LANES + lanes
         for k in range(mine):
             at = k * block_total + half * SUB
             value = jnp.where(node == source_ref[first + k], jnp.float32(0.0), stage[at : at + SUB, :])
             halo_store(x_ref, k, half, groups, span, value)
-        part = plan_rounds(
-            degree, block_total, half, stage_tail, idx_ref, w_ref,
-            left_idx_ref, left_off_ref, left_w_ref,
-        )
-        over = part if over is None else jnp.minimum(over, part)
-    first_over = jnp.min(over.astype(jnp.float32)).astype(jnp.int32)
-    over_ref[0] = first_over
+
+
+def add_kernel(a_ref, b_ref, out_ref):
+    out_ref[...] = a_ref[...] + b_ref[...]
+
+
+def middle_kernel(
+    mine, degree, count, over_ref, start_ref, idx_ref, w_ref, left_idx_ref, left_off_ref,
+    left_w_ref, x_ref, other,
+):
+    x_ref[...] = start_ref[...]
     tables = (idx_ref, w_ref, left_idx_ref, left_off_ref, left_w_ref)
-    sweep_pairs(count, mine, degree, first_over, x_ref, other, tables)
+    sweep_pairs(count, mine, degree, over_ref[0], x_ref, other, tables)
 
 
 def end_kernel(
@@ -285,9 +338,8 @@
     shard_blocks = block_total // peers
     tables = (idx_ref, w_ref, left_idx_ref, left_off_ref, left_w_ref)
     first_over = over_ref[0]
-    sweep_once(mine, degree, first_over, start_ref, other, tables)
-    sweep_once(mine, degree, first_over, other, x_ref, tables)
-    sweep_pairs(count - 2, mine, degree, first_over, x_ref, other, tables)
+    x_ref[...] = start_ref[...]
+    sweep_pairs(count, mine, degree, first_over, x_ref, other, tables)
     square = None
     for b in range(shard_blocks):
         cols = slice(b * LANES, (b + 1) * LANES)
@@ -346,14 +398,29 @@
     def held(x):
         return pltpu.with_memory_space_constraint(x, pltpu.VMEM)
 
+    def far(x):
+        return pltpu.with_memory_space_constraint(x, pltpu.HBM)
+
+    def scratch(*arrays):
+        return [pltpu.VMEM(x.shape, x.dtype) for x in arrays]
+
+    h = functools.partial(pl.BlockSpec, memory_space=pltpu.HBM)
+    params = pltpu.CompilerParams(vmem_limit_bytes=VMEM_GRANT)
+    arcs = (arc_tail, base_cost, arc_price, prev_dist)
     packed = pl.pallas_call(
         functools.partial(pack_kernel, node_count),
         out_shape=near((peers, mine * shard_blocks + 3 * arc_rows, LANES), f32),
-        in_specs=[s(), v(), v(), v(), v(), v()],
+        in_specs=[h()] * 6,
         out_specs=v(),
-        compiler_params=pltpu.CompilerParams(vmem_limit_bytes=VMEM_GRANT),
+        scratch_shapes=[
+            *scratch(path_arcs),
+            pltpu.SMEM(demand.shape, f32),
+            *scratch(*arcs),
+            pltpu.SemaphoreType.DMA((6,)),
+        ],
+        compiler_params=params,
         name="pack",
-    )(demand, prev_dist, arc_tail, base_cost, arc_price, path_arcs)
+    )(far(path_arcs), far(demand), *map(far, arcs))
     received = held(lax.all_to_all(packed, "arc", 0, 0, tiled=True))
 
     flow = pl.pallas_call(
@@ -361,19 +428,24 @@
         out_shape=near((arc_rows, LANES), f32),
         in_specs=[v()],
         out_specs=v(),
-        compiler_params=pltpu.CompilerParams(vmem_limit_bytes=VMEM_GRANT),
+        compiler_params=params,
         name="flow",
     )(received)
-    flows = [flow]
-    for d in range(1, groups):
-        flows.append(lax.ppermute(flow, "comm", [(i, (i + d) % groups) for i in range(groups)]))
-
-    first = (lax.axis_index("arc") * mine).astype(i32).reshape(1)
+
+    def exchange(step):
+        pairs = [(i, i ^ (1 << step)) for i in range(groups)]
+        return held(lax.ppermute(flow, "comm", pairs))
+
+    steps = groups.bit_length() - 1
+    if 1 << steps != groups:
+        flow, steps = held(lax.psum(flow, "comm")), 0
+    arrived = exchange(0) if steps else None
+
     rounds = (2 * REACH + 1) * len(TURNS)
     table = degree * block_total
     state = (mine * span, LANES)
-    *tables, over = pl.pallas_call(
-        functools.partial(begin_kernel, mine, degree, EARLY_SWEEPS),
+    x, *tables, over = pl.pallas_call(
+        functools.partial(begin_kernel, mine, degree),
         out_shape=(
             near(state, f32),
             near((rounds * block_total, LANES), i32),
@@ -383,36 +455,62 @@
             near((table, LANES), f32),
             shape((1,), i32),
         ),
-        in_specs=[s(), s(), v()],
+        in_specs=[h(), v()],
         out_specs=(v(), v(), v(), v(), v(), v(), s()),
         scratch_shapes=[
             pltpu.VMEM((mine * block_total, LANES), f32),
             pltpu.VMEM((table, LANES), f32),
-            pltpu.VMEM(state, f32),
+            pltpu.SMEM(source_node.shape, i32),
+            pltpu.SemaphoreType.DMA((1,)),
         ],
-        compiler_params=pltpu.CompilerParams(vmem_limit_bytes=VMEM_GRANT),
+        compiler_params=params,
         name="begin",
-    )(source_node, first, received)
-
+    )(far(source_node), received)
+
+    tables = tuple(map(held, tables))
+    left = SWEEPS
+    for step in range(1, steps):
+        flow = pl.pallas_call(
+            add_kernel,
+            out_shape=near((arc_rows, LANES), f32),
+            in_specs=[v(), v()],
+            out_specs=v(),
+            compiler_params=params,
+            name="add",
+        )(held(flow), arrived)
+        arrived = exchange(step)
+        count = min(2 if steps > 2 else 4, left - 2)
+        left -= count
+        x = pl.pallas_call(
+            functools.partial(middle_kernel, mine, degree, count),
+            out_shape=near(state, f32),
+            in_specs=[s()] + [v()] * (len(tables) + 1),
+            out_specs=v(),
+            scratch_shapes=[pltpu.VMEM(state, f32)],
+            compiler_params=params,
+            name="middle",
+        )(over, held(x), *tables)
+
+    flows = (held(flow),) if arrived is None else (held(flow), arrived)
     back, gradient = pl.pallas_call(
-        functools.partial(end_kernel, mine, degree, SWEEPS - EARLY_SWEEPS, groups),
+        functools.partial(end_kernel, mine, degree, left, len(flows)),
         out_shape=(
             near((peers, mine * shard_blocks + SUB, LANES), f32),
             near((degree, shard_nodes), f32),
         ),
-        in_specs=[s()] + [v()] * (len(tables) + 1 + groups),
+        in_specs=[s()] + [v()] * (len(tables) + 2 + len(flows)),
         out_specs=(v(), v()),
         scratch_shapes=[pltpu.VMEM(state, f32), pltpu.VMEM(state, f32)],
-        compiler_params=pltpu.CompilerParams(vmem_limit_bytes=VMEM_GRANT),
+        compiler_params=params,
         name="end",
-    )(over, *map(held, tables), capacity, *map(held, flows))
+    )(over, held(x), *tables, capacity, *flows)
     final = held(lax.all_to_all(back, "arc", 0, 0, tiled=True))
     return pl.pallas_call(
         functools.partial(final_kernel, mine, degree * node_count),
         out_shape=(shape((commodities, shard_nodes), f32), shape((degree, shard_nodes), f32)),
         in_specs=[v(), v(), v()],
         out_specs=(v(), v()),
-        compiler_params=pltpu.CompilerParams(vmem_limit_bytes=VMEM_GRANT),
+        compiler_params=params,
         name="finish",
     )(final, held(gradient), arc_price)
 

time: 50.6 us -> 45.7 us (0.903)
  local copies, waits for them, and re-layouts: 5.06 us -> 0.01 us
  waiting for transfers between devices: 0.01 us -> 2.17 us
  starting transfers between devices: 5.57 us -> 4.22 us
    unnamed x18 -> x4, local copies, waits for them, and re-layouts: 5.06 us -> 0.01 us
    ppermute x3 -> x2, waiting for transfers between devices: 0.01 us -> 2.17 us  [exchange(): return held(lax.ppermute(flow, 'comm', pairs))]
    ppermute x3 -> x2, starting transfers between devices: 5.57 us -> 4.22 us  [exchange(): return held(lax.ppermute(flow, 'comm', pairs))]
    pallas_call x2 -> x4, Pallas kernels: 13.4 us -> 12.6 us  [the longest x1 5.26 us: shards(): pl.pallas_call(functools.partial(end_kernel, mine, degree, left, len(flow...]
  transfers between devices with their start and end apart: 3 -> 2, of which waited for: 0 -> 1; matrix products, arithmetic and copies ran while one was open for 0% -> 0% of each run, Pallas kernels for 9% -> 16%
where the time goes in v3:
time: 45.7 us; the launch traced here: 45.4 us
  blocking collectives  23 us (50%)
  Pallas kernels  15.3 us (33%)
  starting transfers between devices  4.22 us (9%)
  waiting for transfers between devices  2.17 us (5%)
  between operations  0.7 us (2%)
    all_to_all x1, blocking collectives, shards(): received = held(lax.all_to_all(packed, 'arc', 0, 0, tiled=True))  14.7 us
    all_to_all x1, blocking collectives, shards(): final = held(lax.all_to_all(back, 'arc', 0, 0, tiled=True))  8.25 us
    pallas_call x1, Pallas kernels, shards(): pl.pallas_call(functools.partial(end_kernel, mine, degree, left, len(flow...  5.26 us
    pallas_call x1, Pallas kernels, shards(): pl.pallas_call(functools.partial(middle_kernel, mine, degree, count), out...  5.19 us
    ppermute x2, starting transfers between devices, exchange(): return held(lax.ppermute(flow, 'comm', pairs))  4.22 us
    pallas_call x1, Pallas kernels, shards(): pl.pallas_call(functools.partial(begin_kernel, mine, degree), out_shape=(...  2.19 us
    ppermute x2, waiting for transfers between devices, exchange(): return held(lax.ppermute(flow, 'comm', pairs))  2.17 us
    pallas_call x1, Pallas kernels, shards(): pl.pallas_call(functools.partial(pack_kernel, node_count), out_shape=near...  1.94 us
  transfers between devices with their start and end apart: 2, of which 1 were waited for; matrix products, arithmetic and copies ran while one was open for 0% of the time, Pallas kernels for 16%

profile of v3, /device:TPU:0, one launch (start us, length us, event | category | flops | bytes accessed | tf_op | source)
XLA Modules:
  0.0 45.4 jit_solution(2911304506487943757)
XLA Ops:
  0.6 1.9 %pack.1 = f32[8,128,128]{2,1,0:T(8,128)S(1)} custom-call(s32[16,128]{1,0:T(8,128)} %path_hbm.1, f32[16]{0:T(128)} %demand_hbm.1, s32[16,256]{1,0:T(8,128)} %tail_hbm.1, f32[16,256]{1,0:T(8,128)} %cost_hbm.1, f32[16,256]{1,0:T(8,128)} %price_ref.1, f32[128,256]{1,0:T(8,128)} %dist_hbm.1), custom_call_target="tpu_custom_call" | custom-call | tf_op jit(solution)/shard_map/pack/pallas_call | solution.py:410
  2.6 14.7 %all_to_all.10.buf_ref = f32[8,128,128]{2,1,0:T(8,128)S(1)} all-to-all(f32[8,128,128]{2,1,0:T(8,128)S(1)} %pack.1), channel_id=1, replica_groups=mesh['comm'=4,'arc'=8] {'arc'}, dimensions={0} | all-to-all | bytes 1048576 | tf_op jit(solution)/shard_map/all_to_all | solution.py:424
  17.3 1.6 %collective-permute-start = (f32[32,128]{1,0:T(8,128)S(1)}, f32[32,128]{1,0:T(8,128)S(1)}, u32[]{:S(2)}, u32[]{:S(2)}) collective-permute-start(f32[32,128]{1,0:T(8,128)S(1)} %flow.1.a_ref), channel_id=1, source_target_pairs={{0,8},{8,0},{16,24},{24,16},{1,9},{9,1},{17,25},{25,17},{2,10},{10... | collective-permute-start | bytes 49160 | tf_op jit(solution)/shard_map/ppermute | solution.py:437
  18.9 2.2 %collective-permute-done.b_ref = f32[32,128]{1,0:T(8,128)S(1)} collective-permute-done((f32[32,128]{1,0:T(8,128)S(1)}, f32[32,128]{1,0:T(8,128)S(1)}, u32[]{:S(2)}, u32[]{:S(2)}) %collective-permute-start) | collective-permute-done | bytes 16416 | tf_op jit(solution)/shard_map/ppermute | solution.py:437
  21.1 2.6 %collective-permute-start.1 = (f32[32,128]{1,0:T(8,128)S(1)}, f32[32,128]{1,0:T(8,128)S(1)}, u32[]{:S(2)}, u32[]{:S(2)}) collective-permute-start(f32[32,128]{1,0:T(8,128)S(1)} %add.1.refs_0_), channel_id=1, source_target_pairs={{0,16},{8,24},{16,0},{24,8},{1,17},{9,25},{17,1},{25,9},{2,18},{10... | collective-permute-start | bytes 49160 | tf_op jit(solution)/shard_map/ppermute | solution.py:437
  23.7 2.2 %begin.1 = (f32[512,128]{1,0:T(8,128)S(1)}, s32[400,128]{1,0:T(8,128)S(1)}, f32[656,128]{1,0:T(8,128)S(1)}, s32[256,128]{1,0:T(8,128)S(1)}, s32[256,128]{1,0:T(8...) custom-call(s32[128]{0:T(128)} %source_hbm.1, f32[8,128,128]{2,1,0:T(8,128)S(1)} %all_to_all.10.buf_ref), custom_call_target="tpu_custom_call" | custom-call | tf_op jit(solution)/shard_map/begin/pallas_call | solution.py:447
  25.9 0.0 copy-start.1
  25.9 5.2 %middle.1.start_ref = f32[512,128]{1,0:T(8,128)S(1)} custom-call(s32[1]{0:T(128)} %get-tuple-element.11.over_ref, f32[512,128]{1,0:T(8,128)S(1)} %get-tuple-element.12.start_ref, s32[400,128]{1,0:T(8,128)S(1)} %get-tuple-element.13.idx_ref, f32[656,128]{1,0:T(8,128)S(1)} %get-tuple-element.14.w_ref, s32[256,128]{1,0:T(8,128)S(1)} %get-tuple-element.15.left_idx_ref, ...), custom_call_target="tpu_custom_call" | custom-call | tf_op jit(solution)/shard_map/middle/pallas_call | solution.py:484
  31.1 0.0 collective-permute-done.1.refs_1_
  31.1 0.0 copy-done.1
  31.1 5.3 %end.1 = (f32[8,40,128]{2,1,0:T(8,128)S(1)}, f32[16,256]{1,0:T(8,128)S(1)}) custom-call(s32[1]{0:T(128)} %get-tuple-element.11.over_ref, f32[512,128]{1,0:T(8,128)S(1)} %middle.1.start_ref, s32[400,128]{1,0:T(8,128)S(1)} %get-tuple-element.13.idx_ref, f32[656,128]{1,0:T(8,128)S(1)} %get-tuple-element.14.w_ref, ...), custom_call_target="tpu_custom_call" | custom-call | tf_op jit(solution)/shard_map/end/pallas_call | solution.py:495
  36.4 0.0 copy-start
  36.4 8.2 %all_to_all.11.buf_ref = f32[8,40,128]{2,1,0:T(8,128)S(1)} all-to-all(f32[8,40,128]{2,1,0:T(8,128)S(1)} %get-tuple-element.18), channel_id=1, replica_groups=mesh['comm'=4,'arc'=8] {'arc'}, dimensions={0} | all-to-all | bytes 327680 | tf_op jit(solution)/shard_map/all_to_all | solution.py:507
  44.6 0.0 copy-done
  44.6 0.7 %finish.1 = (f32[128,256]{1,0:T(8,128)}, f32[16,256]{1,0:T(8,128)}) custom-call(f32[8,40,128]{2,1,0:T(8,128)S(1)} %all_to_all.11.buf_ref, f32[16,256]{1,0:T(8,128)S(1)} %get-tuple-element.19.grad_ref, f32[16,256]{1,0:T(8,128)S(1)} %copy-done), custom_call_target="tpu_custom_call" | custom-call | tf_op jit(solution)/shard_map/finish/pallas_call | solution.py:508
  (2 shorter events, 0.0 us)
Async XLA Ops:
  17.3 3.8 %collective-permute-start = (f32[32,128]{1,0:T(8,128)S(1)}, f32[32,128]{1,0:T(8,128)S(1)}, u32[]{:S(2)}, u32[]{:S(2)}) collective-permute-start(f32[32,128]{1,0:T(8,128)S(1)} %flow.1.a_ref), channel_id=1, source_target_pairs={{0,8},{8,0},{16,24},{24,16},{1,9},{9,1},{17,25},{25,17},{2,10},{10... | collective-permute-start | bytes 49160 | tf_op jit(solution)/shard_map/ppermute | solution.py:437
  21.1 10.0 %collective-permute-start.1 = (f32[32,128]{1,0:T(8,128)S(1)}, f32[32,128]{1,0:T(8,128)S(1)}, u32[]{:S(2)}, u32[]{:S(2)}) collective-permute-start(f32[32,128]{1,0:T(8,128)S(1)} %add.1.refs_0_), channel_id=1, source_target_pairs={{0,16},{8,24},{16,0},{24,8},{1,17},{9,25},{17,1},{25,9},{2,18},{10... | collective-permute-start | bytes 49160 | tf_op jit(solution)/shard_map/ppermute | solution.py:437
  25.9 5.2 %copy-start.1 = (f32[16,256]{1,0:T(8,128)S(1)}, f32[16,256]{1,0:T(8,128)}, u32[]{:S(2)}) copy-start(f32[16,256]{1,0:T(8,128)} %cap_ref.1) | copy-start | bytes 49156
  36.4 8.3 %copy-start = (f32[16,256]{1,0:T(8,128)S(1)}, f32[16,256]{1,0:T(8,128)}, u32[]{:S(2)}) copy-start(f32[16,256]{1,0:T(8,128)} %price_ref.1) | copy-start | bytes 49156

commit v4 on v3

--- a/solution.py
+++ b/solution.py
@@ -314,7 +314,7 @@
             halo_store(x_ref, k, half, groups, span, value)
 
 
-def add_kernel(a_ref, b_ref, out_ref):
+def add_kernel(a_ref, b_ref, after_ref, out_ref):
     out_ref[...] = a_ref[...] + b_ref[...]
 
 
@@ -473,11 +473,11 @@
         flow = pl.pallas_call(
             add_kernel,
             out_shape=near((arc_rows, LANES), f32),
-            in_specs=[v(), v()],
+            in_specs=[v(), v(), v()],
             out_specs=v(),
             compiler_params=params,
             name="add",
-        )(held(flow), arrived)
+        )(held(flow), arrived, held(x))
         arrived = exchange(step)
         count = min(2 if steps > 2 else 4, left - 2)
         left -= count
@@ -488,7 +488,7 @@
             out_specs=v(),
             scratch_shapes=[pltpu.VMEM(state, f32)],
             compiler_params=params,
-            name="middle",
+                name="middle",
         )(over, held(x), *tables)
 
     flows = (held(flow),) if arrived is None else (held(flow), arrived)

time: 45.7 us -> 43.7 us (0.956)
  waiting for transfers between devices: 2.17 us -> 0.01 us
    ppermute x2, waiting for transfers between devices: 2.17 us -> 0.01 us  [exchange(): return held(lax.ppermute(flow, 'comm', pairs))]
  transfers between devices with their start and end apart: 2 -> 2, of which waited for: 1 -> 0; matrix products, arithmetic and copies ran while one was open for 0% -> 0% of each run, Pallas kernels for 16% -> 17%
where the time goes in v4:
time: 43.7 us; the launch traced here: 43.4 us
  blocking collectives  23 us (53%)
  Pallas kernels  15.4 us (35%)
  starting transfers between devices  4.29 us (10%)
  between operations  0.71 us (2%)
    all_to_all x1, blocking collectives, shards(): received = held(lax.all_to_all(packed, 'arc', 0, 0, tiled=True))  14.7 us
    all_to_all x1, blocking collectives, shards(): final = held(lax.all_to_all(back, 'arc', 0, 0, tiled=True))  8.25 us
    pallas_call x1, Pallas kernels, shards(): pl.pallas_call(functools.partial(end_kernel, mine, degree, left, len(flow...  5.3 us
    pallas_call x1, Pallas kernels, shards(): pl.pallas_call(functools.partial(middle_kernel, mine, degree, count), out...  5.22 us
    ppermute x2, starting transfers between devices, exchange(): return held(lax.ppermute(flow, 'comm', pairs))  4.29 us
    pallas_call x1, Pallas kernels, shards(): pl.pallas_call(functools.partial(begin_kernel, mine, degree), out_shape=(...  2.19 us
    pallas_call x1, Pallas kernels, shards(): pl.pallas_call(functools.partial(pack_kernel, node_count), out_shape=near...  1.94 us
  transfers between devices with their start and end apart: 2, of which 0 were waited for; matrix products, arithmetic and copies ran while one was open for 0% of the time, Pallas kernels for 17%

profile of v4, /device:TPU:0, one launch (start us, length us, event | category | flops | bytes accessed | tf_op | source)
XLA Modules:
  0.0 43.4 jit_solution(8483740228175531844)
XLA Ops:
  0.6 1.9 %pack.1 = f32[8,128,128]{2,1,0:T(8,128)S(1)} custom-call(s32[16,128]{1,0:T(8,128)} %path_hbm.1, f32[16]{0:T(128)} %demand_hbm.1, s32[16,256]{1,0:T(8,128)} %tail_hbm.1, f32[16,256]{1,0:T(8,128)} %cost_hbm.1, f32[16,256]{1,0:T(8,128)} %price_ref.1, f32[128,256]{1,0:T(8,128)} %dist_hbm.1), custom_call_target="tpu_custom_call" | custom-call | tf_op jit(solution)/shard_map/pack/pallas_call | solution.py:410
  2.6 14.7 %all_to_all.10.buf_ref = f32[8,128,128]{2,1,0:T(8,128)S(1)} all-to-all(f32[8,128,128]{2,1,0:T(8,128)S(1)} %pack.1), channel_id=1, replica_groups=mesh['comm'=4,'arc'=8] {'arc'}, dimensions={0} | all-to-all | bytes 1048576 | tf_op jit(solution)/shard_map/all_to_all | solution.py:424
  17.3 1.6 %collective-permute-start = (f32[32,128]{1,0:T(8,128)S(1)}, f32[32,128]{1,0:T(8,128)S(1)}, u32[]{:S(2)}, u32[]{:S(2)}) collective-permute-start(f32[32,128]{1,0:T(8,128)S(1)} %flow.1.a_ref), channel_id=1, source_target_pairs={{0,8},{8,0},{16,24},{24,16},{1,9},{9,1},{17,25},{25,17},{2,10},{10... | collective-permute-start | bytes 49160 | tf_op jit(solution)/shard_map/ppermute | solution.py:437
  18.9 2.2 %begin.1 = (f32[512,128]{1,0:T(8,128)S(1)}, s32[400,128]{1,0:T(8,128)S(1)}, f32[656,128]{1,0:T(8,128)S(1)}, s32[256,128]{1,0:T(8,128)S(1)}, s32[256,128]{1,0:T(8...) custom-call(s32[128]{0:T(128)} %source_hbm.1, f32[8,128,128]{2,1,0:T(8,128)S(1)} %all_to_all.10.buf_ref), custom_call_target="tpu_custom_call" | custom-call | tf_op jit(solution)/shard_map/begin/pallas_call | solution.py:447
  21.1 0.0 collective-permute-done.b_ref
  21.2 2.7 %collective-permute-start.1 = (f32[32,128]{1,0:T(8,128)S(1)}, f32[32,128]{1,0:T(8,128)S(1)}, u32[]{:S(2)}, u32[]{:S(2)}) collective-permute-start(f32[32,128]{1,0:T(8,128)S(1)} %add.1.refs_0_), channel_id=1, source_target_pairs={{0,16},{8,24},{16,0},{24,8},{1,17},{9,25},{17,1},{25,9},{2,18},{10... | collective-permute-start | bytes 49160 | tf_op jit(solution)/shard_map/ppermute | solution.py:437
  23.8 0.0 copy-start.1
  23.8 5.2 %middle.1.start_ref = f32[512,128]{1,0:T(8,128)S(1)} custom-call(s32[1]{0:T(128)} %get-tuple-element.11.over_ref, f32[512,128]{1,0:T(8,128)S(1)} %get-tuple-element.12.start_ref.after_ref, s32[400,128]{1,0:T(8,128)S(1)} %get-tuple-element.13.idx_ref, f32[656,128]{1,0:T(8,128)S(1)} %get-tuple-element.14.w_ref, s32[256,128]{1,0:T(8,128)S(1)} %get-tuple-element.15.left_idx_ref, ...), custom_call_target="tpu_custom_call" | custom-call | tf_op jit(solution)/shard_map/middle/pallas_call | solution.py:484
  29.1 0.0 collective-permute-done.1.refs_1_
  29.1 0.0 copy-done.1
  29.1 5.3 %end.1 = (f32[8,40,128]{2,1,0:T(8,128)S(1)}, f32[16,256]{1,0:T(8,128)S(1)}) custom-call(s32[1]{0:T(128)} %get-tuple-element.11.over_ref, f32[512,128]{1,0:T(8,128)S(1)} %middle.1.start_ref, s32[400,128]{1,0:T(8,128)S(1)} %get-tuple-element.13.idx_ref, f32[656,128]{1,0:T(8,128)S(1)} %get-tuple-element.14.w_ref, ...), custom_call_target="tpu_custom_call" | custom-call | tf_op jit(solution)/shard_map/end/pallas_call | solution.py:495
  34.4 0.0 copy-start
  34.4 8.2 %all_to_all.11.buf_ref = f32[8,40,128]{2,1,0:T(8,128)S(1)} all-to-all(f32[8,40,128]{2,1,0:T(8,128)S(1)} %get-tuple-element.18), channel_id=1, replica_groups=mesh['comm'=4,'arc'=8] {'arc'}, dimensions={0} | all-to-all | bytes 327680 | tf_op jit(solution)/shard_map/all_to_all | solution.py:507
  42.6 0.0 copy-done
  42.6 0.7 %finish.1 = (f32[128,256]{1,0:T(8,128)}, f32[16,256]{1,0:T(8,128)}) custom-call(f32[8,40,128]{2,1,0:T(8,128)S(1)} %all_to_all.11.buf_ref, f32[16,256]{1,0:T(8,128)S(1)} %get-tuple-element.19.grad_ref, f32[16,256]{1,0:T(8,128)S(1)} %copy-done), custom_call_target="tpu_custom_call" | custom-call | tf_op jit(solution)/shard_map/finish/pallas_call | solution.py:508
  (2 shorter events, 0.0 us)
Async XLA Ops:
  17.3 3.8 %collective-permute-start = (f32[32,128]{1,0:T(8,128)S(1)}, f32[32,128]{1,0:T(8,128)S(1)}, u32[]{:S(2)}, u32[]{:S(2)}) collective-permute-start(f32[32,128]{1,0:T(8,128)S(1)} %flow.1.a_ref), channel_id=1, source_target_pairs={{0,8},{8,0},{16,24},{24,16},{1,9},{9,1},{17,25},{25,17},{2,10},{10... | collective-permute-start | bytes 49160 | tf_op jit(solution)/shard_map/ppermute | solution.py:437
  21.2 7.9 %collective-permute-start.1 = (f32[32,128]{1,0:T(8,128)S(1)}, f32[32,128]{1,0:T(8,128)S(1)}, u32[]{:S(2)}, u32[]{:S(2)}) collective-permute-start(f32[32,128]{1,0:T(8,128)S(1)} %add.1.refs_0_), channel_id=1, source_target_pairs={{0,16},{8,24},{16,0},{24,8},{1,17},{9,25},{17,1},{25,9},{2,18},{10... | collective-permute-start | bytes 49160 | tf_op jit(solution)/shard_map/ppermute | solution.py:437
  23.8 5.2 %copy-start.1 = (f32[16,256]{1,0:T(8,128)S(1)}, f32[16,256]{1,0:T(8,128)}, u32[]{:S(2)}) copy-start(f32[16,256]{1,0:T(8,128)} %cap_ref.1) | copy-start | bytes 49156
  34.4 8.3 %copy-start = (f32[16,256]{1,0:T(8,128)S(1)}, f32[16,256]{1,0:T(8,128)}, u32[]{:S(2)}) copy-start(f32[16,256]{1,0:T(8,128)} %price_ref.1) | copy-start | bytes 49156

commit v5 on v4

--- a/solution.py
+++ b/solution.py
@@ -11,9 +11,11 @@
 REACH = 2
 LANES = 128
 SUB = 8
+PAD = 2 * REACH + 1
 VMEM_GRANT = 24 * 1024 * 1024
 
-TURNS = ((None, None), (0, 1), (2, 3), (4, 5), (6, 0))
+TURNS = ((None, None, 5), (0, 1, 5), (2, 3, 5), (4, 5, 5), (6, 0, 2))
+ROUNDS = sum(turn[2] for turn in TURNS)
 
 step_size = 0.25
 eps_value = 1e-06
@@ -21,10 +23,6 @@
 
 def vmem_spec():
     return pl.BlockSpec(memory_space=pltpu.VMEM)
-
-
-def smem_spec():
-    return pl.BlockSpec(memory_space=pltpu.SMEM)
 
 
 def three_parts(x):
@@ -119,7 +117,7 @@
 
 def halo_store(ref, k, half, groups, span, value):
     blocks = groups * SUB
-    base = k * span + SUB
+    base = k * span + REACH
     ref[base + half * SUB : base + (half + 1) * SUB, :] = value
     if half == groups - 1:
         ref[base - REACH : base, :] = value[SUB - REACH :, :]
@@ -135,7 +133,9 @@
     flow_ref[...] = total
 
 
-def plan_rounds(degree, block_total, half, stage, idx_ref, w_ref, left_idx_ref, left_off_ref, left_w_ref):
+def plan_rounds(
+    degree, block_total, half, stage, stage_w, idx_ref, w_ref, left_idx_ref, left_off_ref, left_w_ref
+):
     groups = block_total // SUB
     width = 2 * REACH + 1
     rows = lax.broadcasted_iota(jnp.int32, (SUB, LANES), 0) + half * SUB
@@ -143,20 +143,20 @@
     over = jnp.full((SUB, LANES), degree, jnp.int32)
     lanes_of, weights, bits, opens, offs = [], [], [], [], []
     for s in range(degree):
-        at = s * block_total + half * SUB
+        at = s * (stage.shape[0] // degree) + half * SUB
         tail = stage[at : at + SUB, :].astype(jnp.int32)
         block = tail // LANES
         lane = tail - block * LANES
         off = block - rows + REACH
         off = jnp.where(off < 0, off + block_total, off)
         off = jnp.where(off >= block_total, off - block_total, off)
-        weight = w_ref[at : at + SUB, :]
+        weight = stage_w[at : at + SUB, :]
         turned = [jnp.left_shift(1, off)]
         for _ in range(3):
             last = turned[-1]
             turned.append(((last << 1) | (last >> (width - 1))) & (2**width - 1))
         open_rounds = jnp.zeros_like(used)
-        for j, (low, high) in enumerate(TURNS):
+        for j, (low, high, count) in enumerate(TURNS):
             if low is None:
                 spot = turned[0]
             else:
@@ -167,23 +167,36 @@
                     jnp.where(by_low, turned[3], turned[2]),
                     jnp.where(by_low, turned[1], turned[0]),
                 )
+            if count < width:
+                spot = spot & (2**count - 1)
             open_rounds = open_rounds | (spot << (width * j))
         free = open_rounds & ~used
         bit = free & -free
-        if s >= len(TURNS):
-            movable = jnp.zeros_like(used)
-            targets = []
+        if s >= len(TURNS) - 1:
+            near, far = jnp.zeros_like(used), jnp.zeros_like(used)
             for earlier, taken in zip(opens, bits):
-                target = earlier & ~used
-                targets.append(target)
-                movable = movable | jnp.where(target != 0, taken, 0)
-            wanted = open_rounds & movable
+                near = near | jnp.where((earlier & ~used) != 0, taken, 0)
+            for earlier, taken in zip(opens, bits):
+                far = far | jnp.where((earlier & near) != 0, taken, 0)
+            straight = open_rounds & near
+            wanted = jnp.where(straight != 0, straight, open_rounds & far)
             wanted = jnp.where(bit == 0, wanted & -wanted, 0)
-            for e, (target, taken) in enumerate(zip(targets, bits)):
-                moved = (taken & wanted) != 0
-                target = jnp.where(moved, target & -target, 0)
-                used = used | target
-                bits[e] = jnp.where(moved, target, taken)
+            twice = jnp.where(straight != 0, 0, wanted)
+            passed = jnp.zeros_like(used)
+            chain = []
+            for earlier, taken in zip(opens, bits):
+                target = earlier & near
+                target = jnp.where((taken & twice) != 0, target & -target, 0)
+                passed = passed | target
+                chain.append(target)
+            last = jnp.where(straight != 0, wanted, passed)
+            freed = ~used
+            for e, (earlier, taken, target) in enumerate(zip(opens, bits, chain)):
+                end = earlier & freed
+                end = jnp.where((taken & last) != 0, end & -end, 0)
+                used = used | end
+                moved = target | end
+                bits[e] = jnp.where(moved != 0, moved, taken)
             bit = bit | wanted
         used = used | bit
         over = jnp.minimum(over, jnp.where(bit == 0, s, degree))
@@ -197,7 +210,7 @@
         left_idx_ref[at : at + SUB, :] = lanes_of[s]
         left_off_ref[at : at + SUB, :] = offs[s]
         left_w_ref[at : at + SUB, :] = jnp.where(bits[s] == 0, weights[s], jnp.float32(jnp.inf))
-    for r in range(width * len(TURNS)):
+    for r in range(ROUNDS):
         idx = jnp.zeros((SUB, LANES), jnp.int32)
         weight = jnp.full((SUB, LANES), jnp.inf, jnp.float32)
         for s in range(degree):
@@ -206,28 +219,27 @@
             weight = jnp.where(hit, weights[s], weight)
         at = (r * groups + half) * SUB
         idx_ref[at : at + SUB, :] = idx
-        w_ref[degree * block_total + at : degree * block_total + at + SUB, :] = weight
+        w_ref[at : at + SUB, :] = weight
     return over
 
 
 def sweep_once(mine, degree, first_over, src, dst, tables):
     idx_ref, w_ref, left_idx_ref, left_off_ref, left_w_ref = tables
     span = src.shape[0] // mine
-    block_total = span - 2 * SUB
+    block_total = span - PAD
     groups = block_total // SUB
     width = 2 * REACH + 1
-    w_base = degree * block_total
     lane = lax.broadcasted_iota(jnp.int32, (SUB, LANES), 1)
     bit_masks = [((lane >> t) & 1) == 1 for t in range(LANES.bit_length() - 1)]
     for half in range(groups):
-        best = [src[k * span + SUB + half * SUB : k * span + SUB + (half + 1) * SUB, :] for k in range(mine)]
-        for j, (low, high) in enumerate(TURNS):
-            for q in range(width):
+        best = [src[k * span + REACH + half * SUB : k * span + REACH + (half + 1) * SUB, :] for k in range(mine)]
+        for j, (low, high, count) in enumerate(TURNS):
+            for q in range(count):
                 at = ((j * width + q) * groups + half) * SUB
                 idx = idx_ref[at : at + SUB, :]
-                w = w_ref[w_base + at : w_base + at + SUB, :]
+                w = w_ref[at : at + SUB, :]
                 for k in range(mine):
-                    base = k * span + SUB + half * SUB - REACH
+                    base = k * span + half * SUB
 
                     def block(turned):
                         o = base + (q - turned) % width
@@ -254,7 +266,7 @@
             off = left_off_ref[pl.ds(at, SUB), :]
             w = left_w_ref[pl.ds(at, SUB), :]
             for k in range(mine):
-                base = k * span + SUB + half * SUB
+                base = k * span + REACH + half * SUB
                 picked = None
                 for o in range(width):
                     start = base + o - REACH
@@ -276,12 +288,13 @@
 def begin_kernel(
     mine, degree, source_hbm, buf_ref,
     x_ref, idx_ref, w_ref, left_idx_ref, left_off_ref, left_w_ref, over_ref,
-    stage, stage_tail, source_ref, sems,
+    stage, stage_tail, stage_w, source_ref, sems,
 ):
     (copy,) = fetch(((source_hbm, source_ref),), sems)
+    pitch = stage.shape[0] // mine
     peers = buf_ref.shape[0]
     span = x_ref.shape[0] // mine
-    block_total = span - 2 * SUB
+    block_total = span - PAD
     groups = block_total // SUB
     shard_blocks = block_total // peers
     arc_rows = degree * shard_blocks
@@ -289,19 +302,18 @@
     for i in range(peers):
         for b in range(shard_blocks):
             blk = i * shard_blocks + b
-            stage[pl.ds(blk, mine, stride=block_total), :] = buf_ref[i, b * mine : (b + 1) * mine, :]
+            stage[pl.ds(blk, mine, stride=pitch), :] = buf_ref[i, b * mine : (b + 1) * mine, :]
             s0 = base + b * degree
-            stage_tail[pl.ds(blk, degree, stride=block_total), :] = buf_ref[i, s0 : s0 + degree, :]
+            stage_tail[pl.ds(blk, degree, stride=pitch), :] = buf_ref[i, s0 : s0 + degree, :]
             s1 = base + arc_rows + b * degree
-            w_ref[pl.ds(blk, degree, stride=block_total), :] = buf_ref[i, s1 : s1 + degree, :]
+            stage_w[pl.ds(blk, degree, stride=pitch), :] = buf_ref[i, s1 : s1 + degree, :]
     over = None
     for half in range(groups):
         part = plan_rounds(
-            degree, block_total, half, stage_tail, idx_ref, w_ref,
+            degree, block_total, half, stage_tail, stage_w, idx_ref, w_ref,
             left_idx_ref, left_off_ref, left_w_ref,
         )
         over = part if over is None else jnp.minimum(over, part)
-    over_ref[0] = jnp.min(over.astype(jnp.float32)).astype(jnp.int32)
     copy.wait()
     rows = lax.broadcasted_iota(jnp.int32, (SUB, LANES), 0)
     lanes = lax.broadcasted_iota(jnp.int32, (SUB, LANES), 1)
@@ -309,9 +321,10 @@
     for half in range(groups):
         node = (rows + half * SUB) * LANES + lanes
         for k in range(mine):
-            at = k * block_total + half * SUB
+            at = k * pitch + half * SUB
             value = jnp.where(node == source_ref[first + k], jnp.float32(0.0), stage[at : at + SUB, :])
             halo_store(x_ref, k, half, groups, span, value)
+    over_ref[...] = jnp.full(over_ref.shape, jnp.min(over.astype(jnp.float32)).astype(jnp.int32))
 
 
 def add_kernel(a_ref, b_ref, after_ref, out_ref):
@@ -324,7 +337,7 @@
 ):
     x_ref[...] = start_ref[...]
     tables = (idx_ref, w_ref, left_idx_ref, left_off_ref, left_w_ref)
-    sweep_pairs(count, mine, degree, over_ref[0], x_ref, other, tables)
+    sweep_pairs(count, mine, degree, over_ref[0, 0], x_ref, other, tables)
 
 
 def end_kernel(
@@ -334,10 +347,10 @@
     flow_refs, (out_ref, grad_ref, x_ref, other) = refs[:parts], refs[parts:]
     peers = out_ref.shape[0]
     span = x_ref.shape[0] // mine
-    block_total = span - 2 * SUB
+    block_total = span - PAD
     shard_blocks = block_total // peers
     tables = (idx_ref, w_ref, left_idx_ref, left_off_ref, left_w_ref)
-    first_over = over_ref[0]
+    first_over = over_ref[0, 0]
     x_ref[...] = start_ref[...]
     sweep_pairs(count, mine, degree, first_over, x_ref, other, tables)
     square = None
@@ -355,7 +368,7 @@
     base = mine * shard_blocks
     for i in range(peers):
         for b in range(shard_blocks):
-            blk = SUB + i * shard_blocks + b
+            blk = REACH + i * shard_blocks + b
             out_ref[i, b * mine : (b + 1) * mine, :] = x_ref[pl.ds(blk, mine, stride=span), :]
         out_ref[i, base : base + SUB, :] = folded
 
@@ -388,12 +401,12 @@
     mine = commodities // peers
     shard_blocks = shard_nodes // LANES
     block_total = node_count // LANES
-    span = block_total + 2 * SUB
+    span = block_total + PAD
     arc_rows = degree * shard_blocks
     f32, i32 = jnp.float32, jnp.int32
     shape = jax.ShapeDtypeStruct
     near = pltpu.VMEM
-    v, s = vmem_spec, smem_spec
+    v = vmem_spec
 
     def held(x):
         return pltpu.with_memory_space_constraint(x, pltpu.VMEM)
@@ -441,7 +454,7 @@
         flow, steps = held(lax.psum(flow, "comm")), 0
     arrived = exchange(0) if steps else None
 
-    rounds = (2 * REACH + 1) * len(TURNS)
+    rounds = ROUNDS
     table = degree * block_total
     state = (mine * span, LANES)
     x, *tables, over = pl.pallas_call(
@@ -449,17 +462,18 @@
         out_shape=(
             near(state, f32),
             near((rounds * block_total, LANES), i32),
-            near((table + rounds * block_total, LANES), f32),
+            near((rounds * block_total, LANES), f32),
             near((table, LANES), i32),
             near((table, LANES), i32),
             near((table, LANES), f32),
-            shape((1,), i32),
+            near((SUB, LANES), i32),
         ),
         in_specs=[h(), v()],
-        out_specs=(v(), v(), v(), v(), v(), v(), s()),
+        out_specs=(v(),) * 7,
         scratch_shapes=[
-            pltpu.VMEM((mine * block_total, LANES), f32),
-            pltpu.VMEM((table, LANES), f32),
+            pltpu.VMEM((mine * (block_total + 1), LANES), f32),
+            pltpu.VMEM((degree * (block_total + 1), LANES), f32),
+            pltpu.VMEM((degree * (block_total + 1), LANES), f32),
             pltpu.SMEM(source_node.shape, i32),
             pltpu.SemaphoreType.DMA((1,)),
         ],
@@ -467,7 +481,7 @@
         name="begin",
     )(far(source_node), received)
 
-    tables = tuple(map(held, tables))
+    tables, over = tuple(map(held, tables)), held(over)
     left = SWEEPS
     for step in range(1, steps):
         flow = pl.pallas_call(
@@ -484,7 +498,7 @@
         x = pl.pallas_call(
             functools.partial(middle_kernel, mine, degree, count),
             out_shape=near(state, f32),
-            in_specs=[s()] + [v()] * (len(tables) + 1),
+            in_specs=[v()] * (len(tables) + 2),
             out_specs=v(),
             scratch_shapes=[pltpu.VMEM(state, f32)],
             compiler_params=params,
@@ -498,7 +512,7 @@
             near((peers, mine * shard_blocks + SUB, LANES), f32),
             near((degree, shard_nodes), f32),
         ),
-        in_specs=[s()] + [v()] * (len(tables) + 2 + len(flows)),
+        in_specs=[v()] * (len(tables) + 3 + len(flows)),
         out_specs=(v(), v()),
         scratch_shapes=[pltpu.VMEM(state, f32), pltpu.VMEM(state, f32)],
         compiler_params=params,

time: 43.7 us -> 40.9 us (0.936)
  Pallas kernels: 15.4 us -> 12.3 us
  waiting for transfers between devices: 0.01 us -> 0.47 us
    pallas_call x1, Pallas kernels: 5.3 us -> 3.99 us  [shards(): pl.pallas_call(functools.partial(end_kernel, mine, degree, left, len(flow...]
    pallas_call x1, Pallas kernels: 5.22 us -> 3.96 us  [shards(): pl.pallas_call(functools.partial(middle_kernel, mine, degree, count), out...]
    pallas_call x1, Pallas kernels: 2.19 us -> 1.69 us  [shards(): pl.pallas_call(functools.partial(begin_kernel, mine, degree), out_shape=(...]
    ppermute x2, waiting for transfers between devices: 0.01 us -> 0.47 us  [exchange(): return held(lax.ppermute(flow, 'comm', pairs))]
  transfers between devices with their start and end apart: 2 -> 2, of which waited for: 0 -> 1; matrix products, arithmetic and copies ran while one was open for 0% -> 0% of each run, Pallas kernels for 17% -> 14%
where the time goes in v5:
time: 40.9 us; the launch traced here: 40.7 us
  blocking collectives  23 us (56%)
  Pallas kernels  12.3 us (30%)
  starting transfers between devices  4.22 us (10%)
  between operations  0.69 us (2%)
  waiting for transfers between devices  0.47 us (1%)
    all_to_all x1, blocking collectives, shards(): received = held(lax.all_to_all(packed, 'arc', 0, 0, tiled=True))  14.7 us
    all_to_all x1, blocking collectives, shards(): final = held(lax.all_to_all(back, 'arc', 0, 0, tiled=True))  8.25 us
    ppermute x2, starting transfers between devices, exchange(): return held(lax.ppermute(flow, 'comm', pairs))  4.22 us
    pallas_call x1, Pallas kernels, shards(): pl.pallas_call(functools.partial(end_kernel, mine, degree, left, len(flow...  3.99 us
    pallas_call x1, Pallas kernels, shards(): pl.pallas_call(functools.partial(middle_kernel, mine, degree, count), out...  3.96 us
    pallas_call x1, Pallas kernels, shards(): pl.pallas_call(functools.partial(pack_kernel, node_count), out_shape=near...  1.94 us
    pallas_call x1, Pallas kernels, shards(): pl.pallas_call(functools.partial(begin_kernel, mine, degree), out_shape=(...  1.69 us
  transfers between devices with their start and end apart: 2, of which 1 were waited for; matrix products, arithmetic and copies ran while one was open for 0% of the time, Pallas kernels for 14%

profile of v5, /device:TPU:0, one launch (start us, length us, event | category | flops | bytes accessed | tf_op | source)
XLA Modules:
  0.0 40.7 jit_solution(10230026664936364152)
XLA Ops:
  0.6 1.9 %pack.1 = f32[8,128,128]{2,1,0:T(8,128)S(1)} custom-call(s32[16,128]{1,0:T(8,128)} %path_hbm.1, f32[16]{0:T(128)} %demand_hbm.1, s32[16,256]{1,0:T(8,128)} %tail_hbm.1, f32[16,256]{1,0:T(8,128)} %cost_hbm.1, f32[16,256]{1,0:T(8,128)} %price_ref.1, f32[128,256]{1,0:T(8,128)} %dist_hbm.1), custom_call_target="tpu_custom_call" | custom-call | tf_op jit(solution)/shard_map/pack/pallas_call | solution.py:423
  2.6 14.7 %all_to_all.10.buf_ref = f32[8,128,128]{2,1,0:T(8,128)S(1)} all-to-all(f32[8,128,128]{2,1,0:T(8,128)S(1)} %pack.1), channel_id=1, replica_groups=mesh['comm'=4,'arc'=8] {'arc'}, dimensions={0} | all-to-all | bytes 1048576 | tf_op jit(solution)/shard_map/all_to_all | solution.py:437
  17.3 1.6 %collective-permute-start = (f32[32,128]{1,0:T(8,128)S(1)}, f32[32,128]{1,0:T(8,128)S(1)}, u32[]{:S(2)}, u32[]{:S(2)}) collective-permute-start(f32[32,128]{1,0:T(8,128)S(1)} %flow.1.a_ref), channel_id=1, source_target_pairs={{0,8},{8,0},{16,24},{24,16},{1,9},{9,1},{17,25},{25,17},{2,10},{10... | collective-permute-start | bytes 49160 | tf_op jit(solution)/shard_map/ppermute | solution.py:450
  18.9 1.7 %begin.1 = (f32[336,128]{1,0:T(8,128)S(1)}, s32[352,128]{1,0:T(8,128)S(1)}, f32[352,128]{1,0:T(8,128)S(1)}, s32[256,128]{1,0:T(8,128)S(1)}, s32[256,128]{1,0:T(8...) custom-call(s32[128]{0:T(128)} %source_hbm.1, f32[8,128,128]{2,1,0:T(8,128)S(1)} %all_to_all.10.buf_ref), custom_call_target="tpu_custom_call" | custom-call | tf_op jit(solution)/shard_map/begin/pallas_call | solution.py:460
  20.6 0.5 %collective-permute-done.b_ref = f32[32,128]{1,0:T(8,128)S(1)} collective-permute-done((f32[32,128]{1,0:T(8,128)S(1)}, f32[32,128]{1,0:T(8,128)S(1)}, u32[]{:S(2)}, u32[]{:S(2)}) %collective-permute-start) | collective-permute-done | bytes 16416 | tf_op jit(solution)/shard_map/ppermute | solution.py:450
  21.1 2.6 %collective-permute-start.1 = (f32[32,128]{1,0:T(8,128)S(1)}, f32[32,128]{1,0:T(8,128)S(1)}, u32[]{:S(2)}, u32[]{:S(2)}) collective-permute-start(f32[32,128]{1,0:T(8,128)S(1)} %add.1.refs_0_), channel_id=1, source_target_pairs={{0,16},{8,24},{16,0},{24,8},{1,17},{9,25},{17,1},{25,9},{2,18},{10... | collective-permute-start | bytes 49160 | tf_op jit(solution)/shard_map/ppermute | solution.py:450
  23.7 0.0 copy-start.1
  23.7 4.0 %middle.1.start_ref = f32[336,128]{1,0:T(8,128)S(1)} custom-call(s32[8,128]{1,0:T(8,128)S(1)} %get-tuple-element.11.over_ref, f32[336,128]{1,0:T(8,128)S(1)} %get-tuple-element.12.start_ref.after_ref, s32[352,128]{1,0:T(8,128)S(1)} %get-tuple-element.13.idx_ref, f32[352,128]{1,0:T(8,128)S(1)} %get-tuple-element.14.w_ref, ...), custom_call_target="tpu_custom_call" | custom-call | tf_op jit(solution)/shard_map/middle/pallas_call | solution.py:498
  27.7 0.0 collective-permute-done.1.refs_1_
  27.7 0.0 copy-done.1
  27.7 4.0 %end.1 = (f32[8,40,128]{2,1,0:T(8,128)S(1)}, f32[16,256]{1,0:T(8,128)S(1)}) custom-call(s32[8,128]{1,0:T(8,128)S(1)} %get-tuple-element.11.over_ref, f32[336,128]{1,0:T(8,128)S(1)} %middle.1.start_ref, s32[352,128]{1,0:T(8,128)S(1)} %get-tuple-element.13.idx_ref, f32[352,128]{1,0:T(8,128)S(1)} %get-tuple-element.14.w_ref, ...), custom_call_target="tpu_custom_call" | custom-call | tf_op jit(solution)/shard_map/end/pallas_call | solution.py:509
  31.7 0.0 copy-start
  31.7 8.2 %all_to_all.11.buf_ref = f32[8,40,128]{2,1,0:T(8,128)S(1)} all-to-all(f32[8,40,128]{2,1,0:T(8,128)S(1)} %get-tuple-element.18), channel_id=1, replica_groups=mesh['comm'=4,'arc'=8] {'arc'}, dimensions={0} | all-to-all | bytes 327680 | tf_op jit(solution)/shard_map/all_to_all | solution.py:521
  39.9 0.0 copy-done
  39.9 0.7 %finish.1 = (f32[128,256]{1,0:T(8,128)}, f32[16,256]{1,0:T(8,128)}) custom-call(f32[8,40,128]{2,1,0:T(8,128)S(1)} %all_to_all.11.buf_ref, f32[16,256]{1,0:T(8,128)S(1)} %get-tuple-element.19.grad_ref, f32[16,256]{1,0:T(8,128)S(1)} %copy-done), custom_call_target="tpu_custom_call" | custom-call | tf_op jit(solution)/shard_map/finish/pallas_call | solution.py:522
  (2 shorter events, 0.0 us)
Async XLA Ops:
  17.3 3.8 %collective-permute-start = (f32[32,128]{1,0:T(8,128)S(1)}, f32[32,128]{1,0:T(8,128)S(1)}, u32[]{:S(2)}, u32[]{:S(2)}) collective-permute-start(f32[32,128]{1,0:T(8,128)S(1)} %flow.1.a_ref), channel_id=1, source_target_pairs={{0,8},{8,0},{16,24},{24,16},{1,9},{9,1},{17,25},{25,17},{2,10},{10... | collective-permute-start | bytes 49160 | tf_op jit(solution)/shard_map/ppermute | solution.py:450
  21.1 6.6 %collective-permute-start.1 = (f32[32,128]{1,0:T(8,128)S(1)}, f32[32,128]{1,0:T(8,128)S(1)}, u32[]{:S(2)}, u32[]{:S(2)}) collective-permute-start(f32[32,128]{1,0:T(8,128)S(1)} %add.1.refs_0_), channel_id=1, source_target_pairs={{0,16},{8,24},{16,0},{24,8},{1,17},{9,25},{17,1},{25,9},{2,18},{10... | collective-permute-start | bytes 49160 | tf_op jit(solution)/shard_map/ppermute | solution.py:450
  23.7 4.0 %copy-start.1 = (f32[16,256]{1,0:T(8,128)S(1)}, f32[16,256]{1,0:T(8,128)}, u32[]{:S(2)}) copy-start(f32[16,256]{1,0:T(8,128)} %cap_ref.1) | copy-start | bytes 49156
  31.7 8.3 %copy-start = (f32[16,256]{1,0:T(8,128)S(1)}, f32[16,256]{1,0:T(8,128)}, u32[]{:S(2)}) copy-start(f32[16,256]{1,0:T(8,128)} %price_ref.1) | copy-start | bytes 49156

commit v6 on v5

--- a/solution.py
+++ b/solution.py
@@ -103,15 +103,18 @@
     tail = tail_ref[...].astype(jnp.float32)
     weight = cost_ref[...] + price_ref[...]
     arc_rows = degree * shard_blocks
+    half = degree // 2
+    half_rows = half * shard_blocks
     base = mine * shard_blocks
     for j in range(peers):
+        slots = slice(j % 2 * half, (j % 2 + 1) * half)
         for b in range(shard_blocks):
             cols = slice(b * LANES, (b + 1) * LANES)
             out_ref[j, b * mine : (b + 1) * mine, :] = dist_ref[j * mine : (j + 1) * mine, cols]
-            out_ref[j, base + b * degree : base + (b + 1) * degree, :] = tail[:, cols]
-            start = base + arc_rows + b * degree
-            out_ref[j, start : start + degree, :] = weight[:, cols]
-        start = base + 2 * arc_rows
+            out_ref[j, base + b * half : base + (b + 1) * half, :] = tail[slots, cols]
+            start = base + half_rows + b * half
+            out_ref[j, start : start + half, :] = weight[slots, cols]
+        start = base + 2 * half_rows
         out_ref[j, start : start + arc_rows, :] = flow[j * arc_rows : (j + 1) * arc_rows, :]
 
 
@@ -125,11 +128,14 @@
         ref[base + blocks : base + blocks + REACH, :] = value[:REACH, :]
 
 
-def flow_kernel(rows, buf_ref, flow_ref):
+def split_kernel(buf_ref, flow_ref, arcs_ref):
     total = None
+    rows = flow_ref.shape[0]
+    end = buf_ref.shape[1] - rows
     for i in range(buf_ref.shape[0]):
-        part = buf_ref[i, buf_ref.shape[1] - rows :, :]
+        part = buf_ref[i, end:, :]
         total = part if total is None else total + part
+        arcs_ref[i, :, :] = buf_ref[i, end - arcs_ref.shape[1] : end, :]
     flow_ref[...] = total
 
 
@@ -286,7 +292,7 @@
 
 
 def begin_kernel(
-    mine, degree, source_hbm, buf_ref,
+    mine, degree, source_hbm, buf_ref, own_ref, partner_ref,
     x_ref, idx_ref, w_ref, left_idx_ref, left_off_ref, left_w_ref, over_ref,
     stage, stage_tail, stage_w, source_ref, sems,
 ):
@@ -297,16 +303,16 @@
     block_total = span - PAD
     groups = block_total // SUB
     shard_blocks = block_total // peers
-    arc_rows = degree * shard_blocks
-    base = mine * shard_blocks
+    half = degree // 2
     for i in range(peers):
         for b in range(shard_blocks):
             blk = i * shard_blocks + b
             stage[pl.ds(blk, mine, stride=pitch), :] = buf_ref[i, b * mine : (b + 1) * mine, :]
-            s0 = base + b * degree
-            stage_tail[pl.ds(blk, degree, stride=pitch), :] = buf_ref[i, s0 : s0 + degree, :]
-            s1 = base + arc_rows + b * degree
-            stage_w[pl.ds(blk, degree, stride=pitch), :] = buf_ref[i, s1 : s1 + degree, :]
+            for side, ref in enumerate((own_ref, partner_ref)):
+                at = pl.ds(side * half * pitch + blk, half, stride=pitch)
+                stage_tail[at, :] = ref[i, b * half : (b + 1) * half, :]
+                start = half * shard_blocks + b * half
+                stage_w[at, :] = ref[i, start : start + half, :]
     over = None
     for half in range(groups):
         part = plan_rounds(
@@ -422,7 +428,7 @@
     arcs = (arc_tail, base_cost, arc_price, prev_dist)
     packed = pl.pallas_call(
         functools.partial(pack_kernel, node_count),
-        out_shape=near((peers, mine * shard_blocks + 3 * arc_rows, LANES), f32),
+        out_shape=near((peers, mine * shard_blocks + 2 * arc_rows, LANES), f32),
         in_specs=[h()] * 6,
         out_specs=v(),
         scratch_shapes=[
@@ -436,14 +442,16 @@
     )(far(path_arcs), far(demand), *map(far, arcs))
     received = held(lax.all_to_all(packed, "arc", 0, 0, tiled=True))
 
-    flow = pl.pallas_call(
-        functools.partial(flow_kernel, arc_rows),
-        out_shape=near((arc_rows, LANES), f32),
+    flow, own = pl.pallas_call(
+        split_kernel,
+        out_shape=(near((arc_rows, LANES), f32), near((peers, arc_rows, LANES), f32)),
         in_specs=[v()],
-        out_specs=v(),
+        out_specs=(v(), v()),
         compiler_params=params,
-        name="flow",
+        name="split",
     )(received)
+    own = held(own)
+    partner = held(lax.ppermute(own, "arc", [(i, i ^ 1) for i in range(peers)]))
 
     def exchange(step):
         pairs = [(i, i ^ (1 << step)) for i in range(groups)]
@@ -468,7 +476,7 @@
             near((table, LANES), f32),
             near((SUB, LANES), i32),
         ),
-        in_specs=[h(), v()],
+        in_specs=[h(), v(), v(), v()],
         out_specs=(v(),) * 7,
         scratch_shapes=[
             pltpu.VMEM((mine * (block_total + 1), LANES), f32),
@@ -479,7 +487,7 @@
         ],
         compiler_params=params,
         name="begin",
-    )(far(source_node), received)
+    )(far(source_node), received, own, partner)
 
     tables, over = tuple(map(held, tables)), held(over)
     left = SWEEPS

time: 40.9 us -> 39.6 us (0.968)
  blocking collectives: 23 us -> 21.6 us
    all_to_all x1, blocking collectives: 14.7 us -> 13.3 us  [shards(): received = held(lax.all_to_all(packed, 'arc', 0, 0, tiled=True))]
  transfers between devices with their start and end apart: 2 -> 3, of which waited for: 1 -> 1; matrix products, arithmetic and copies ran while one was open for 0% -> 0% of each run, Pallas kernels for 14% -> 14%
where the time goes in v6:
time: 39.6 us; the launch traced here: 39.3 us
  blocking collectives  21.6 us (55%)
  Pallas kernels  12.3 us (31%)
  starting transfers between devices  4.29 us (11%)
  between operations  0.7 us (2%)
  waiting for transfers between devices  0.46 us (1%)
    all_to_all x1, blocking collectives, shards(): received = held(lax.all_to_all(packed, 'arc', 0, 0, tiled=True))  13.3 us
    all_to_all x1, blocking collectives, shards(): final = held(lax.all_to_all(back, 'arc', 0, 0, tiled=True))  8.25 us
    ppermute x2, starting transfers between devices, exchange(): return held(lax.ppermute(flow, 'comm', pairs))  4.22 us
    pallas_call x1, Pallas kernels, shards(): pl.pallas_call(functools.partial(end_kernel, mine, degree, left, len(flow...  3.99 us
    pallas_call x1, Pallas kernels, shards(): pl.pallas_call(functools.partial(middle_kernel, mine, degree, count), out...  3.96 us
    pallas_call x1, Pallas kernels, shards(): pl.pallas_call(functools.partial(pack_kernel, node_count), out_shape=near...  1.93 us
    pallas_call x1, Pallas kernels, shards(): pl.pallas_call(functools.partial(begin_kernel, mine, degree), out_shape=(...  1.71 us
  transfers between devices with their start and end apart: 3, of which 1 were waited for; matrix products, arithmetic and copies ran while one was open for 0% of the time, Pallas kernels for 14%

profile of v6, /device:TPU:0, one launch (start us, length us, event | category | flops | bytes accessed | tf_op | source)
XLA Modules:
  0.0 39.3 jit_solution(3684138983732369265)
XLA Ops:
  0.6 1.9 %pack.1 = f32[8,96,128]{2,1,0:T(8,128)S(1)} custom-call(s32[16,128]{1,0:T(8,128)} %path_hbm.1, f32[16]{0:T(128)} %demand_hbm.1, s32[16,256]{1,0:T(8,128)} %tail_hbm.1, f32[16,256]{1,0:T(8,128)} %cost_hbm.1, f32[16,256]{1,0:T(8,128)} %price_ref.1, f32[128,256]{1,0:T(8,128)} %dist_hbm.1), custom_call_target="tpu_custom_call" | custom-call | tf_op jit(solution)/shard_map/pack/pallas_call | solution.py:429
  2.6 13.3 %all_to_all.10.buf_ref = f32[8,96,128]{2,1,0:T(8,128)S(1)} all-to-all(f32[8,96,128]{2,1,0:T(8,128)S(1)} %pack.1), channel_id=1, replica_groups=mesh['comm'=4,'arc'=8] {'arc'}, dimensions={0} | all-to-all | bytes 786432 | tf_op jit(solution)/shard_map/all_to_all | solution.py:443
  15.9 0.1 collective-permute-start
  16.0 1.6 %collective-permute-start.1 = (f32[32,128]{1,0:T(8,128)S(1)}, f32[32,128]{1,0:T(8,128)S(1)}, u32[]{:S(2)}, u32[]{:S(2)}) collective-permute-start(f32[32,128]{1,0:T(8,128)S(1)} %get-tuple-element.21.a_ref), channel_id=1, source_target_pairs={{0,8},{8,0},{16,24},{24,16},{1,9},{9,1},{17,25},{25,17},{2,10},{10... | collective-permute-start | bytes 49160 | tf_op jit(solution)/shard_map/ppermute | solution.py:458
  17.6 0.0 collective-permute-done.partner_ref
  17.6 1.7 %begin.1 = (f32[336,128]{1,0:T(8,128)S(1)}, s32[352,128]{1,0:T(8,128)S(1)}, f32[352,128]{1,0:T(8,128)S(1)}, s32[256,128]{1,0:T(8,128)S(1)}, s32[256,128]{1,0:T(8...) custom-call(s32[128]{0:T(128)} %source_hbm.1, f32[8,96,128]{2,1,0:T(8,128)S(1)} %all_to_all.10.buf_ref, ...), custom_call_target="tpu_custom_call" | custom-call | tf_op jit(solution)/shard_map/begin/pallas_call | solution.py:468
  19.3 0.5 %collective-permute-done.1.b_ref = f32[32,128]{1,0:T(8,128)S(1)} collective-permute-done((f32[32,128]{1,0:T(8,128)S(1)}, f32[32,128]{1,0:T(8,128)S(1)}, u32[]{:S(2)}, u32[]{:S(2)}) %collective-permute-start.1) | collective-permute-done | bytes 16416 | tf_op jit(solution)/shard_map/ppermute | solution.py:458
  19.8 2.6 %collective-permute-start.2 = (f32[32,128]{1,0:T(8,128)S(1)}, f32[32,128]{1,0:T(8,128)S(1)}, u32[]{:S(2)}, u32[]{:S(2)}) collective-permute-start(f32[32,128]{1,0:T(8,128)S(1)} %add.1.refs_0_), channel_id=1, source_target_pairs={{0,16},{8,24},{16,0},{24,8},{1,17},{9,25},{17,1},{25,9},{2,18},{10... | collective-permute-start | bytes 49160 | tf_op jit(solution)/shard_map/ppermute | solution.py:458
  22.4 0.0 copy-start.1
  22.4 4.0 %middle.1.start_ref = f32[336,128]{1,0:T(8,128)S(1)} custom-call(s32[8,128]{1,0:T(8,128)S(1)} %get-tuple-element.14.over_ref, f32[336,128]{1,0:T(8,128)S(1)} %get-tuple-element.15.start_ref.after_ref, s32[352,128]{1,0:T(8,128)S(1)} %get-tuple-element.16.idx_ref, f32[352,128]{1,0:T(8,128)S(1)} %get-tuple-element.17.w_ref, ...), custom_call_target="tpu_custom_call" | custom-call | tf_op jit(solution)/shard_map/middle/pallas_call | solution.py:506
  26.3 0.0 collective-permute-done.2.refs_1_
  26.3 0.0 copy-done.1
  26.4 4.0 %end.1 = (f32[8,40,128]{2,1,0:T(8,128)S(1)}, f32[16,256]{1,0:T(8,128)S(1)}) custom-call(s32[8,128]{1,0:T(8,128)S(1)} %get-tuple-element.14.over_ref, f32[336,128]{1,0:T(8,128)S(1)} %middle.1.start_ref, s32[352,128]{1,0:T(8,128)S(1)} %get-tuple-element.16.idx_ref, f32[352,128]{1,0:T(8,128)S(1)} %get-tuple-element.17.w_ref, ...), custom_call_target="tpu_custom_call" | custom-call | tf_op jit(solution)/shard_map/end/pallas_call | solution.py:517
  30.3 0.0 copy-start
  30.4 8.2 %all_to_all.11.buf_ref = f32[8,40,128]{2,1,0:T(8,128)S(1)} all-to-all(f32[8,40,128]{2,1,0:T(8,128)S(1)} %get-tuple-element.22), channel_id=1, replica_groups=mesh['comm'=4,'arc'=8] {'arc'}, dimensions={0} | all-to-all | bytes 327680 | tf_op jit(solution)/shard_map/all_to_all | solution.py:529
  38.6 0.0 copy-done
  38.6 0.7 %finish.1 = (f32[128,256]{1,0:T(8,128)}, f32[16,256]{1,0:T(8,128)}) custom-call(f32[8,40,128]{2,1,0:T(8,128)S(1)} %all_to_all.11.buf_ref, f32[16,256]{1,0:T(8,128)S(1)} %get-tuple-element.23.grad_ref, f32[16,256]{1,0:T(8,128)S(1)} %copy-done), custom_call_target="tpu_custom_call" | custom-call | tf_op jit(solution)/shard_map/finish/pallas_call | solution.py:530
  (2 shorter events, 0.0 us)
Async XLA Ops:
  15.9 1.7 %collective-permute-start = (f32[8,32,128]{2,1,0:T(8,128)S(1)}, f32[8,32,128]{2,1,0:T(8,128)S(1)}, u32[]{:S(2)}, u32[]{:S(2)}) collective-permute-start(f32[8,32,128]{2,1,0:T(8,128)S(1)} %get-tuple-element.13.own_ref), channel_id=1, source_target_pairs={{0,1},{1,0},{2,3},{3,2},{4,5},{5,4},{6,7},{7,6},{8,9},{9,8},{10,11... | collective-permute-start | bytes 393224 | tf_op jit(solution)/shard_map/ppermute | solution.py:454
  16.0 3.8 %collective-permute-start.1 = (f32[32,128]{1,0:T(8,128)S(1)}, f32[32,128]{1,0:T(8,128)S(1)}, u32[]{:S(2)}, u32[]{:S(2)}) collective-permute-start(f32[32,128]{1,0:T(8,128)S(1)} %get-tuple-element.21.a_ref), channel_id=1, source_target_pairs={{0,8},{8,0},{16,24},{24,16},{1,9},{9,1},{17,25},{25,17},{2,10},{10... | collective-permute-start | bytes 49160 | tf_op jit(solution)/shard_map/ppermute | solution.py:458
  19.8 6.6 %collective-permute-start.2 = (f32[32,128]{1,0:T(8,128)S(1)}, f32[32,128]{1,0:T(8,128)S(1)}, u32[]{:S(2)}, u32[]{:S(2)}) collective-permute-start(f32[32,128]{1,0:T(8,128)S(1)} %add.1.refs_0_), channel_id=1, source_target_pairs={{0,16},{8,24},{16,0},{24,8},{1,17},{9,25},{17,1},{25,9},{2,18},{10... | collective-permute-start | bytes 49160 | tf_op jit(solution)/shard_map/ppermute | solution.py:458
  22.4 4.0 %copy-start.1 = (f32[16,256]{1,0:T(8,128)S(1)}, f32[16,256]{1,0:T(8,128)}, u32[]{:S(2)}) copy-start(f32[16,256]{1,0:T(8,128)} %cap_ref.1) | copy-start | bytes 49156
  30.3 8.3 %copy-start = (f32[16,256]{1,0:T(8,128)S(1)}, f32[16,256]{1,0:T(8,128)}, u32[]{:S(2)}) copy-start(f32[16,256]{1,0:T(8,128)} %price_ref.1) | copy-start | bytes 49156

commit v7 on v5

--- a/solution.py
+++ b/solution.py
@@ -55,7 +55,7 @@
         ),
         sems,
     )
-    peers = out_ref.shape[0]
+    peers = 2 * out_ref.shape[0]
     degree, shard_nodes = tail_ref.shape
     shard_blocks = shard_nodes // LANES
     mine = dist_ref.shape[0] // peers
@@ -103,16 +103,29 @@
     tail = tail_ref[...].astype(jnp.float32)
     weight = cost_ref[...] + price_ref[...]
     arc_rows = degree * shard_blocks
-    base = mine * shard_blocks
-    for j in range(peers):
+    dist_rows = mine * shard_blocks
+    even = lax.axis_index("arc") % 2 == 0
+    for pair in range(peers // 2):
         for b in range(shard_blocks):
             cols = slice(b * LANES, (b + 1) * LANES)
-            out_ref[j, b * mine : (b + 1) * mine, :] = dist_ref[j * mine : (j + 1) * mine, cols]
-            out_ref[j, base + b * degree : base + (b + 1) * degree, :] = tail[:, cols]
-            start = base + arc_rows + b * degree
-            out_ref[j, start : start + degree, :] = weight[:, cols]
-        start = base + 2 * arc_rows
-        out_ref[j, start : start + arc_rows, :] = flow[j * arc_rows : (j + 1) * arc_rows, :]
+            first, second = (
+                dist_ref[j * mine : (j + 1) * mine, cols] for j in (2 * pair, 2 * pair + 1)
+            )
+            at = b * mine
+            out_ref[pair, at : at + mine, :] = jnp.where(even, first, second)
+            at = dist_rows + b * degree
+            out_ref[pair, at : at + degree, :] = tail[:, cols]
+            at = at + arc_rows
+            out_ref[pair, at : at + degree, :] = weight[:, cols]
+            at = dist_rows + 2 * arc_rows + b * mine
+            out_ref[pair, at : at + mine, :] = jnp.where(even, second, first)
+        first, second = (
+            flow[j * arc_rows : (j + 1) * arc_rows, :] for j in (2 * pair, 2 * pair + 1)
+        )
+        at = 2 * dist_rows + 2 * arc_rows
+        out_ref[pair, at : at + arc_rows, :] = jnp.where(even, first, second)
+        at = at + arc_rows
+        out_ref[pair, at : at + arc_rows, :] = jnp.where(even, second, first)
 
 
 def halo_store(ref, k, half, groups, span, value):
@@ -125,11 +138,13 @@
         ref[base + blocks : base + blocks + REACH, :] = value[:REACH, :]
 
 
-def flow_kernel(rows, buf_ref, flow_ref):
+def split_kernel(buf_ref, flow_ref, pass_ref):
     total = None
+    end = buf_ref.shape[1] - flow_ref.shape[0]
     for i in range(buf_ref.shape[0]):
-        part = buf_ref[i, buf_ref.shape[1] - rows :, :]
+        part = buf_ref[i, end:, :]
         total = part if total is None else total + part
+        pass_ref[i, :, :] = buf_ref[i, end - pass_ref.shape[1] : end, :]
     flow_ref[...] = total
 
 
@@ -181,22 +196,22 @@
             straight = open_rounds & near
             wanted = jnp.where(straight != 0, straight, open_rounds & far)
             wanted = jnp.where(bit == 0, wanted & -wanted, 0)
-            twice = jnp.where(straight != 0, 0, wanted)
+            twice = jnp.where((straight != 0) | (wanted == 0), -1, wanted)
             passed = jnp.zeros_like(used)
-            chain = []
             for earlier, taken in zip(opens, bits):
-                target = earlier & near
-                target = jnp.where((taken & twice) != 0, target & -target, 0)
-                passed = passed | target
-                chain.append(target)
-            last = jnp.where(straight != 0, wanted, passed)
-            freed = ~used
-            for e, (earlier, taken, target) in enumerate(zip(opens, bits, chain)):
-                end = earlier & freed
-                end = jnp.where((taken & last) != 0, end & -end, 0)
-                used = used | end
-                moved = target | end
-                bits[e] = jnp.where(moved != 0, moved, taken)
+                passed = passed | jnp.where(taken == twice, earlier, 0)
+            passed = passed & near
+            passed = passed & -passed
+            last = passed | jnp.where(straight != 0, wanted, 0)
+            last = jnp.where(last == 0, -1, last)
+            end = jnp.zeros_like(used)
+            for earlier, taken in zip(opens, bits):
+                end = end | jnp.where(taken == last, earlier, 0)
+            end = end & ~used
+            end = end & -end
+            used = used | end
+            for e, taken in enumerate(bits):
+                bits[e] = jnp.where(taken == last, end, jnp.where(taken == twice, passed, taken))
             bit = bit | wanted
         used = used | bit
         over = jnp.minimum(over, jnp.where(bit == 0, s, degree))
@@ -286,27 +301,34 @@
 
 
 def begin_kernel(
-    mine, degree, source_hbm, buf_ref,
+    mine, degree, source_hbm, buf_ref, partner_ref,
     x_ref, idx_ref, w_ref, left_idx_ref, left_off_ref, left_w_ref, over_ref,
     stage, stage_tail, stage_w, source_ref, sems,
 ):
     (copy,) = fetch(((source_hbm, source_ref),), sems)
     pitch = stage.shape[0] // mine
-    peers = buf_ref.shape[0]
+    peers = 2 * buf_ref.shape[0]
     span = x_ref.shape[0] // mine
     block_total = span - PAD
     groups = block_total // SUB
     shard_blocks = block_total // peers
     arc_rows = degree * shard_blocks
-    base = mine * shard_blocks
-    for i in range(peers):
+    dist_rows = mine * shard_blocks
+    even = lax.axis_index("arc") % 2 == 0
+
+    def unpack(target, i, b, rows, own_at, partner_at):
+        own = buf_ref[i, own_at + b * rows : own_at + (b + 1) * rows, :]
+        partner = partner_ref[i, partner_at + b * rows : partner_at + (b + 1) * rows, :]
+        blk = 2 * i * shard_blocks + b
+        target[pl.ds(blk, rows, stride=pitch), :] = jnp.where(even, own, partner)
+        blk = blk + shard_blocks
+        target[pl.ds(blk, rows, stride=pitch), :] = jnp.where(even, partner, own)
+
+    for i in range(peers // 2):
         for b in range(shard_blocks):
-            blk = i * shard_blocks + b
-            stage[pl.ds(blk, mine, stride=pitch), :] = buf_ref[i, b * mine : (b + 1) * mine, :]
-            s0 = base + b * degree
-            stage_tail[pl.ds(blk, degree, stride=pitch), :] = buf_ref[i, s0 : s0 + degree, :]
-            s1 = base + arc_rows + b * degree
-            stage_w[pl.ds(blk, degree, stride=pitch), :] = buf_ref[i, s1 : s1 + degree, :]
+            unpack(stage, i, b, mine, 0, 2 * arc_rows)
+            unpack(stage_tail, i, b, degree, dist_rows, 0)
+            unpack(stage_w, i, b, degree, dist_rows + arc_rows, arc_rows)
     over = None
     for half in range(groups):
         part = plan_rounds(
@@ -327,8 +349,11 @@
     over_ref[...] = jnp.full(over_ref.shape, jnp.min(over.astype(jnp.float32)).astype(jnp.int32))
 
 
-def add_kernel(a_ref, b_ref, after_ref, out_ref):
-    out_ref[...] = a_ref[...] + b_ref[...]
+def merge_kernel(a_ref, b_ref, after_ref, *out_refs):
+    total = a_ref[...] + b_ref[...]
+    for n, ref in enumerate(out_refs):
+        rows = ref.shape[0]
+        ref[...] = total[n * rows : (n + 1) * rows, :]
 
 
 def middle_kernel(
@@ -422,7 +447,7 @@
     arcs = (arc_tail, base_cost, arc_price, prev_dist)
     packed = pl.pallas_call(
         functools.partial(pack_kernel, node_count),
-        out_shape=near((peers, mine * shard_blocks + 3 * arc_rows, LANES), f32),
+        out_shape=near((peers // 2, 2 * mine * shard_blocks + 4 * arc_rows, LANES), f32),
         in_specs=[h()] * 6,
         out_specs=v(),
         scratch_shapes=[
@@ -434,25 +459,45 @@
         compiler_params=params,
         name="pack",
     )(far(path_arcs), far(demand), *map(far, arcs))
-    received = held(lax.all_to_all(packed, "arc", 0, 0, tiled=True))
-
-    flow = pl.pallas_call(
-        functools.partial(flow_kernel, arc_rows),
-        out_shape=near((arc_rows, LANES), f32),
+    parities = [list(range(side, peers, 2)) for side in range(2)]
+    received = held(
+        lax.all_to_all(packed, "arc", 0, 0, tiled=True, axis_index_groups=parities)
+    )
+
+    def swap(x):
+        return held(lax.ppermute(x, "arc", [(i, i ^ 1) for i in range(peers)]))
+
+    def exchange(x, step):
+        pairs = [(i, i ^ (1 << step)) for i in range(groups)]
+        return held(lax.ppermute(x, "comm", pairs))
+
+    def merge(a, b, after, parts):
+        return pl.pallas_call(
+            merge_kernel,
+            out_shape=(near((arc_rows, LANES), f32),) * parts,
+            in_specs=[v(), v(), v()],
+            out_specs=(v(),) * parts,
+            compiler_params=params,
+            name="merge",
+        )(held(a), b, held(after))
+
+    flow, passed = pl.pallas_call(
+        split_kernel,
+        out_shape=(
+            near((2 * arc_rows, LANES), f32),
+            near((peers // 2, 2 * arc_rows + mine * shard_blocks, LANES), f32),
+        ),
         in_specs=[v()],
-        out_specs=v(),
+        out_specs=(v(), v()),
         compiler_params=params,
-        name="flow",
+        name="split",
     )(received)
-
-    def exchange(step):
-        pairs = [(i, i ^ (1 << step)) for i in range(groups)]
-        return held(lax.ppermute(flow, "comm", pairs))
+    partner = swap(held(passed))
 
     steps = groups.bit_length() - 1
     if 1 << steps != groups:
         flow, steps = held(lax.psum(flow, "comm")), 0
-    arrived = exchange(0) if steps else None
+    arrived = exchange(flow, 0) if steps else jnp.zeros_like(flow)
 
     rounds = ROUNDS
     table = degree * block_total
@@ -468,7 +513,7 @@
             near((table, LANES), f32),
             near((SUB, LANES), i32),
         ),
-        in_specs=[h(), v()],
+        in_specs=[h(), v(), v()],
         out_specs=(v(),) * 7,
         scratch_shapes=[
             pltpu.VMEM((mine * (block_total + 1), LANES), f32),
@@ -479,21 +524,14 @@
         ],
         compiler_params=params,
         name="begin",
-    )(far(source_node), received)
+    )(far(source_node), received, partner)
 
     tables, over = tuple(map(held, tables)), held(over)
+    flow, other = merge(flow, held(arrived), x, 2)
+    arrived = swap(held(other))
     left = SWEEPS
-    for step in range(1, steps):
-        flow = pl.pallas_call(
-            add_kernel,
-            out_shape=near((arc_rows, LANES), f32),
-            in_specs=[v(), v(), v()],
-            out_specs=v(),
-            compiler_params=params,
-            name="add",
-        )(held(flow), arrived, held(x))
-        arrived = exchange(step)
-        count = min(2 if steps > 2 else 4, left - 2)
+    for step in range(1, max(steps, 1) + 1):
+        count = min(2 if step < steps else 4, left - 2)
         left -= count
         x = pl.pallas_call(
             functools.partial(middle_kernel, mine, degree, count),
@@ -502,10 +540,13 @@
             out_specs=v(),
             scratch_shapes=[pltpu.VMEM(state, f32)],
             compiler_params=params,
-                name="middle",
+            name="middle",
         )(over, held(x), *tables)
-
-    flows = (held(flow),) if arrived is None else (held(flow), arrived)
+        if step < steps:
+            (flow,) = merge(flow, arrived, x, 1)
+            arrived = exchange(held(flow), step)
+
+    flows = (held(flow), arrived)
     back, gradient = pl.pallas_call(
         functools.partial(end_kernel, mine, degree, left, len(flows)),
         out_shape=(

time: 40.9 us -> 38.8 us (0.949)
  blocking collectives: 23 us -> 20.4 us
    all_to_all x1, blocking collectives: 14.7 us -> 12.1 us  [shards(): lax.all_to_all(packed, 'arc', 0, 0, tiled=True, axis_index_groups=parities)]
    pallas_call x1 -> x2, Pallas kernels: 3.96 us -> 6.06 us  [shards(): pl.pallas_call(functools.partial(middle_kernel, mine, degree, count), out...]
    pallas_call x1, Pallas kernels: 3.99 us -> 2 us  [shards(): pl.pallas_call(functools.partial(end_kernel, mine, degree, left, len(flow...]
    ppermute x2 -> x4, starting transfers between devices: 4.22 us -> 4.38 us  [the longest x2 4.3 us: exchange(): return held(lax.ppermute(x, 'comm', pairs))]
  transfers between devices with their start and end apart: 2 -> 4, of which waited for: 1 -> 1; matrix products, arithmetic and copies ran while one was open for 0% -> 0% of each run, Pallas kernels for 14% -> 20%
where the time goes in v7:
time: 38.8 us; the launch traced here: 38.5 us
  blocking collectives  20.4 us (53%)
  Pallas kernels  12.4 us (32%)
  starting transfers between devices  4.38 us (11%)
  between operations  0.74 us (2%)
  waiting for transfers between devices  0.71 us (2%)
    all_to_all x1, blocking collectives, shards(): lax.all_to_all(packed, 'arc', 0, 0, tiled=True, axis_index_groups=parities)  12.1 us
    all_to_all x1, blocking collectives, shards(): final = held(lax.all_to_all(back, 'arc', 0, 0, tiled=True))  8.25 us
    pallas_call x2, Pallas kernels, shards(): pl.pallas_call(functools.partial(middle_kernel, mine, degree, count), out...  6.06 us
    ppermute x2, starting transfers between devices, exchange(): return held(lax.ppermute(x, 'comm', pairs))  4.3 us
    pallas_call x1, Pallas kernels, shards(): pl.pallas_call(functools.partial(end_kernel, mine, degree, left, len(flow...  2 us
    pallas_call x1, Pallas kernels, shards(): pl.pallas_call(functools.partial(pack_kernel, node_count), out_shape=near...  1.93 us
    pallas_call x1, Pallas kernels, shards(): pl.pallas_call(functools.partial(begin_kernel, mine, degree), out_shape=(...  1.62 us
  transfers between devices with their start and end apart: 4, of which 1 were waited for; matrix products, arithmetic and copies ran while one was open for 0% of the time, Pallas kernels for 20%

profile of v7, /device:TPU:0, one launch (start us, length us, event | category | flops | bytes accessed | tf_op | source)
XLA Modules:
  0.0 38.5 jit_solution(11875845570080735307)
XLA Ops:
  0.6 1.9 %pack.1 = f32[4,192,128]{2,1,0:T(8,128)S(1)} custom-call(s32[16,128]{1,0:T(8,128)} %path_hbm.1, f32[16]{0:T(128)} %demand_hbm.1, s32[16,256]{1,0:T(8,128)} %tail_hbm.1, f32[16,256]{1,0:T(8,128)} %cost_hbm.1, f32[16,256]{1,0:T(8,128)} %price_ref.1, f32[128,256]{1,0:T(8,128)} %dist_hbm.1), custom_call_target="tpu_custom_call" | custom-call | tf_op jit(solution)/shard_map/pack/pallas_call | solution.py:448
  2.6 12.1 %all_to_all.10.buf_ref = f32[4,192,128]{2,1,0:T(8,128)S(1)} all-to-all(f32[4,192,128]{2,1,0:T(8,128)S(1)} %pack.1), channel_id=1, replica_groups={{0,2,4,6},{1,3,5,7},{8,10,12,14},{9,11,13,15},{16,18,20,22},{17,19,21,2..., dimensions={0} | all-to-all | bytes 786432 | tf_op jit(solution)/shard_map/all_to_all | solution.py:464
  14.7 0.1 collective-permute-start
  14.8 1.6 %collective-permute-start.1 = (f32[64,128]{1,0:T(8,128)S(1)}, f32[64,128]{1,0:T(8,128)S(1)}, u32[]{:S(2)}, u32[]{:S(2)}) collective-permute-start(f32[64,128]{1,0:T(8,128)S(1)} %get-tuple-element.23.a_ref), channel_id=1, source_target_pairs={{0,8},{8,0},{16,24},{24,16},{1,9},{9,1},{17,25},{25,17},{2,10},{10... | collective-permute-start | bytes 98312 | tf_op jit(solution)/shard_map/ppermute | solution.py:472
  16.4 0.0 collective-permute-done.partner_ref
  16.4 1.6 %begin.1 = (f32[336,128]{1,0:T(8,128)S(1)}, s32[352,128]{1,0:T(8,128)S(1)}, f32[352,128]{1,0:T(8,128)S(1)}, s32[256,128]{1,0:T(8,128)S(1)}, s32[256,128]{1,0:T(8...) custom-call(s32[128]{0:T(128)} %source_hbm.1, f32[4,192,128]{2,1,0:T(8,128)S(1)} %all_to_all.10.buf_ref, ...), custom_call_target="tpu_custom_call" | custom-call | tf_op jit(solution)/shard_map/begin/pallas_call | solution.py:505
  18.0 0.7 %collective-permute-done.1.b_ref = f32[64,128]{1,0:T(8,128)S(1)} collective-permute-done((f32[64,128]{1,0:T(8,128)S(1)}, f32[64,128]{1,0:T(8,128)S(1)}, u32[]{:S(2)}, u32[]{:S(2)}) %collective-permute-start.1) | collective-permute-done | bytes 32800 | tf_op jit(solution)/shard_map/ppermute | solution.py:472
  18.8 0.0 collective-permute-start.2
  18.8 2.0 %middle.2.start_ref.after_ref = f32[336,128]{1,0:T(8,128)S(1)} custom-call(s32[8,128]{1,0:T(8,128)S(1)} %get-tuple-element.16.over_ref, f32[336,128]{1,0:T(8,128)S(1)} %get-tuple-element.17.start_ref.after_ref, s32[352,128]{1,0:T(8,128)S(1)} %get-tuple-element.18.idx_ref, f32[352,128]{1,0:T(8,128)S(1)} %get-tuple-element.19.w_ref, ...), custom_call_target="tpu_custom_call" | custom-call | tf_op jit(solution)/shard_map/middle/pallas_call | solution.py:536
  20.8 0.0 collective-permute-done.2.b_ref
  20.8 0.0 copy-start.1
  20.8 2.7 %collective-permute-start.3 = (f32[32,128]{1,0:T(8,128)S(1)}, f32[32,128]{1,0:T(8,128)S(1)}, u32[]{:S(2)}, u32[]{:S(2)}) collective-permute-start(f32[32,128]{1,0:T(8,128)S(1)} %merge.3.refs_0_), channel_id=1, source_target_pairs={{0,16},{8,24},{16,0},{24,8},{1,17},{9,25},{17,1},{25,9},{2,18},{10... | collective-permute-start | bytes 49160 | tf_op jit(solution)/shard_map/ppermute | solution.py:472
  23.5 4.0 %middle.3.start_ref = f32[336,128]{1,0:T(8,128)S(1)} custom-call(s32[8,128]{1,0:T(8,128)S(1)} %get-tuple-element.16.over_ref, f32[336,128]{1,0:T(8,128)S(1)} %middle.2.start_ref.after_ref, s32[352,128]{1,0:T(8,128)S(1)} %get-tuple-element.18.idx_ref, f32[352,128]{1,0:T(8,128)S(1)} %get-tuple-element.19.w_ref, s32[256,128]{1,0:T(8,128)S(1)} %get-tuple-element.20.left_idx_ref, ...), custom_call_target="tpu_custom_call" | custom-call | tf_op jit(solution)/shard_map/middle/pallas_call | solution.py:536
  27.5 0.0 collective-permute-done.3.refs_1_
  27.6 0.0 copy-done.1
  27.6 2.0 %end.1 = (f32[8,40,128]{2,1,0:T(8,128)S(1)}, f32[16,256]{1,0:T(8,128)S(1)}) custom-call(s32[8,128]{1,0:T(8,128)S(1)} %get-tuple-element.16.over_ref, f32[336,128]{1,0:T(8,128)S(1)} %middle.3.start_ref, s32[352,128]{1,0:T(8,128)S(1)} %get-tuple-element.18.idx_ref, f32[352,128]{1,0:T(8,128)S(1)} %get-tuple-element.19.w_ref, ...), custom_call_target="tpu_custom_call" | custom-call | tf_op jit(solution)/shard_map/end/pallas_call | solution.py:550
  29.6 0.0 copy-start
  29.6 8.2 %all_to_all.11.buf_ref = f32[8,40,128]{2,1,0:T(8,128)S(1)} all-to-all(f32[8,40,128]{2,1,0:T(8,128)S(1)} %get-tuple-element.26), channel_id=1, replica_groups=mesh['comm'=4,'arc'=8] {'arc'}, dimensions={0} | all-to-all | bytes 327680 | tf_op jit(solution)/shard_map/all_to_all | solution.py:562
  37.8 0.0 copy-done
  37.8 0.7 %finish.1 = (f32[128,256]{1,0:T(8,128)}, f32[16,256]{1,0:T(8,128)}) custom-call(f32[8,40,128]{2,1,0:T(8,128)S(1)} %all_to_all.11.buf_ref, f32[16,256]{1,0:T(8,128)S(1)} %get-tuple-element.27.grad_ref, f32[16,256]{1,0:T(8,128)S(1)} %copy-done), custom_call_target="tpu_custom_call" | custom-call | tf_op jit(solution)/shard_map/finish/pallas_call | solution.py:563
  (3 shorter events, 0.0 us)
Async XLA Ops:
  14.7 1.7 %collective-permute-start = (f32[4,96,128]{2,1,0:T(8,128)S(1)}, f32[4,96,128]{2,1,0:T(8,128)S(1)}, u32[]{:S(2)}, u32[]{:S(2)}) collective-permute-start(f32[4,96,128]{2,1,0:T(8,128)S(1)} %get-tuple-element.15), channel_id=1, source_target_pairs={{0,1},{1,0},{2,3},{3,2},{4,5},{5,4},{6,7},{7,6},{8,9},{9,8},{10,11... | collective-permute-start | bytes 589832 | tf_op jit(solution)/shard_map/ppermute | solution.py:468
  14.8 4.0 %collective-permute-start.1 = (f32[64,128]{1,0:T(8,128)S(1)}, f32[64,128]{1,0:T(8,128)S(1)}, u32[]{:S(2)}, u32[]{:S(2)}) collective-permute-start(f32[64,128]{1,0:T(8,128)S(1)} %get-tuple-element.23.a_ref), channel_id=1, source_target_pairs={{0,8},{8,0},{16,24},{24,16},{1,9},{9,1},{17,25},{25,17},{2,10},{10... | collective-permute-start | bytes 98312 | tf_op jit(solution)/shard_map/ppermute | solution.py:472
  18.8 2.0 %collective-permute-start.2 = (f32[32,128]{1,0:T(8,128)S(1)}, f32[32,128]{1,0:T(8,128)S(1)}, u32[]{:S(2)}, u32[]{:S(2)}) collective-permute-start(f32[32,128]{1,0:T(8,128)S(1)} %get-tuple-element.25), channel_id=1, source_target_pairs={{0,1},{1,0},{2,3},{3,2},{4,5},{5,4},{6,7},{7,6},{8,9},{9,8},{10,11... | collective-permute-start | bytes 49160 | tf_op jit(solution)/shard_map/ppermute | solution.py:468
  20.8 6.7 %copy-start.1 = (f32[16,256]{1,0:T(8,128)S(1)}, f32[16,256]{1,0:T(8,128)}, u32[]{:S(2)}) copy-start(f32[16,256]{1,0:T(8,128)} %cap_ref.1) | copy-start | bytes 49156
  20.8 6.7 %collective-permute-start.3 = (f32[32,128]{1,0:T(8,128)S(1)}, f32[32,128]{1,0:T(8,128)S(1)}, u32[]{:S(2)}, u32[]{:S(2)}) collective-permute-start(f32[32,128]{1,0:T(8,128)S(1)} %merge.3.refs_0_), channel_id=1, source_target_pairs={{0,16},{8,24},{16,0},{24,8},{1,17},{9,25},{17,1},{25,9},{2,18},{10... | collective-permute-start | bytes 49160 | tf_op jit(solution)/shard_map/ppermute | solution.py:472
  29.6 8.3 %copy-start = (f32[16,256]{1,0:T(8,128)S(1)}, f32[16,256]{1,0:T(8,128)}, u32[]{:S(2)}) copy-start(f32[16,256]{1,0:T(8,128)} %price_ref.1) | copy-start | bytes 49156

commit v8 on v7

--- a/solution.py
+++ b/solution.py
@@ -377,7 +377,8 @@
     tables = (idx_ref, w_ref, left_idx_ref, left_off_ref, left_w_ref)
     first_over = over_ref[0, 0]
     x_ref[...] = start_ref[...]
-    sweep_pairs(count, mine, degree, first_over, x_ref, other, tables)
+    if count:
+        sweep_pairs(count, mine, degree, first_over, x_ref, other, tables)
     square = None
     for b in range(shard_blocks):
         cols = slice(b * LANES, (b + 1) * LANES)
@@ -527,13 +528,8 @@
     )(far(source_node), received, partner)
 
     tables, over = tuple(map(held, tables)), held(over)
-    flow, other = merge(flow, held(arrived), x, 2)
-    arrived = swap(held(other))
-    left = SWEEPS
-    for step in range(1, max(steps, 1) + 1):
-        count = min(2 if step < steps else 4, left - 2)
-        left -= count
-        x = pl.pallas_call(
+    def sweep(x, count):
+        return pl.pallas_call(
             functools.partial(middle_kernel, mine, degree, count),
             out_shape=near(state, f32),
             in_specs=[v()] * (len(tables) + 2),
@@ -542,6 +538,15 @@
             compiler_params=params,
             name="middle",
         )(over, held(x), *tables)
+
+    x = sweep(x, 2)
+    left = SWEEPS - 2
+    flow, other = merge(flow, held(arrived), x, 2)
+    arrived = swap(held(other))
+    for step in range(1, max(steps, 1) + 1):
+        count = min(2 if step < steps else 4, left)
+        left -= count
+        x = sweep(x, count)
         if step < steps:
             (flow,) = merge(flow, arrived, x, 1)
             arrived = exchange(held(flow), step)

time: 38.8 us -> 38.4 us (0.990)
  waiting for transfers between devices: 0.71 us -> 0.01 us
    pallas_call x2 -> x3, Pallas kernels: 6.06 us -> 8.04 us  [sweep(): pl.pallas_call(functools.partial(middle_kernel, mine, degree, count), out...]
    pallas_call x1, Pallas kernels: 2 us -> 0.03 us  [shards(): pl.pallas_call(functools.partial(end_kernel, mine, degree, left, len(flow...]
    ppermute x2, waiting for transfers between devices: 0.71 us -> 0.01 us  [exchange(): return held(lax.ppermute(x, 'comm', pairs))]
  transfers between devices with their start and end apart: 4 -> 4, of which waited for: 1 -> 0; matrix products, arithmetic and copies ran while one was open for 0% -> 0% of each run, Pallas kernels for 20% -> 25%
where the time goes in v8:
time: 38.4 us; the launch traced here: 38.1 us
  blocking collectives  20.4 us (53%)
  Pallas kernels  12.4 us (32%)
  starting transfers between devices  4.59 us (12%)
  between operations  0.75 us (2%)
    all_to_all x1, blocking collectives, shards(): lax.all_to_all(packed, 'arc', 0, 0, tiled=True, axis_index_groups=parities)  12.1 us
    all_to_all x1, blocking collectives, shards(): final = held(lax.all_to_all(back, 'arc', 0, 0, tiled=True))  8.25 us
    pallas_call x3, Pallas kernels, sweep(): pl.pallas_call(functools.partial(middle_kernel, mine, degree, count), out...  8.04 us
    ppermute x2, starting transfers between devices, exchange(): return held(lax.ppermute(x, 'comm', pairs))  4.3 us
    pallas_call x1, Pallas kernels, shards(): pl.pallas_call(functools.partial(pack_kernel, node_count), out_shape=near...  1.93 us
    pallas_call x1, Pallas kernels, shards(): pl.pallas_call(functools.partial(begin_kernel, mine, degree), out_shape=(...  1.62 us
  transfers between devices with their start and end apart: 4, of which 0 were waited for; matrix products, arithmetic and copies ran while one was open for 0% of the time, Pallas kernels for 25%

profile of v8, /device:TPU:0, one launch (start us, length us, event | category | flops | bytes accessed | tf_op | source)
XLA Modules:
  0.0 38.1 jit_solution(10552816298195630819)
XLA Ops:
  0.6 1.9 %pack.1 = f32[4,192,128]{2,1,0:T(8,128)S(1)} custom-call(s32[16,128]{1,0:T(8,128)} %path_hbm.1, f32[16]{0:T(128)} %demand_hbm.1, s32[16,256]{1,0:T(8,128)} %tail_hbm.1, f32[16,256]{1,0:T(8,128)} %cost_hbm.1, f32[16,256]{1,0:T(8,128)} %price_ref.1, f32[128,256]{1,0:T(8,128)} %dist_hbm.1), custom_call_target="tpu_custom_call" | custom-call | tf_op jit(solution)/shard_map/pack/pallas_call | solution.py:449
  2.6 12.1 %all_to_all.10.buf_ref = f32[4,192,128]{2,1,0:T(8,128)S(1)} all-to-all(f32[4,192,128]{2,1,0:T(8,128)S(1)} %pack.1), channel_id=1, replica_groups={{0,2,4,6},{1,3,5,7},{8,10,12,14},{9,11,13,15},{16,18,20,22},{17,19,21,2..., dimensions={0} | all-to-all | bytes 786432 | tf_op jit(solution)/shard_map/all_to_all | solution.py:465
  14.7 0.1 collective-permute-start
  14.8 1.6 %collective-permute-start.1 = (f32[64,128]{1,0:T(8,128)S(1)}, f32[64,128]{1,0:T(8,128)S(1)}, u32[]{:S(2)}, u32[]{:S(2)}) collective-permute-start(f32[64,128]{1,0:T(8,128)S(1)} %get-tuple-element.23.a_ref), channel_id=1, source_target_pairs={{0,8},{8,0},{16,24},{24,16},{1,9},{9,1},{17,25},{25,17},{2,10},{10... | collective-permute-start | bytes 98312 | tf_op jit(solution)/shard_map/ppermute | solution.py:473
  16.4 0.0 collective-permute-done.partner_ref
  16.4 1.6 %begin.1 = (f32[336,128]{1,0:T(8,128)S(1)}, s32[352,128]{1,0:T(8,128)S(1)}, f32[352,128]{1,0:T(8,128)S(1)}, s32[256,128]{1,0:T(8,128)S(1)}, s32[256,128]{1,0:T(8...) custom-call(s32[128]{0:T(128)} %source_hbm.1, f32[4,192,128]{2,1,0:T(8,128)S(1)} %all_to_all.10.buf_ref, ...), custom_call_target="tpu_custom_call" | custom-call | tf_op jit(solution)/shard_map/begin/pallas_call | solution.py:506
  18.0 2.0 %middle.3.start_ref.after_ref = f32[336,128]{1,0:T(8,128)S(1)} custom-call(s32[8,128]{1,0:T(8,128)S(1)} %get-tuple-element.16.over_ref, f32[336,128]{1,0:T(8,128)S(1)} %get-tuple-element.17.start_ref, s32[352,128]{1,0:T(8,128)S(1)} %get-tuple-element.18.idx_ref, f32[352,128]{1,0:T(8,128)S(1)} %get-tuple-element.19.w_ref, ...), custom_call_target="tpu_custom_call" | custom-call | tf_op jit(solution)/shard_map/middle/pallas_call | solution.py:532
  20.1 0.0 collective-permute-done.1.b_ref
  20.1 0.2 collective-permute-start.2
  20.3 2.0 %middle.4.start_ref.after_ref = f32[336,128]{1,0:T(8,128)S(1)} custom-call(s32[8,128]{1,0:T(8,128)S(1)} %get-tuple-element.16.over_ref, f32[336,128]{1,0:T(8,128)S(1)} %middle.3.start_ref.after_ref, s32[352,128]{1,0:T(8,128)S(1)} %get-tuple-element.18.idx_ref, f32[352,128]{1,0:T(8,128)S(1)} %get-tuple-element.19.w_ref, ...), custom_call_target="tpu_custom_call" | custom-call | tf_op jit(solution)/shard_map/middle/pallas_call | solution.py:532
  22.3 0.0 collective-permute-done.2.b_ref
  22.3 0.0 copy-start.1
  22.3 2.7 %collective-permute-start.3 = (f32[32,128]{1,0:T(8,128)S(1)}, f32[32,128]{1,0:T(8,128)S(1)}, u32[]{:S(2)}, u32[]{:S(2)}) collective-permute-start(f32[32,128]{1,0:T(8,128)S(1)} %merge.3.refs_0_), channel_id=1, source_target_pairs={{0,16},{8,24},{16,0},{24,8},{1,17},{9,25},{17,1},{25,9},{2,18},{10... | collective-permute-start | bytes 49160 | tf_op jit(solution)/shard_map/ppermute | solution.py:473
  25.0 4.0 %middle.5.start_ref = f32[336,128]{1,0:T(8,128)S(1)} custom-call(s32[8,128]{1,0:T(8,128)S(1)} %get-tuple-element.16.over_ref, f32[336,128]{1,0:T(8,128)S(1)} %middle.4.start_ref.after_ref, s32[352,128]{1,0:T(8,128)S(1)} %get-tuple-element.18.idx_ref, f32[352,128]{1,0:T(8,128)S(1)} %get-tuple-element.19.w_ref, s32[256,128]{1,0:T(8,128)S(1)} %get-tuple-element.20.left_idx_ref, ...), custom_call_target="tpu_custom_call" | custom-call | tf_op jit(solution)/shard_map/middle/pallas_call | solution.py:532
  29.0 0.0 collective-permute-done.3.refs_1_
  29.1 0.0 copy-done.1
  29.1 0.0 copy-start
  29.1 8.2 %all_to_all.11.buf_ref = f32[8,40,128]{2,1,0:T(8,128)S(1)} all-to-all(f32[8,40,128]{2,1,0:T(8,128)S(1)} %get-tuple-element.26), channel_id=1, replica_groups=mesh['comm'=4,'arc'=8] {'arc'}, dimensions={0} | all-to-all | bytes 327680 | tf_op jit(solution)/shard_map/all_to_all | solution.py:567
  37.4 0.0 copy-done
  37.4 0.7 %finish.1 = (f32[128,256]{1,0:T(8,128)}, f32[16,256]{1,0:T(8,128)}) custom-call(f32[8,40,128]{2,1,0:T(8,128)S(1)} %all_to_all.11.buf_ref, f32[16,256]{1,0:T(8,128)S(1)} %get-tuple-element.27.grad_ref, f32[16,256]{1,0:T(8,128)S(1)} %copy-done), custom_call_target="tpu_custom_call" | custom-call | tf_op jit(solution)/shard_map/finish/pallas_call | solution.py:568
  (4 shorter events, 0.1 us)
Async XLA Ops:
  14.7 1.7 %collective-permute-start = (f32[4,96,128]{2,1,0:T(8,128)S(1)}, f32[4,96,128]{2,1,0:T(8,128)S(1)}, u32[]{:S(2)}, u32[]{:S(2)}) collective-permute-start(f32[4,96,128]{2,1,0:T(8,128)S(1)} %get-tuple-element.15), channel_id=1, source_target_pairs={{0,1},{1,0},{2,3},{3,2},{4,5},{5,4},{6,7},{7,6},{8,9},{9,8},{10,11... | collective-permute-start | bytes 589832 | tf_op jit(solution)/shard_map/ppermute | solution.py:469
  14.8 5.3 %collective-permute-start.1 = (f32[64,128]{1,0:T(8,128)S(1)}, f32[64,128]{1,0:T(8,128)S(1)}, u32[]{:S(2)}, u32[]{:S(2)}) collective-permute-start(f32[64,128]{1,0:T(8,128)S(1)} %get-tuple-element.23.a_ref), channel_id=1, source_target_pairs={{0,8},{8,0},{16,24},{24,16},{1,9},{9,1},{17,25},{25,17},{2,10},{10... | collective-permute-start | bytes 98312 | tf_op jit(solution)/shard_map/ppermute | solution.py:473
  20.1 2.2 %collective-permute-start.2 = (f32[32,128]{1,0:T(8,128)S(1)}, f32[32,128]{1,0:T(8,128)S(1)}, u32[]{:S(2)}, u32[]{:S(2)}) collective-permute-start(f32[32,128]{1,0:T(8,128)S(1)} %get-tuple-element.25), channel_id=1, source_target_pairs={{0,1},{1,0},{2,3},{3,2},{4,5},{5,4},{6,7},{7,6},{8,9},{9,8},{10,11... | collective-permute-start | bytes 49160 | tf_op jit(solution)/shard_map/ppermute | solution.py:469
  22.3 6.7 %copy-start.1 = (f32[16,256]{1,0:T(8,128)S(1)}, f32[16,256]{1,0:T(8,128)}, u32[]{:S(2)}) copy-start(f32[16,256]{1,0:T(8,128)} %cap_ref.1) | copy-start | bytes 49156
  22.3 6.7 %collective-permute-start.3 = (f32[32,128]{1,0:T(8,128)S(1)}, f32[32,128]{1,0:T(8,128)S(1)}, u32[]{:S(2)}, u32[]{:S(2)}) collective-permute-start(f32[32,128]{1,0:T(8,128)S(1)} %merge.3.refs_0_), channel_id=1, source_target_pairs={{0,16},{8,24},{16,0},{24,8},{1,17},{9,25},{17,1},{25,9},{2,18},{10... | collective-permute-start | bytes 49160 | tf_op jit(solution)/shard_map/ppermute | solution.py:473
  29.1 8.3 %copy-start = (f32[16,256]{1,0:T(8,128)S(1)}, f32[16,256]{1,0:T(8,128)}, u32[]{:S(2)}) copy-start(f32[16,256]{1,0:T(8,128)} %price_ref.1) | copy-start | bytes 49156
